TPU v7x, 32 devices: a whole 2x2x4 slice. The times are simulated.
32 devices in a mesh: sub: 4 (over x, core), gx: 4 (over z), gy: 2 (over y).
Axes of the slice: x: 2, y: 2, z: 4, core: 2. Of those that a mesh axis runs over, the one named last changes fastest.
Arguments:
- state: float32 [4, 256, 512], P(None, ('sub', 'gx'), 'gy'), may hold values from -4 to 4
- damping: float32 [4, 256, 512], P(None, ('sub', 'gx'), 'gy'), may hold values from 0.005 to 0.1
- weights: float32 [4], replicated, may hold values from 0.5 to 1.5
Outputs:
- combined: float32 [4, 256, 512], P(None, ('sub', 'gx'), 'gy')
- column_error: float32 [4, 512], P(None, 'gy')
All inputs are finite; a program needn't handle non-finite values.
Results may differ from a plain program's by a relative error of at most 0.0003.
Values sent between devices are 32-bit elements; how exact they have to be, the bound alone decides.
No kernel may reach another device: no remote copies, remote signals or barrier semaphores. Data moves between devices by JAX's collectives and lax.ppermute only.
A program may use at most 64 MiB of HBM per device.

v0:
```python
import jax
import jax.numpy as jnp
from jax import lax
from jax.sharding import PartitionSpec as P

KRYLOV = 12
SUBSTEPS = 4


dt_total = 4.0
sound_sq = 1.0
buoyancy_sq = 0.5
norm_eps = 1e-06
taylor_degree = 12
squarings = 8


def padded(cells, sides, width):
    for axis, dim in sides:
        count = lax.axis_size(axis)
        ends = count - 1
        head = lax.slice_in_dim(cells, 0, width, axis=dim)
        tail = lax.slice_in_dim(cells, cells.shape[dim] - width, cells.shape[dim], axis=dim)
        cells = jnp.concatenate(
            [
                lax.ppermute(tail, axis, [(i, (i + 1) % count) for i in range(ends)]),
                cells,
                lax.ppermute(head, axis, [((i + 1) % count, i) for i in range(ends)]),
            ],
            axis=dim,
        )
    return cells


def wave(field):
    row_pair = jnp.stack([field[0], field[3]])
    column_pair = jnp.stack([field[1], field[3]])
    rows_padded = padded(row_pair, ((("sub", "gx"), 1),), 1)
    columns_padded = padded(column_pair, (("gy", 2),), 1)
    rise_x = 0.5 * (rows_padded[1, 2:, :] - rows_padded[1, :-2, :])
    rise_y = 0.5 * (columns_padded[1, :, 2:] - columns_padded[1, :, :-2])
    spread = 0.5 * (rows_padded[0, 2:, :] - rows_padded[0, :-2, :]) + 0.5 * (
        columns_padded[0, :, 2:] - columns_padded[0, :, :-2]
    )
    return jnp.stack([-rise_x, -rise_y + field[2], -buoyancy_sq * field[1], -sound_sq * spread])


def phi_first(hessenberg):
    extent = hessenberg.shape[0]
    augmented = jnp.zeros((extent + 1, extent + 1), jnp.float32)
    augmented = augmented.at[:extent, :extent].set(hessenberg).at[0, extent].set(1.0)
    scaled = augmented / 2.0**squarings
    result = jnp.eye(extent + 1, dtype=jnp.float32)
    power_term = result
    for degree in range(1, taylor_degree + 1):
        power_term = jnp.dot(power_term, scaled, precision=lax.Precision.HIGHEST) / degree
        result = result + power_term
    for repeat in range(squarings):
        result = jnp.dot(result, result, precision=lax.Precision.HIGHEST)
    return result[:extent, extent]


def arnoldi(start, stiffness):
    shape = start.shape
    basis = jnp.zeros((KRYLOV + 1, start.size), jnp.float32).at[0].set(start.reshape(-1))
    hessenberg = jnp.zeros((KRYLOV + 1, KRYLOV), jnp.float32)
    for column in range(KRYLOV):
        current = basis[column].reshape(shape)
        image = (dt_total * (wave(current) - stiffness * current)).reshape(-1)
        partial_value = jnp.dot(basis[: column + 1], image, precision=lax.Precision.HIGHEST)
        products, squared = lax.psum((partial_value, jnp.sum(image * image)), ("sub", "gx", "gy"))
        image = image - jnp.dot(products, basis[: column + 1], precision=lax.Precision.HIGHEST)
        length = jnp.sqrt(jnp.maximum(squared - jnp.sum(products * products), 0.0) + norm_eps)
        hessenberg = (
            hessenberg.at[: column + 1, column].set(products).at[column + 1, column].set(length)
        )
        basis = basis.at[column + 1].set(image / length)
    return (basis, hessenberg)


def shards(state, damping, weights):
    stiffness = 3.0 * damping * state * state
    forcing = wave(state) - damping * state * state * state
    beta_norm = jnp.sqrt(lax.psum(jnp.sum(forcing * forcing), ("sub", "gx", "gy")) + norm_eps)
    basis, hessenberg = arnoldi(forcing / beta_norm, stiffness)
    mixing = jnp.zeros((KRYLOV,), jnp.float32)
    highest = jnp.zeros((), jnp.float32)
    for member in range(SUBSTEPS):
        fraction = (member + 1) / SUBSTEPS
        factor = dt_total * fraction
        coefficients = phi_first(fraction * hessenberg[:KRYLOV])
        mixing = mixing + weights[member] * factor * beta_norm * coefficients
        estimate = (
            factor
            * beta_norm
            * fraction
            * hessenberg[KRYLOV, KRYLOV - 1]
            * jnp.abs(coefficients[KRYLOV - 1])
        )
        highest = jnp.maximum(highest, estimate)
    increment = jnp.dot(mixing, basis[:KRYLOV], precision=lax.Precision.HIGHEST)
    combined = state + increment.reshape(state.shape)
    local_peak = highest * jnp.max(jnp.abs(basis[KRYLOV].reshape(state.shape)), axis=1)
    column_error = lax.pmax(local_peak, ("sub", "gx"))
    return (combined, column_error)


def solution(mesh):
    return jax.shard_map(
        shards,
        mesh=mesh,
        in_specs=(P(None, ("sub", "gx"), "gy"), P(None, ("sub", "gx"), "gy"), P()),
        out_specs=(P(None, ("sub", "gx"), "gy"), P(None, "gy")),
        check_vma=False,
    )
```

profile of v0, /device:TPU:0, one launch (start us, length us, event | category | flops | bytes accessed | tf_op | source)
XLA Modules:
  0.0 885.9 jit_solution(2977581656855364826)
XLA Ops:
  2.7 4.9 collective-permute-start.3
  23.8 5.2 collective-permute-start.1
  33.7 41.0 %psum.175 = f32[]{:T(128)} all-reduce(f32[]{:T(128)} %get-tuple-element.640), channel_id=1, replica_groups=mesh['sub'=4,'gx'=4,'gy'=2] {'sub','gx','gy'}, use_global_device_ids=true, to_apply=%region_1.0 | all-reduce | flops 1 | bytes 8 | tf_op jit(solution)/shard_map/psum | solution.py:84
  77.1 4.7 collective-permute-start.5
  83.1 4.5 collective-permute-start.7
  89.8 42.5 %all-reduce.17 = (f32[]{:T(128)}, f32[1]{0:T(128)}) all-reduce(f32[]{:T(128)} %get-tuple-element.587, f32[1]{0:T(128)} %bitcast.1), channel_id=1, replica_groups=mesh['sub'=4,'gx'=4,'gy'=2] {'sub','gx','gy'}, use_global_device_ids=true, to_apply=%region_4.0 | all-reduce | flops 2 | bytes 16 | tf_op jit(solution)/shard_map/psum | solution.py:71
  136.6 4.5 collective-permute-start.9
  142.5 4.5 collective-permute-start.11
  150.5 41.8 %all-reduce.16 = (f32[2]{0:T(128)S(1)}, f32[]{:T(128)}) all-reduce(f32[2]{0:T(128)S(1)} %convolution_bitcast_fusion.10, f32[]{:T(128)} %get-tuple-element.636), channel_id=1, replica_groups=mesh['sub'=4,'gx'=4,'gy'=2] {'sub','gx','gy'}, use_global_device_ids=true, to_apply=%region_6.0 | all-reduce | flops 3 | bytes 24 | tf_op jit(solution)/shard_map/psum | solution.py:71
  197.9 4.7 collective-permute-start.13
  202.5 1.9 broadcast_select_fusion.10
  204.5 4.5 collective-permute-start.15
  209.5 1.4 scatter.150
  213.2 41.8 %all-reduce.15 = (f32[3]{0:T(128)S(1)}, f32[]{:T(128)}) all-reduce(f32[3]{0:T(128)S(1)} %convolution_bitcast_fusion.9, f32[]{:T(128)} %get-tuple-element.634), channel_id=1, replica_groups=mesh['sub'=4,'gx'=4,'gy'=2] {'sub','gx','gy'}, use_global_device_ids=true, to_apply=%region_11.0 | all-reduce | flops 4 | bytes 32 | tf_op jit(solution)/shard_map/psum | solution.py:71
  260.5 4.5 collective-permute-start.17
  265.0 1.9 broadcast_select_fusion.9
  267.0 4.5 collective-permute-start.19
  275.9 41.0 %all-reduce.14 = (f32[4]{0:T(128)S(1)}, f32[]{:T(128)}) all-reduce(f32[4]{0:T(128)S(1)} %convolution_bitcast_fusion.8, f32[]{:T(128)} %get-tuple-element.632), channel_id=1, replica_groups=mesh['sub'=4,'gx'=4,'gy'=2] {'sub','gx','gy'}, use_global_device_ids=true, to_apply=%region_16.0 | all-reduce | flops 5 | bytes 40 | tf_op jit(solution)/shard_map/psum | solution.py:71
  322.4 4.7 collective-permute-start.21
  327.0 2.0 broadcast_select_fusion.8
  329.1 4.5 collective-permute-start.23
  334.1 1.4 scatter.160
  337.8 41.8 %all-reduce.13 = (f32[5]{0:T(128)S(1)}, f32[]{:T(128)}) all-reduce(f32[5]{0:T(128)S(1)} %convolution_bitcast_fusion.7, f32[]{:T(128)} %get-tuple-element.630), channel_id=1, replica_groups=mesh['sub'=4,'gx'=4,'gy'=2] {'sub','gx','gy'}, use_global_device_ids=true, to_apply=%region_21.0 | all-reduce | flops 6 | bytes 48 | tf_op jit(solution)/shard_map/psum | solution.py:71
  385.0 4.5 collective-permute-start.25
  389.6 1.9 broadcast_select_fusion.7
  391.5 4.5 collective-permute-start.27
  400.2 41.1 %all-reduce.12 = (f32[6]{0:T(128)S(1)}, f32[]{:T(128)}) all-reduce(f32[6]{0:T(128)S(1)} %convolution_bitcast_fusion.6, f32[]{:T(128)} %get-tuple-element.628), channel_id=1, replica_groups=mesh['sub'=4,'gx'=4,'gy'=2] {'sub','gx','gy'}, use_global_device_ids=true, to_apply=%region_26.0 | all-reduce | flops 7 | bytes 56 | tf_op jit(solution)/shard_map/psum | solution.py:71
  446.9 4.7 collective-permute-start.29
  451.5 2.0 broadcast_select_fusion.6
  453.6 4.5 collective-permute-start.31
  458.6 1.4 scatter.170
  462.3 42.2 %all-reduce.11 = (f32[7]{0:T(128)S(1)}, f32[]{:T(128)}) all-reduce(f32[7]{0:T(128)S(1)} %convolution_bitcast_fusion.5, f32[]{:T(128)} %get-tuple-element.626), channel_id=1, replica_groups=mesh['sub'=4,'gx'=4,'gy'=2] {'sub','gx','gy'}, use_global_device_ids=true, to_apply=%region_31.0 | all-reduce | flops 8 | bytes 64 | tf_op jit(solution)/shard_map/psum | solution.py:71
  510.0 4.5 collective-permute-start.33
  514.5 2.0 broadcast_select_fusion.5
  516.6 4.5 collective-permute-start.35
  521.6 1.4 scatter.175
  525.3 41.1 %all-reduce.10 = (f32[8]{0:T(128)S(1)}, f32[]{:T(128)}) all-reduce(f32[8]{0:T(128)S(1)} %convolution_bitcast_fusion.4, f32[]{:T(128)} %get-tuple-element.624), channel_id=1, replica_groups=mesh['sub'=4,'gx'=4,'gy'=2] {'sub','gx','gy'}, use_global_device_ids=true, to_apply=%region_36.0 | all-reduce | flops 9 | bytes 72 | tf_op jit(solution)/shard_map/psum | solution.py:71
  571.9 4.7 collective-permute-start.37
  576.6 1.9 broadcast_select_fusion.4
  578.5 4.5 collective-permute-start.39
  587.3 41.8 %all-reduce.9 = (f32[9]{0:T(128)S(1)}, f32[]{:T(128)}) all-reduce(f32[9]{0:T(128)S(1)} %convolution_bitcast_fusion.3, f32[]{:T(128)} %get-tuple-element.622), channel_id=1, replica_groups=mesh['sub'=4,'gx'=4,'gy'=2] {'sub','gx','gy'}, use_global_device_ids=true, to_apply=%region_41.0 | all-reduce | flops 10 | bytes 80 | tf_op jit(solution)/shard_map/psum | solution.py:71
  634.7 4.5 collective-permute-start.41
  639.2 1.9 broadcast_select_fusion.3
  641.2 4.5 collective-permute-start.43
  646.2 1.4 scatter.185
  650.0 41.3 %all-reduce.8 = (f32[10]{0:T(128)S(1)}, f32[]{:T(128)}) all-reduce(f32[10]{0:T(128)S(1)} %convolution_bitcast_fusion.2, f32[]{:T(128)} %get-tuple-element.620), channel_id=1, replica_groups=mesh['sub'=4,'gx'=4,'gy'=2] {'sub','gx','gy'}, use_global_device_ids=true, to_apply=%region_46.0 | all-reduce | flops 11 | bytes 88 | tf_op jit(solution)/shard_map/psum | solution.py:71
  696.9 4.7 collective-permute-start.45
  701.5 2.0 broadcast_select_fusion.2
  703.5 4.5 collective-permute-start.47
  712.4 41.8 %all-reduce.7 = (f32[11]{0:T(128)S(1)}, f32[]{:T(128)}) all-reduce(f32[11]{0:T(128)S(1)} %convolution_bitcast_fusion.1, f32[]{:T(128)} %get-tuple-element.618), channel_id=1, replica_groups=mesh['sub'=4,'gx'=4,'gy'=2] {'sub','gx','gy'}, use_global_device_ids=true, to_apply=%region_51.0 | all-reduce | flops 12 | bytes 96 | tf_op jit(solution)/shard_map/psum | solution.py:71
  759.7 4.5 collective-permute-start.49
  764.2 1.9 broadcast_select_fusion.1
  766.2 4.5 collective-permute-start.51
  771.2 1.4 scatter.195
  775.4 40.7 %all-reduce.6 = (f32[12]{0:T(128)S(1)}, f32[]{:T(128)}) all-reduce(f32[12]{0:T(128)S(1)} %convolution_bitcast_fusion, f32[]{:T(128)} %get-tuple-element.616), channel_id=1, replica_groups=mesh['sub'=4,'gx'=4,'gy'=2] {'sub','gx','gy'}, use_global_device_ids=true, to_apply=%region_56.0 | all-reduce | flops 13 | bytes 104 | tf_op jit(solution)/shard_map/psum | solution.py:71
  816.7 2.0 broadcast_select_fusion
  818.7 1.5 scatter.200
  820.2 2.5 fusion.334
  822.7 2.6 fusion.336
  827.2 2.0 scatter.214
  833.3 1.9 scatter.210
  839.3 2.0 scatter.206
  845.4 2.0 scatter.204
  851.6 32.4 %pmax.7 = f32[4,256]{1,0:T(4,128)} all-reduce(f32[4,256]{1,0:T(4,128)S(1)} %broadcast_multiply_fusion.68), channel_id=1, replica_groups=mesh['sub'=4,'gx'=4,'gy'=2] {'sub','gx'}, use_global_device_ids=true, to_apply=%region_62.0 | all-reduce | flops 1024 | bytes 8192 | tf_op jit(solution)/shard_map/pmax | solution.py:104
  (495 shorter events, 123.4 us)
Async XLA Ops:
  1.4 21.0 %copy-start = (f32[4,16,256]{2,1,0:T(8,128)S(1)}, f32[4,16,256]{2,1,0:T(8,128)}, u32[]{:S(2)}) copy-start(f32[4,16,256]{2,1,0:T(8,128)} %param.93) | copy-start | bytes 196612
  1.4 20.9 %collective-permute-start.2 = (f32[2,16,1]{2,1,0:T(8,128)S(1)}, f32[2,16,1]{2,1,0:T(8,128)S(1)}, u32[]{:S(2)}, u32[]{:S(2)}) collective-permute-start(f32[2,16,1]{2,1,0:T(8,128)S(1)} %get-tuple-element.735), channel_id=1, source_target_pairs={{1,0},{3,2},{5,4},{7,6},{9,8},{11,10},{13,12},{15,14},{17,16},{19,... | collective-permute-start | bytes 392 | tf_op jit(solution)/shard_map/ppermute | solution.py:28
  2.7 19.7 %collective-permute-start.3 = (f32[2,16,1]{2,1,0:T(8,128)S(1)}, f32[2,16,1]{2,1,0:T(8,128)S(1)}, u32[]{:S(2)}, u32[]{:S(2)}) collective-permute-start(f32[2,16,1]{2,1,0:T(8,128)S(1)} %get-tuple-element.736), channel_id=1, source_target_pairs={{0,1},{2,3},{4,5},{6,7},{8,9},{10,11},{12,13},{14,15},{16,17},{18,... | collective-permute-start | bytes 392 | tf_op jit(solution)/shard_map/ppermute | solution.py:26
  8.4 0.7 copy-start.12
  9.7 0.7 copy-start.11
  11.0 0.7 copy-start.10
  12.3 0.7 copy-start.9
  13.7 0.7 copy-start.8
  15.1 0.7 copy-start.7
  16.4 0.7 copy-start.6
  17.7 0.7 copy-start.5
  19.1 0.7 copy-start.4
  21.0 0.7 copy-start.2
  22.5 10.5 %collective-permute-start = (f32[2,1,256]{2,1,0:T(1,128)S(1)}, f32[2,1,256]{2,1,0:T(1,128)S(1)}, u32[]{:S(2)}, u32[]{:S(2)}) collective-permute-start(f32[2,1,256]{2,1,0:T(1,128)S(1)} %get-tuple-element.733), channel_id=1, source_target_pairs={{2,0},{4,2},{6,4},{8,6},{10,8},{12,10},{14,12},{16,14},{18,16},{20... | collective-permute-start | bytes 6152 | tf_op jit(solution)/shard_map/ppermute | solution.py:28
  23.8 9.2 %collective-permute-start.1 = (f32[2,1,256]{2,1,0:T(1,128)S(1)}, f32[2,1,256]{2,1,0:T(1,128)S(1)}, u32[]{:S(2)}, u32[]{:S(2)}) collective-permute-start(f32[2,1,256]{2,1,0:T(1,128)S(1)} %get-tuple-element.734), channel_id=1, source_target_pairs={{0,2},{2,4},{4,6},{6,8},{8,10},{10,12},{12,14},{14,16},{16,18},{18... | collective-permute-start | bytes 6152 | tf_op jit(solution)/shard_map/ppermute | solution.py:26
  31.6 1.5 copy-start.1
  75.8 13.3 %collective-permute-start.4 = (f32[2,1,256]{2,1,0:T(1,128)S(1)}, f32[2,1,256]{2,1,0:T(1,128)S(1)}, u32[]{:S(2)}, u32[]{:S(2)}) collective-permute-start(f32[2,1,256]{2,1,0:T(1,128)S(1)} %get-tuple-element.729), channel_id=1, source_target_pairs={{2,0},{4,2},{6,4},{8,6},{10,8},{12,10},{14,12},{16,14},{18,16},{20... | collective-permute-start | bytes 6152 | tf_op jit(solution)/shard_map/ppermute | solution.py:28
  77.1 12.0 %collective-permute-start.5 = (f32[2,1,256]{2,1,0:T(1,128)S(1)}, f32[2,1,256]{2,1,0:T(1,128)S(1)}, u32[]{:S(2)}, u32[]{:S(2)}) collective-permute-start(f32[2,1,256]{2,1,0:T(1,128)S(1)} %get-tuple-element.730), channel_id=1, source_target_pairs={{0,2},{2,4},{4,6},{6,8},{8,10},{10,12},{12,14},{14,16},{16,18},{18... | collective-permute-start | bytes 6152 | tf_op jit(solution)/shard_map/ppermute | solution.py:26
  81.8 6.6 collective-permute-start.6
  83.1 6.0 collective-permute-start.7
  135.3 13.2 %collective-permute-start.8 = (f32[2,1,256]{2,1,0:T(1,128)S(1)}, f32[2,1,256]{2,1,0:T(1,128)S(1)}, u32[]{:S(2)}, u32[]{:S(2)}) collective-permute-start(f32[2,1,256]{2,1,0:T(1,128)S(1)} %get-tuple-element.725), channel_id=1, source_target_pairs={{2,0},{4,2},{6,4},{8,6},{10,8},{12,10},{14,12},{16,14},{18,16},{20... | collective-permute-start | bytes 6152 | tf_op jit(solution)/shard_map/ppermute | solution.py:28
  136.6 11.9 %collective-permute-start.9 = (f32[2,1,256]{2,1,0:T(1,128)S(1)}, f32[2,1,256]{2,1,0:T(1,128)S(1)}, u32[]{:S(2)}, u32[]{:S(2)}) collective-permute-start(f32[2,1,256]{2,1,0:T(1,128)S(1)} %get-tuple-element.726), channel_id=1, source_target_pairs={{0,2},{2,4},{4,6},{6,8},{8,10},{10,12},{12,14},{14,16},{16,18},{18... | collective-permute-start | bytes 6152 | tf_op jit(solution)/shard_map/ppermute | solution.py:26
  141.2 7.2 collective-permute-start.10
  142.5 6.0 collective-permute-start.11
  195.3 15.9 %collective-permute-start.14 = (f32[2,16,1]{2,1,0:T(8,128)S(1)}, f32[2,16,1]{2,1,0:T(8,128)S(1)}, u32[]{:S(2)}, u32[]{:S(2)}) collective-permute-start(f32[2,16,1]{2,1,0:T(8,128)S(1)} %get-tuple-element.723), channel_id=1, source_target_pairs={{1,0},{3,2},{5,4},{7,6},{9,8},{11,10},{13,12},{15,14},{17,16},{19,... | collective-permute-start | bytes 392 | tf_op jit(solution)/shard_map/ppermute | solution.py:28
  196.6 14.6 %collective-permute-start.12 = (f32[2,1,256]{2,1,0:T(1,128)S(1)}, f32[2,1,256]{2,1,0:T(1,128)S(1)}, u32[]{:S(2)}, u32[]{:S(2)}) collective-permute-start(f32[2,1,256]{2,1,0:T(1,128)S(1)} %get-tuple-element.721), channel_id=1, source_target_pairs={{2,0},{4,2},{6,4},{8,6},{10,8},{12,10},{14,12},{16,14},{18,16},{20... | collective-permute-start | bytes 6152 | tf_op jit(solution)/shard_map/ppermute | solution.py:28
  197.9 13.3 %collective-permute-start.13 = (f32[2,1,256]{2,1,0:T(1,128)S(1)}, f32[2,1,256]{2,1,0:T(1,128)S(1)}, u32[]{:S(2)}, u32[]{:S(2)}) collective-permute-start(f32[2,1,256]{2,1,0:T(1,128)S(1)} %get-tuple-element.722), channel_id=1, source_target_pairs={{0,2},{2,4},{4,6},{6,8},{8,10},{10,12},{12,14},{14,16},{16,18},{18... | collective-permute-start | bytes 6152 | tf_op jit(solution)/shard_map/ppermute | solution.py:26
  204.5 6.7 collective-permute-start.15
  257.9 15.9 %collective-permute-start.18 = (f32[2,16,1]{2,1,0:T(8,128)S(1)}, f32[2,16,1]{2,1,0:T(8,128)S(1)}, u32[]{:S(2)}, u32[]{:S(2)}) collective-permute-start(f32[2,16,1]{2,1,0:T(8,128)S(1)} %get-tuple-element.719), channel_id=1, source_target_pairs={{1,0},{3,2},{5,4},{7,6},{9,8},{11,10},{13,12},{15,14},{17,16},{19,... | collective-permute-start | bytes 392 | tf_op jit(solution)/shard_map/ppermute | solution.py:28
  259.2 14.6 %collective-permute-start.16 = (f32[2,1,256]{2,1,0:T(1,128)S(1)}, f32[2,1,256]{2,1,0:T(1,128)S(1)}, u32[]{:S(2)}, u32[]{:S(2)}) collective-permute-start(f32[2,1,256]{2,1,0:T(1,128)S(1)} %get-tuple-element.717), channel_id=1, source_target_pairs={{2,0},{4,2},{6,4},{8,6},{10,8},{12,10},{14,12},{16,14},{18,16},{20... | collective-permute-start | bytes 6152 | tf_op jit(solution)/shard_map/ppermute | solution.py:28
  260.5 13.4 %collective-permute-start.17 = (f32[2,1,256]{2,1,0:T(1,128)S(1)}, f32[2,1,256]{2,1,0:T(1,128)S(1)}, u32[]{:S(2)}, u32[]{:S(2)}) collective-permute-start(f32[2,1,256]{2,1,0:T(1,128)S(1)} %get-tuple-element.718), channel_id=1, source_target_pairs={{0,2},{2,4},{4,6},{6,8},{8,10},{10,12},{12,14},{14,16},{16,18},{18... | collective-permute-start | bytes 6152 | tf_op jit(solution)/shard_map/ppermute | solution.py:26
  267.0 6.8 collective-permute-start.19
  319.7 16.0 %collective-permute-start.22 = (f32[2,16,1]{2,1,0:T(8,128)S(1)}, f32[2,16,1]{2,1,0:T(8,128)S(1)}, u32[]{:S(2)}, u32[]{:S(2)}) collective-permute-start(f32[2,16,1]{2,1,0:T(8,128)S(1)} %get-tuple-element.715), channel_id=1, source_target_pairs={{1,0},{3,2},{5,4},{7,6},{9,8},{11,10},{13,12},{15,14},{17,16},{19,... | collective-permute-start | bytes 392 | tf_op jit(solution)/shard_map/ppermute | solution.py:28
  321.1 14.7 %collective-permute-start.20 = (f32[2,1,256]{2,1,0:T(1,128)S(1)}, f32[2,1,256]{2,1,0:T(1,128)S(1)}, u32[]{:S(2)}, u32[]{:S(2)}) collective-permute-start(f32[2,1,256]{2,1,0:T(1,128)S(1)} %get-tuple-element.713), channel_id=1, source_target_pairs={{2,0},{4,2},{6,4},{8,6},{10,8},{12,10},{14,12},{16,14},{18,16},{20... | collective-permute-start | bytes 6152 | tf_op jit(solution)/shard_map/ppermute | solution.py:28
  322.4 13.4 %collective-permute-start.21 = (f32[2,1,256]{2,1,0:T(1,128)S(1)}, f32[2,1,256]{2,1,0:T(1,128)S(1)}, u32[]{:S(2)}, u32[]{:S(2)}) collective-permute-start(f32[2,1,256]{2,1,0:T(1,128)S(1)} %get-tuple-element.714), channel_id=1, source_target_pairs={{0,2},{2,4},{4,6},{6,8},{8,10},{10,12},{12,14},{14,16},{16,18},{18... | collective-permute-start | bytes 6152 | tf_op jit(solution)/shard_map/ppermute | solution.py:26
  329.1 6.7 collective-permute-start.23
  382.4 15.7 %collective-permute-start.26 = (f32[2,16,1]{2,1,0:T(8,128)S(1)}, f32[2,16,1]{2,1,0:T(8,128)S(1)}, u32[]{:S(2)}, u32[]{:S(2)}) collective-permute-start(f32[2,16,1]{2,1,0:T(8,128)S(1)} %get-tuple-element.711), channel_id=1, source_target_pairs={{1,0},{3,2},{5,4},{7,6},{9,8},{11,10},{13,12},{15,14},{17,16},{19,... | collective-permute-start | bytes 392 | tf_op jit(solution)/shard_map/ppermute | solution.py:28
  383.7 14.4 %collective-permute-start.24 = (f32[2,1,256]{2,1,0:T(1,128)S(1)}, f32[2,1,256]{2,1,0:T(1,128)S(1)}, u32[]{:S(2)}, u32[]{:S(2)}) collective-permute-start(f32[2,1,256]{2,1,0:T(1,128)S(1)} %get-tuple-element.709), channel_id=1, source_target_pairs={{2,0},{4,2},{6,4},{8,6},{10,8},{12,10},{14,12},{16,14},{18,16},{20... | collective-permute-start | bytes 6152 | tf_op jit(solution)/shard_map/ppermute | solution.py:28
  385.0 13.2 %collective-permute-start.25 = (f32[2,1,256]{2,1,0:T(1,128)S(1)}, f32[2,1,256]{2,1,0:T(1,128)S(1)}, u32[]{:S(2)}, u32[]{:S(2)}) collective-permute-start(f32[2,1,256]{2,1,0:T(1,128)S(1)} %get-tuple-element.710), channel_id=1, source_target_pairs={{0,2},{2,4},{4,6},{6,8},{8,10},{10,12},{12,14},{14,16},{16,18},{18... | collective-permute-start | bytes 6152 | tf_op jit(solution)/shard_map/ppermute | solution.py:26
  391.5 6.7 collective-permute-start.27
  444.3 16.0 %collective-permute-start.30 = (f32[2,16,1]{2,1,0:T(8,128)S(1)}, f32[2,16,1]{2,1,0:T(8,128)S(1)}, u32[]{:S(2)}, u32[]{:S(2)}) collective-permute-start(f32[2,16,1]{2,1,0:T(8,128)S(1)} %get-tuple-element.707), channel_id=1, source_target_pairs={{1,0},{3,2},{5,4},{7,6},{9,8},{11,10},{13,12},{15,14},{17,16},{19,... | collective-permute-start | bytes 392 | tf_op jit(solution)/shard_map/ppermute | solution.py:28
  445.6 14.7 %collective-permute-start.28 = (f32[2,1,256]{2,1,0:T(1,128)S(1)}, f32[2,1,256]{2,1,0:T(1,128)S(1)}, u32[]{:S(2)}, u32[]{:S(2)}) collective-permute-start(f32[2,1,256]{2,1,0:T(1,128)S(1)} %get-tuple-element.705), channel_id=1, source_target_pairs={{2,0},{4,2},{6,4},{8,6},{10,8},{12,10},{14,12},{16,14},{18,16},{20... | collective-permute-start | bytes 6152 | tf_op jit(solution)/shard_map/ppermute | solution.py:28
  446.9 13.4 %collective-permute-start.29 = (f32[2,1,256]{2,1,0:T(1,128)S(1)}, f32[2,1,256]{2,1,0:T(1,128)S(1)}, u32[]{:S(2)}, u32[]{:S(2)}) collective-permute-start(f32[2,1,256]{2,1,0:T(1,128)S(1)} %get-tuple-element.706), channel_id=1, source_target_pairs={{0,2},{2,4},{4,6},{6,8},{8,10},{10,12},{12,14},{14,16},{16,18},{18... | collective-permute-start | bytes 6152 | tf_op jit(solution)/shard_map/ppermute | solution.py:26
  453.6 6.7 collective-permute-start.31
  507.4 15.9 %collective-permute-start.34 = (f32[2,16,1]{2,1,0:T(8,128)S(1)}, f32[2,16,1]{2,1,0:T(8,128)S(1)}, u32[]{:S(2)}, u32[]{:S(2)}) collective-permute-start(f32[2,16,1]{2,1,0:T(8,128)S(1)} %get-tuple-element.703), channel_id=1, source_target_pairs={{1,0},{3,2},{5,4},{7,6},{9,8},{11,10},{13,12},{15,14},{17,16},{19,... | collective-permute-start | bytes 392 | tf_op jit(solution)/shard_map/ppermute | solution.py:28
  508.7 14.6 %collective-permute-start.32 = (f32[2,1,256]{2,1,0:T(1,128)S(1)}, f32[2,1,256]{2,1,0:T(1,128)S(1)}, u32[]{:S(2)}, u32[]{:S(2)}) collective-permute-start(f32[2,1,256]{2,1,0:T(1,128)S(1)} %get-tuple-element.701), channel_id=1, source_target_pairs={{2,0},{4,2},{6,4},{8,6},{10,8},{12,10},{14,12},{16,14},{18,16},{20... | collective-permute-start | bytes 6152 | tf_op jit(solution)/shard_map/ppermute | solution.py:28
  510.0 13.3 %collective-permute-start.33 = (f32[2,1,256]{2,1,0:T(1,128)S(1)}, f32[2,1,256]{2,1,0:T(1,128)S(1)}, u32[]{:S(2)}, u32[]{:S(2)}) collective-permute-start(f32[2,1,256]{2,1,0:T(1,128)S(1)} %get-tuple-element.702), channel_id=1, source_target_pairs={{0,2},{2,4},{4,6},{6,8},{8,10},{10,12},{12,14},{14,16},{16,18},{18... | collective-permute-start | bytes 6152 | tf_op jit(solution)/shard_map/ppermute | solution.py:26
  516.6 6.7 collective-permute-start.35
  569.3 15.8 %collective-permute-start.38 = (f32[2,16,1]{2,1,0:T(8,128)S(1)}, f32[2,16,1]{2,1,0:T(8,128)S(1)}, u32[]{:S(2)}, u32[]{:S(2)}) collective-permute-start(f32[2,16,1]{2,1,0:T(8,128)S(1)} %get-tuple-element.699), channel_id=1, source_target_pairs={{1,0},{3,2},{5,4},{7,6},{9,8},{11,10},{13,12},{15,14},{17,16},{19,... | collective-permute-start | bytes 392 | tf_op jit(solution)/shard_map/ppermute | solution.py:28
  570.6 14.5 %collective-permute-start.36 = (f32[2,1,256]{2,1,0:T(1,128)S(1)}, f32[2,1,256]{2,1,0:T(1,128)S(1)}, u32[]{:S(2)}, u32[]{:S(2)}) collective-permute-start(f32[2,1,256]{2,1,0:T(1,128)S(1)} %get-tuple-element.697), channel_id=1, source_target_pairs={{2,0},{4,2},{6,4},{8,6},{10,8},{12,10},{14,12},{16,14},{18,16},{20... | collective-permute-start | bytes 6152 | tf_op jit(solution)/shard_map/ppermute | solution.py:28
  571.9 13.2 %collective-permute-start.37 = (f32[2,1,256]{2,1,0:T(1,128)S(1)}, f32[2,1,256]{2,1,0:T(1,128)S(1)}, u32[]{:S(2)}, u32[]{:S(2)}) collective-permute-start(f32[2,1,256]{2,1,0:T(1,128)S(1)} %get-tuple-element.698), channel_id=1, source_target_pairs={{0,2},{2,4},{4,6},{6,8},{8,10},{10,12},{12,14},{14,16},{16,18},{18... | collective-permute-start | bytes 6152 | tf_op jit(solution)/shard_map/ppermute | solution.py:26
  578.5 6.6 collective-permute-start.39
  632.1 15.8 %collective-permute-start.42 = (f32[2,16,1]{2,1,0:T(8,128)S(1)}, f32[2,16,1]{2,1,0:T(8,128)S(1)}, u32[]{:S(2)}, u32[]{:S(2)}) collective-permute-start(f32[2,16,1]{2,1,0:T(8,128)S(1)} %get-tuple-element.695), channel_id=1, source_target_pairs={{1,0},{3,2},{5,4},{7,6},{9,8},{11,10},{13,12},{15,14},{17,16},{19,... | collective-permute-start | bytes 392 | tf_op jit(solution)/shard_map/ppermute | solution.py:28
  633.4 14.5 %collective-permute-start.40 = (f32[2,1,256]{2,1,0:T(1,128)S(1)}, f32[2,1,256]{2,1,0:T(1,128)S(1)}, u32[]{:S(2)}, u32[]{:S(2)}) collective-permute-start(f32[2,1,256]{2,1,0:T(1,128)S(1)} %get-tuple-element.693), channel_id=1, source_target_pairs={{2,0},{4,2},{6,4},{8,6},{10,8},{12,10},{14,12},{16,14},{18,16},{20... | collective-permute-start | bytes 6152 | tf_op jit(solution)/shard_map/ppermute | solution.py:28
  634.7 13.2 %collective-permute-start.41 = (f32[2,1,256]{2,1,0:T(1,128)S(1)}, f32[2,1,256]{2,1,0:T(1,128)S(1)}, u32[]{:S(2)}, u32[]{:S(2)}) collective-permute-start(f32[2,1,256]{2,1,0:T(1,128)S(1)} %get-tuple-element.694), channel_id=1, source_target_pairs={{0,2},{2,4},{4,6},{6,8},{8,10},{10,12},{12,14},{14,16},{16,18},{18... | collective-permute-start | bytes 6152 | tf_op jit(solution)/shard_map/ppermute | solution.py:26
  641.2 6.7 collective-permute-start.43
  694.3 15.9 %collective-permute-start.46 = (f32[2,16,1]{2,1,0:T(8,128)S(1)}, f32[2,16,1]{2,1,0:T(8,128)S(1)}, u32[]{:S(2)}, u32[]{:S(2)}) collective-permute-start(f32[2,16,1]{2,1,0:T(8,128)S(1)} %get-tuple-element.691), channel_id=1, source_target_pairs={{1,0},{3,2},{5,4},{7,6},{9,8},{11,10},{13,12},{15,14},{17,16},{19,... | collective-permute-start | bytes 392 | tf_op jit(solution)/shard_map/ppermute | solution.py:28
  695.6 14.7 %collective-permute-start.44 = (f32[2,1,256]{2,1,0:T(1,128)S(1)}, f32[2,1,256]{2,1,0:T(1,128)S(1)}, u32[]{:S(2)}, u32[]{:S(2)}) collective-permute-start(f32[2,1,256]{2,1,0:T(1,128)S(1)} %get-tuple-element.689), channel_id=1, source_target_pairs={{2,0},{4,2},{6,4},{8,6},{10,8},{12,10},{14,12},{16,14},{18,16},{20... | collective-permute-start | bytes 6152 | tf_op jit(solution)/shard_map/ppermute | solution.py:28
  696.9 13.4 %collective-permute-start.45 = (f32[2,1,256]{2,1,0:T(1,128)S(1)}, f32[2,1,256]{2,1,0:T(1,128)S(1)}, u32[]{:S(2)}, u32[]{:S(2)}) collective-permute-start(f32[2,1,256]{2,1,0:T(1,128)S(1)} %get-tuple-element.690), channel_id=1, source_target_pairs={{0,2},{2,4},{4,6},{6,8},{8,10},{10,12},{12,14},{14,16},{16,18},{18... | collective-permute-start | bytes 6152 | tf_op jit(solution)/shard_map/ppermute | solution.py:26
  703.5 6.7 collective-permute-start.47
  757.1 16.1 %collective-permute-start.50 = (f32[2,16,1]{2,1,0:T(8,128)S(1)}, f32[2,16,1]{2,1,0:T(8,128)S(1)}, u32[]{:S(2)}, u32[]{:S(2)}) collective-permute-start(f32[2,16,1]{2,1,0:T(8,128)S(1)} %get-tuple-element.687), channel_id=1, source_target_pairs={{1,0},{3,2},{5,4},{7,6},{9,8},{11,10},{13,12},{15,14},{17,16},{19,... | collective-permute-start | bytes 392 | tf_op jit(solution)/shard_map/ppermute | solution.py:28
  758.4 14.9 %collective-permute-start.48 = (f32[2,1,256]{2,1,0:T(1,128)S(1)}, f32[2,1,256]{2,1,0:T(1,128)S(1)}, u32[]{:S(2)}, u32[]{:S(2)}) collective-permute-start(f32[2,1,256]{2,1,0:T(1,128)S(1)} %get-tuple-element.685), channel_id=1, source_target_pairs={{2,0},{4,2},{6,4},{8,6},{10,8},{12,10},{14,12},{16,14},{18,16},{20... | collective-permute-start | bytes 6152 | tf_op jit(solution)/shard_map/ppermute | solution.py:28
  759.7 13.6 %collective-permute-start.49 = (f32[2,1,256]{2,1,0:T(1,128)S(1)}, f32[2,1,256]{2,1,0:T(1,128)S(1)}, u32[]{:S(2)}, u32[]{:S(2)}) collective-permute-start(f32[2,1,256]{2,1,0:T(1,128)S(1)} %get-tuple-element.686), channel_id=1, source_target_pairs={{0,2},{2,4},{4,6},{6,8},{8,10},{10,12},{12,14},{14,16},{16,18},{18... | collective-permute-start | bytes 6152 | tf_op jit(solution)/shard_map/ppermute | solution.py:26
  766.2 7.1 collective-permute-start.51
  (1 other events, 0.7 us)
where the time goes:
time: 899 us; the launch traced here: 886 us
  blocking collectives  572 us (64%)
  starting transfers between devices  153 us (17%)
  other arithmetic  52.4 us (6%)
  local copies, waits for them, and re-layouts  48.3 us (5%)
  matrix products  32.9 us (4%)
  between operations  26 us (3%)
    psum x12, blocking collectives, arnoldi(): lax.psum((partial_value, jnp.sum(image * image)), ('sub', 'gx', 'gy'))  499 us
    ppermute x26, starting transfers between devices, padded(): lax.ppermute(tail, axis, [(i, (i + 1) % count) for i in range(ends)])  120 us
    psum x1, blocking collectives, shards(): lax.psum(jnp.sum(forcing * forcing), ('sub', 'gx', 'gy')) + norm_eps  41 us
    another operation x36, other arithmetic  34.7 us
    ppermute x26, starting transfers between devices, padded(): lax.ppermute(head, axis, [((i + 1) % count, i) for i in range(ends)])  33.5 us
    pmax x1, blocking collectives, shards(): column_error = lax.pmax(local_peak, ('sub', 'gx'))  32.4 us
    scatter x23, local copies, waits for them, and re-layouts, arnoldi(): hessenberg.at[:column + 1, column].set(products).at[column + 1, column]  18.1 us
  transfers between devices with their start and end apart: 52, of which 2 were waited for; matrix products, arithmetic and copies ran while one was open for 7% of the time, Pallas kernels for 0%

commit v1 on v0

v1 whole, which is shorter than its diff:
```python
import functools

import jax
import jax.numpy as jnp
from jax import lax
from jax.experimental import pallas as pl
from jax.experimental.pallas import tpu as pltpu
from jax.sharding import PartitionSpec as P

KRYLOV = 12
SUBSTEPS = 4
STEPS = 4
HALO = 16
LANES = 128
SLOTS = 16

dt_total = 4.0
buoyancy_sq = 0.5
norm_eps = 1e-06
taylor_degree = 12
squarings = 8
SHIFT = -2.0
RADIUS = 4.0

ROWS = ("sub", "gx")
ALL = ("sub", "gx", "gy")
HIGH = lax.Precision.HIGHEST
VMEM = pl.BlockSpec(memory_space=pltpu.VMEM)


def iota(shape, dim):
    return lax.broadcasted_iota(jnp.int32, shape, dim)


def rise_rows(x):
    return pltpu.roll(x, x.shape[0] - 1, 0) - pltpu.roll(x, 1, 0)


def rise_columns(x):
    return pltpu.roll(x, x.shape[1] - 1, 1) - pltpu.roll(x, 1, 1)


def grid_mask(rows, columns, halo_rows):
    line, lane = iota((rows, columns), 0), iota((rows, columns), 1)
    place = lax.axis_index("sub") * lax.axis_size("gx") + lax.axis_index("gx")
    last = lax.axis_size("sub") * lax.axis_size("gx") - 1
    side = lax.axis_index("gy")
    first_line = jnp.where(place > 0, 0, halo_rows)
    end_line = jnp.where(place < last, rows, rows - halo_rows)
    body = columns - LANES
    right_end = jnp.where(side < lax.axis_size("gy") - 1, body + LANES // 2, body)
    left_start = jnp.where(side > 0, body + LANES // 2, columns)
    inside = (line >= first_line) & (line < end_line) & ((lane < right_end) | (lane >= left_start))
    return jnp.where(inside, 1.0, 0.0)


def power_step(fields, drag, half):
    vx, vy, b, p = fields
    quarter = dt_total / RADIUS
    return (
        -half * rise_rows(p) - drag[0] * vx,
        -half * rise_columns(p) + quarter * b - drag[1] * vy,
        (-buoyancy_sq * quarter) * vy - drag[2] * b,
        -half * (rise_rows(vx) + rise_columns(vy)) - drag[3] * p,
    )


def pair_rows(one, two):
    total = None
    for f in range(4):
        prod = one[f] * two[f]
        part = None
        for r in range(0, prod.shape[0], 8):
            for c in range(0, prod.shape[1], LANES):
                tile = prod[r : r + 8, c : c + LANES]
                part = tile if part is None else part + tile
        total = part if total is None else total + part
    return jnp.sum(total, axis=0, keepdims=True)


def gram_out(old, new, table_ref, send_ref):
    first = len(old)
    table_ref[...] = jnp.zeros_like(table_ref)
    for j in range(len(new)):
        for i in range(first):
            table_ref[j * SLOTS + i : j * SLOTS + i + 1, :] = pair_rows(old[i](), new[j]())
        for i in range(j + 1):
            row = pair_rows(new[i](), new[j]())
            table_ref[j * SLOTS + first + i : j * SLOTS + first + i + 1, :] = row
            if i != j:
                table_ref[i * SLOTS + first + j : i * SLOTS + first + j + 1, :] = row
    packed = lax.dot_general(
        jnp.ones((8, LANES), jnp.float32),
        table_ref[...],
        (((1,), (1,)), ((), ())),
        precision=HIGH,
        preferred_element_type=jnp.float32,
    )
    for d in range(send_ref.shape[0]):
        send_ref[d] = packed[0:1]


def first_kernel(own_ref, up_ref, down_ref, basis_ref, drag_ref, send_ref, table_ref):
    rows = own_ref.shape[2] + 2 * HALO
    columns = own_ref.shape[3]
    mask = grid_mask(rows, columns, HALO)

    def whole(kind, f):
        joined = jnp.concatenate([up_ref[kind, f], own_ref[kind, f], down_ref[kind, f]], axis=0)
        return jnp.where(mask > 0, joined, 0.0)

    state = [whole(0, f) for f in range(4)]
    damping = [whole(1, f) for f in range(4)]
    vx, vy, b, p = state
    half = 0.5 * mask
    linear = (
        -half * rise_rows(p),
        -half * rise_columns(p) + b,
        -buoyancy_sq * vy,
        -half * (rise_rows(vx) + rise_columns(vy)),
    )
    for f in range(4):
        square = damping[f] * state[f] * state[f]
        basis_ref[0, f] = linear[f] - square * state[f]
        drag_ref[f] = (3.0 * dt_total / RADIUS) * square + SHIFT / RADIUS
    half = (0.5 * dt_total / RADIUS) * mask
    for step in range(STEPS):
        current = [basis_ref[step, f] for f in range(4)]
        drag = [drag_ref[f] for f in range(4)]
        for f, value in enumerate(power_step(current, drag, half)):
            basis_ref[step + 1, f] = value
    body = columns - LANES

    def interior(j):
        return lambda: [basis_ref[j, f, HALO : rows - HALO, :body] for f in range(4)]

    gram_out([], [interior(j) for j in range(STEPS + 1)], table_ref, send_ref)


def gram_matrix(received_ref, first):
    packed = jnp.sum(received_ref[...], axis=0)
    tile = (SLOTS, LANES)
    row, lane = iota(tile, 0), iota(tile, 1)
    tall = (LANES, LANES)
    tall_row, tall_lane = iota(tall, 0), iota(tall, 1)
    packed = jnp.broadcast_to(packed, tile)
    dot = functools.partial(jnp.dot, precision=HIGH, preferred_element_type=jnp.float32)
    by_row = jnp.where(lane % SLOTS == row, packed, 0.0)
    right = dot(by_row, jnp.where(tall_row // SLOTS == tall_lane - first, 1.0, 0.0))
    by_column = jnp.where(lane // SLOTS == row - first, packed, 0.0)
    below = dot(by_column, jnp.where(tall_row % SLOTS == tall_lane, 1.0, 0.0))
    unit = jnp.where(row == lane, 1.0, 0.0)
    return jnp.where(lane >= first, right, jnp.where(row >= first, below, unit)), unit


def orthogonalize(gram, unit, first, hess):
    tile = (SLOTS, LANES)
    row, lane = iota(tile, 0), iota(tile, 1)
    down = lambda x: jnp.sum(x, axis=0, keepdims=True)
    across = lambda x: jnp.sum(x, axis=1, keepdims=True)
    fresh = (row >= first) & (row < first + STEPS)
    chain = jnp.where(fresh & (lane == row), SHIFT, 0.0) + jnp.where(fresh & (lane == row + 1), RADIUS, 0.0)
    steps = hess + chain
    old = row < first
    beta = None
    if first == 0:
        beta = jnp.sqrt(gram[0:1, 0:1] + norm_eps)
        start = 1.0 / beta
    else:
        start = jnp.ones((1, 1), jnp.float32)
    scale = jnp.where(row == first, start, jnp.where(old, 1.0, 0.0))
    coefs = unit * scale
    images = gram * scale
    column = jnp.where(row[:, 0:1] == first, start, 0.0)
    for c in range(first, first + STEPS):
        z = down(steps * column)
        products = across(images * z)
        z = z - down(coefs * products)
        column = across(unit * z)
        image = across(gram * z)
        length = jnp.sqrt(jnp.maximum(down(column * image), 0.0) + norm_eps)
        inverse = 1.0 / length
        hess_row = down(unit * products) + jnp.where(lane[0:1] == c + 1, length, 0.0)
        hess = jnp.where(row == c, hess_row, hess)
        coefs = jnp.where(row == c + 1, z * inverse, coefs)
        images = jnp.where(row == c + 1, down(gram * column) * inverse, images)
        column = column * inverse
    return coefs, hess, beta


def combine(coefs, c, parts):
    total = None
    for i, part in parts:
        term = coefs[c : c + 1, i : i + 1] * part()
        total = term if total is None else total + term
    return total


def next_kernel(first, received_ref, small_ref, drag_in_ref, old_ref, basis_in_ref, basis_ref, kept_ref, small_out_ref, send_ref, table_ref):
    edge = (basis_in_ref.shape[2] - basis_ref.shape[2]) // 2
    rows, columns = basis_ref.shape[2:]
    gram, unit = gram_matrix(received_ref, first)
    hess = small_ref[0] if first else jnp.zeros((SLOTS, LANES), jnp.float32)
    coefs, hess, beta = orthogonalize(gram, unit, first, hess)
    small_out_ref[0] = hess
    small_out_ref[1] = jnp.broadcast_to(beta, (SLOTS, LANES)) if first == 0 else small_ref[1]
    for f in range(4):
        parts = [(first + j, lambda j=j: basis_in_ref[j, f, edge : edge + rows]) for j in range(STEPS + 1)]
        if first:
            for i in range(first):
                kept_ref[i, f] = old_ref[i, f]
            parts = [(i, lambda i=i: old_ref[i, f]) for i in range(first)] + parts
        for c in range(first, first + STEPS):
            kept_ref[c, f] = combine(coefs, c, parts[: c + 1])
        basis_ref[0, f] = combine(coefs, first + STEPS, parts)
    halo = (rows - (drag_in_ref.shape[1] - 2 * HALO)) // 2
    half = (0.5 * dt_total / RADIUS) * grid_mask(rows, columns, halo)
    skip = HALO - halo
    for step in range(STEPS):
        current = [basis_ref[step, f] for f in range(4)]
        drag = [drag_in_ref[f, skip : skip + rows] for f in range(4)]
        for f, value in enumerate(power_step(current, drag, half)):
            basis_ref[step + 1, f] = value
    body = columns - LANES

    def interior(ref, j):
        return lambda: [ref[j, f, halo : rows - halo, :body] for f in range(4)]

    gram_out(
        [interior(kept_ref, i) for i in range(first + STEPS)],
        [interior(basis_ref, j) for j in range(STEPS + 1)],
        table_ref,
        send_ref,
    )


def last_kernel(first, received_ref, small_ref, old_ref, basis_ref, small_out_ref, peak_ref):
    rows, columns = basis_ref.shape[2:]
    body = columns - LANES
    halo = HALO // 2
    gram, unit = gram_matrix(received_ref, first)
    coefs, hess, _ = orthogonalize(gram, unit, first, small_ref[0])
    small_out_ref[0] = hess
    small_out_ref[1] = small_ref[1]
    small_out_ref[2] = coefs
    tiles = body // LANES
    for f in range(4):
        parts = [(i, lambda i=i: old_ref[i, f, halo : rows - halo, :body]) for i in range(first)]
        parts += [(first + j, lambda j=j: basis_ref[j, f, halo : rows - halo, :body]) for j in range(STEPS + 1)]
        peak = jnp.max(jnp.abs(combine(coefs, KRYLOV, parts)), axis=0, keepdims=True)
        for d in range(peak_ref.shape[0]):
            for t in range(tiles):
                peak_ref[d, f * tiles + t : f * tiles + t + 1, :] = peak[:, t * LANES : (t + 1) * LANES]


def finish_kernel(first, weights_ref, small_ref, state_ref, old_ref, basis_ref, peaks_ref, combined_ref, error_ref):
    rows, columns = basis_ref.shape[2:]
    body = columns - LANES
    halo = HALO // 2
    hess, beta, coefs = small_ref[0], small_ref[1, 0:1, 0:1], small_ref[2]
    dot = functools.partial(jnp.dot, precision=HIGH, preferred_element_type=jnp.float32)
    size = SUBSTEPS * SLOTS
    row, lane = iota((size, LANES), 0), iota((size, LANES), 1)
    row_in, lane_in = row % SLOTS, lane % SLOTS
    same = (row // SLOTS == lane // SLOTS) & (lane < size)
    spread = jnp.where(iota((LANES, LANES), 0) == iota((LANES, LANES), 1) % SLOTS, 1.0, 0.0)
    wide = dot(jnp.concatenate([hess] * SUBSTEPS, axis=0), spread)
    fraction = ((row // SLOTS) + 1).astype(jnp.float32) * (1.0 / SUBSTEPS)
    scaled = jnp.where(same & (row_in < KRYLOV) & (lane_in < KRYLOV), wide * fraction, 0.0)
    scaled = scaled + jnp.where(same & (row_in == KRYLOV) & (lane_in == 0), 1.0, 0.0)
    scaled = scaled * (1.0 / 2.0**squarings)
    unit = jnp.where(row == lane, 1.0, 0.0)
    pad = jnp.zeros((LANES - size, LANES), jnp.float32)

    def times(a, b):
        return dot(a, jnp.concatenate([b, pad], axis=0))

    result, term = unit, unit
    for degree in range(1, taylor_degree + 1):
        term = times(term, scaled) * (1.0 / degree)
        result = result + term
    for _ in range(squarings):
        result = times(result, result)
    mixing = jnp.zeros((1, LANES), jnp.float32)
    highest = jnp.zeros((1, 1), jnp.float32)
    gather = jnp.where(iota((LANES, LANES), 0) % SLOTS == iota((LANES, LANES), 1), 1.0, 0.0)
    for k in range(SUBSTEPS):
        tau = (k + 1) / SUBSTEPS
        factor = dt_total * tau
        g = result[k * SLOTS + KRYLOV : k * SLOTS + KRYLOV + 1, :]
        mixing = mixing + jnp.where(lane[0:1] // SLOTS == k, weights_ref[k] * factor, 0.0) * beta * g
        last = jnp.abs(g[:, k * SLOTS + KRYLOV - 1 : k * SLOTS + KRYLOV])
        estimate = (factor * tau) * beta * hess[KRYLOV - 1 : KRYLOV, KRYLOV : KRYLOV + 1] * last
        highest = jnp.maximum(highest, estimate)
    mixing = jnp.where(lane_in[0:1] < KRYLOV, mixing, 0.0)
    mixing = dot(jnp.broadcast_to(mixing, (8, LANES)), gather)
    coef_pad = jnp.concatenate([coefs, jnp.zeros((LANES - SLOTS, LANES), jnp.float32)], axis=0)
    share = dot(jnp.where(iota((8, LANES), 1) < KRYLOV, mixing, 0.0), coef_pad)
    for f in range(4):
        parts = [(i, lambda i=i: old_ref[i, f, halo : rows - halo, :body]) for i in range(first)]
        parts += [(first + j, lambda j=j: basis_ref[j, f, halo : rows - halo, :body]) for j in range(STEPS + 1)]
        combined_ref[f] = state_ref[f] + combine(share, 0, parts)
    peak = jnp.max(peaks_ref[...], axis=0) * highest
    tiles = body // LANES
    for f in range(4):
        for t in range(tiles):
            error_ref[f : f + 1, t * LANES : (t + 1) * LANES] = peak[f * tiles + t : f * tiles + t + 1]


def shards(state, damping, weights):
    fields, height, width = state.shape
    body = width
    columns = width + LANES
    devices = lax.axis_size("sub") * lax.axis_size("gx") * lax.axis_size("gy")
    lines = lax.axis_size("sub") * lax.axis_size("gx")
    sides = lax.axis_size("gy")
    f32 = functools.partial(jax.ShapeDtypeStruct, dtype=jnp.float32)
    pair = jnp.stack([state, damping])
    head, tail = pair[..., :LANES], pair[..., body - LANES :]
    if sides == 2:
        halo = lax.ppermute(jnp.where(lax.axis_index("gy") == 0, tail, head), "gy", [(0, 1), (1, 0)])
    else:
        from_right = lax.ppermute(head, "gy", [((i + 1) % sides, i) for i in range(sides)])
        from_left = lax.ppermute(tail, "gy", [(i, (i + 1) % sides) for i in range(sides)])
        halo = jnp.concatenate([from_right[..., : LANES // 2], from_left[..., LANES // 2 :]], axis=-1)
    own = jnp.concatenate([pair, halo], axis=-1)
    up = lax.ppermute(own[:, :, height - HALO :], ROWS, [(i, (i + 1) % lines) for i in range(lines)])
    down = lax.ppermute(own[:, :, :HALO], ROWS, [((i + 1) % lines, i) for i in range(lines)])

    def call(body_fn, outs, *args, smem=(), scratch=()):
        specs = [pl.BlockSpec(memory_space=pltpu.SMEM) if k in smem else VMEM for k in range(len(args))]
        return pl.pallas_call(
            body_fn,
            out_shape=outs,
            in_specs=specs,
            out_specs=[VMEM] * len(outs),
            scratch_shapes=list(scratch),
        )(*args)

    table = pltpu.VMEM((LANES, LANES), jnp.float32)
    send_shape = f32((devices, 1, LANES))
    small_shape = f32((2, SLOTS, LANES))
    tall = height + 2 * HALO
    short = height + HALO
    basis, drag, send = call(
        first_kernel,
        [f32((STEPS + 1, fields, tall, columns)), f32((fields, tall, columns)), send_shape],
        own,
        up,
        down,
        scratch=[table],
    )
    exchange = lambda x, axes: lax.all_to_all(x, axes, 0, 0)
    received = exchange(send, ALL)
    small = jnp.zeros((2, SLOTS, LANES), jnp.float32)
    kept = drag
    for first in range(0, KRYLOV - STEPS, STEPS):
        basis, kept, small, send = call(
            functools.partial(next_kernel, first),
            [
                f32((STEPS + 1, fields, short, columns)),
                f32((first + STEPS, fields, short, columns)),
                small_shape,
                send_shape,
            ],
            received,
            small,
            drag,
            kept,
            basis,
            scratch=[table],
        )
        received = exchange(send, ALL)
    first = KRYLOV - STEPS
    peak_rows = fields * (body // LANES)
    small, peaks = call(
        functools.partial(last_kernel, first),
        [f32((3, SLOTS, LANES)), f32((lines, peak_rows, LANES))],
        received,
        small,
        kept,
        basis,
    )
    peaks = exchange(peaks, ROWS)
    combined, column_error = call(
        functools.partial(finish_kernel, first),
        [f32((fields, height, width)), f32((fields, width))],
        weights,
        small,
        state,
        kept,
        basis,
        peaks,
        smem=(0,),
    )
    return combined, column_error


def solution(mesh):
    return jax.shard_map(
        shards,
        mesh=mesh,
        in_specs=(P(None, ROWS, "gy"), P(None, ROWS, "gy"), P()),
        out_specs=(P(None, ROWS, "gy"), P(None, "gy")),
        check_vma=False,
    )
```

time: 899 us -> 87 us (0.10); the launches traced: 886 us -> 86.4 us
  blocking collectives: 572 us -> 42.3 us
  starting transfers between devices: 153 us -> 6.44 us
  other arithmetic: 52.4 us -> 1.71 us
  local copies, waits for them, and re-layouts: 48.3 us -> 1.29 us
  matrix products: 32.9 us -> 0 us
  between operations: 26 us -> 0.66 us
  Pallas kernels: 0 us -> 22.4 us
  waiting for transfers between devices: 0.88 us -> 11.6 us
    psum x13 -> x0, blocking collectives: 540 us -> none  [the longest x12 499 us: arnoldi(): lax.psum((partial_value, jnp.sum(image * image)), ('sub', 'gx', 'gy'))]
    ppermute x52 -> x3, starting transfers between devices: 153 us -> 6.44 us  [the longest x1 3.38 us: shards(): lax.ppermute(own[:, :, :HALO], ROWS, [((i + 1) % lines, i) for i in range...]
    all_to_all x0 -> x4, blocking collectives: none -> 42.3 us  [shards(): exchange = lambda x, axes: lax.all_to_all(x, axes, 0, 0)]
    another operation x38 -> x0, other arithmetic: 34.8 us -> none
    dot_general x103 -> x0, matrix products: 32.9 us -> none  [the longest x11 14 us: arnoldi(): jnp.dot(basis[:column + 1], image, precision=lax.Precision.HIGHEST)]
    pmax x1 -> x0, blocking collectives: 32.4 us -> none  [shards(): column_error = lax.pmax(local_peak, ('sub', 'gx'))]
    scatter x43 -> x0, local copies, waits for them, and re-layouts: 31.5 us -> none  [the longest x23 18.1 us: arnoldi(): hessenberg.at[:column + 1, column].set(products).at[column + 1, column]]
    pallas_call x0 -> x5, Pallas kernels: none -> 22.4 us  [call(): pl.pallas_call(body_fn, out_shape=outs, in_specs=specs, out_specs=[VMEM]...]
  transfers between devices with their start and end apart: 52 -> 3, of which waited for: 2 -> 3; matrix products, arithmetic and copies ran while one was open for 7% -> 0% of each run, Pallas kernels for 0% -> 0%
where the time goes in v1:
time: 87 us; the launch traced here: 86.4 us
  blocking collectives  42.3 us (49%)
  Pallas kernels  22.4 us (26%)
  waiting for transfers between devices  11.6 us (13%)
  starting transfers between devices  6.44 us (7%)
  other arithmetic  1.71 us (2%)
  local copies, waits for them, and re-layouts  1.29 us (1%)
    all_to_all x4, blocking collectives, shards(): exchange = lambda x, axes: lax.all_to_all(x, axes, 0, 0)  42.3 us
    pallas_call x5, Pallas kernels, call(): pl.pallas_call(body_fn, out_shape=outs, in_specs=specs, out_specs=[VMEM]...  22.4 us
    ppermute x1, waiting for transfers between devices, shards(): lax.ppermute(own[:, :, :HALO], ROWS, [((i + 1) % lines, i) for i in range...  5.13 us
    ppermute x1, waiting for transfers between devices, shards(): lax.ppermute(own[:, :, height - HALO:], ROWS, [(i, (i + 1) % lines) for i...  4.21 us
    ppermute x1, starting transfers between devices, shards(): lax.ppermute(own[:, :, :HALO], ROWS, [((i + 1) % lines, i) for i in range...  3.38 us
    ppermute x1, starting transfers between devices, shards(): lax.ppermute(jnp.where(lax.axis_index('gy') == 0, tail, head), 'gy', [(0,...  3.06 us
    ppermute x1, waiting for transfers between devices, shards(): lax.ppermute(jnp.where(lax.axis_index('gy') == 0, tail, head), 'gy', [(0,...  2.25 us
  transfers between devices with their start and end apart: 3, of which 3 were waited for; matrix products, arithmetic and copies ran while one was open for 0% of the time, Pallas kernels for 0%

profile of v1, /device:TPU:0, one launch (start us, length us, event | category | flops | bytes accessed | tf_op | source)
XLA Modules:
  0.0 86.4 jit_solution(2630508566624523398)
XLA Ops:
  0.6 0.8 fusion.1
  1.5 3.1 %collective-permute-start = (f32[2,4,16,128]{3,2,1,0:T(8,128)S(1)}, f32[2,4,16,128]{3,2,1,0:T(8,128)S(1)}, u32[]{:S(2)}, u32[]{:S(2)}) collective-permute-start(f32[2,4,16,128]{3,2,1,0:T(8,128)S(1)} %fusion.1), channel_id=1, source_target_pairs={{0,1},{1,0},{2,3},{3,2},{4,5},{5,4},{6,7},{7,6},{8,9},{9,8},{10,11... | collective-permute-start | bytes 196616 | tf_op jit(solution)/shard_map/ppermute | solution.py:321
  4.5 2.2 %collective-permute-done = f32[2,4,16,128]{3,2,1,0:T(8,128)S(1)} collective-permute-done((f32[2,4,16,128]{3,2,1,0:T(8,128)S(1)}, f32[2,4,16,128]{3,2,1,0:T(8,128)S(1)}, u32[]{:S(2)}, u32[]{:S(2)}) %collective-permute-start) | collective-permute-done | bytes 65568 | tf_op jit(solution)/shard_map/ppermute | solution.py:321
  6.8 0.9 %pad_maximum_fusion.own_ref = f32[2,4,16,384]{3,2,1,0:T(8,128)S(1)} fusion(f32[2,4,16,128]{3,2,1,0:T(8,128)S(1)} %collective-permute-done, f32[1,4,16,256]{3,2,1,0:T(8,128)} %bitcast.5, f32[1,4,16,256]{3,2,1,0:T(8,128)} %bitcast.3), kind=kLoop, calls=%fused_computation | loop fusion | flops 98304 | bytes 393216 | tf_op jit(solution)/shard_map/concatenate | solution.py:326
  7.7 0.0 copy-start
  7.7 3.4 %collective-permute-start.2 = (f32[2,4,16,384]{3,2,1,0:T(8,128)S(1)}, f32[2,4,16,384]{3,2,1,0:T(8,128)S(1)}, u32[]{:S(2)}, u32[]{:S(2)}) collective-permute-start(f32[2,4,16,384]{3,2,1,0:T(8,128)S(1)} %pad_maximum_fusion.own_ref), channel_id=1, source_target_pairs={{2,0},{4,2},{6,4},{8,6},{10,8},{12,10},{14,12},{16,14},{18,16},{20... | collective-permute-start | bytes 589832 | tf_op jit(solution)/shard_map/ppermute | solution.py:328
  11.0 0.0 collective-permute-start.1
  11.0 5.1 %collective-permute-done.2.down_ref = f32[2,4,16,384]{3,2,1,0:T(8,128)S(1)} collective-permute-done((f32[2,4,16,384]{3,2,1,0:T(8,128)S(1)}, f32[2,4,16,384]{3,2,1,0:T(8,128)S(1)}, u32[]{:S(2)}, u32[]{:S(2)}) %collective-permute-start.2) | collective-permute-done | bytes 196640 | tf_op jit(solution)/shard_map/ppermute | solution.py:328
  16.2 0.0 copy-start.1
  16.2 4.2 %collective-permute-done.1.up_ref = f32[2,4,16,384]{3,2,1,0:T(8,128)S(1)} collective-permute-done((f32[2,4,16,384]{3,2,1,0:T(8,128)S(1)}, f32[2,4,16,384]{3,2,1,0:T(8,128)S(1)}, u32[]{:S(2)}, u32[]{:S(2)}) %collective-permute-start.1) | collective-permute-done | bytes 196640 | tf_op jit(solution)/shard_map/ppermute | solution.py:327
  20.4 0.0 copy-done
  20.4 0.0 copy-done.1
  20.4 0.0 copy-start.2
  20.4 0.7 copy-done.2
  21.1 2.9 %shard_map.50 = (f32[5,4,48,384]{3,2,1,0:T(8,128)}, f32[4,48,384]{2,1,0:T(8,128)}, f32[32,1,128]{2,1,0:T(1,128)}) custom-call(f32[2,4,16,384]{3,2,1,0:T(8,128)} %copy-done, f32[2,4,16,384]{3,2,1,0:T(8,128)} %copy-done.2, f32[2,4,16,384]{3,2,1,0:T(8,128)} %copy-done.1), custom_call_target="tpu_custom_call" | custom-call | tf_op jit(solution)/shard_map/pallas_call | solution.py:332
  24.0 11.0 %all_to_all.20.received_ref = f32[32,1,128]{2,1,0:T(1,128)} all-to-all(f32[32,1,128]{2,1,0:T(1,128)} %get-tuple-element.15), channel_id=1, replica_groups=mesh['sub'=4,'gx'=4,'gy'=2] {'sub','gx','gy'}, dimensions={0} | all-to-all | bytes 32768 | tf_op jit(solution)/shard_map/all_to_all | solution.py:353
  35.0 0.6 broadcast_in_dim.3.small_ref
  35.6 4.6 %shard_map.51 = (f32[5,4,32,384]{3,2,1,0:T(8,128)}, f32[4,4,32,384]{3,2,1,0:T(8,128)}, f32[2,16,128]{2,1,0:T(8,128)}, f32[32,1,128]{2,1,0:T(1,128)}) custom-call(f32[32,1,128]{2,1,0:T(1,128)} %all_to_all.20.received_ref, f32[2,16,128]{2,1,0:T(8,128)} %broadcast_in_dim.3.small_ref, f32[4,48,384]{2,1,0:T(8,128)} %get-tuple-element.16.drag_in_ref.old_ref, ...), custom_call_target="tpu_custom_call" | custom-call | tf_op jit(solution)/shard_map/pallas_call | solution.py:332
  40.2 10.3 %all_to_all.21.received_ref = f32[32,1,128]{2,1,0:T(1,128)} all-to-all(f32[32,1,128]{2,1,0:T(1,128)} %get-tuple-element.18), channel_id=1, replica_groups=mesh['sub'=4,'gx'=4,'gy'=2] {'sub','gx','gy'}, dimensions={0} | all-to-all | bytes 32768 | tf_op jit(solution)/shard_map/all_to_all | solution.py:353
  50.5 4.9 %shard_map.52 = (f32[5,4,32,384]{3,2,1,0:T(8,128)}, f32[8,4,32,384]{3,2,1,0:T(8,128)}, f32[2,16,128]{2,1,0:T(8,128)}, f32[32,1,128]{2,1,0:T(1,128)}) custom-call(f32[32,1,128]{2,1,0:T(1,128)} %all_to_all.21.received_ref, f32[2,16,128]{2,1,0:T(8,128)} %get-tuple-element.19.small_ref, f32[4,48,384]{2,1,0:T(8,128)} %get-tuple-element.16.drag_in_ref.old_ref, ...), custom_call_target="tpu_custom_call" | custom-call | tf_op jit(solution)/shard_map/pallas_call | solution.py:332
  55.4 10.3 %all_to_all.22.received_ref = f32[32,1,128]{2,1,0:T(1,128)} all-to-all(f32[32,1,128]{2,1,0:T(1,128)} %get-tuple-element.22), channel_id=1, replica_groups=mesh['sub'=4,'gx'=4,'gy'=2] {'sub','gx','gy'}, dimensions={0} | all-to-all | bytes 32768 | tf_op jit(solution)/shard_map/all_to_all | solution.py:353
  65.7 3.6 %shard_map.53 = (f32[3,16,128]{2,1,0:T(8,128)}, f32[16,8,128]{2,1,0:T(8,128)}) custom-call(f32[32,1,128]{2,1,0:T(1,128)} %all_to_all.22.received_ref, f32[2,16,128]{2,1,0:T(8,128)} %get-tuple-element.23.small_ref, f32[8,4,32,384]{3,2,1,0:T(8,128)} %get-tuple-element.24.old_ref, f32[5,4,32,384]{3,2,1,0:T(8,128)} %get-tuple-element.25.basis_ref), custom_call_target="tpu_custom_call" | custom-call | tf_op jit(solution)/shard_map/pallas_call | solution.py:332
  69.3 10.8 %all_to_all.23.peaks_ref = f32[16,8,128]{2,1,0:T(8,128)} all-to-all(f32[16,8,128]{2,1,0:T(8,128)} %get-tuple-element.27), channel_id=1, replica_groups=mesh['sub'=4,'gx'=4,'gy'=2] {'sub','gx'}, dimensions={0} | all-to-all | bytes 131072 | tf_op jit(solution)/shard_map/all_to_all | solution.py:353
  80.1 6.4 %shard_map.54 = (f32[4,16,256]{2,1,0:T(8,128)}, f32[4,256]{1,0:T(4,128)}) custom-call(f32[4]{0:T(128)} %weights_ref.1, f32[3,16,128]{2,1,0:T(8,128)} %get-tuple-element.26.small_ref, f32[4,16,256]{2,1,0:T(8,128)} %state_ref.1, f32[8,4,32,384]{3,2,1,0:T(8,128)} %get-tuple-element.24.old_ref, f32[5,4,32,384]{3,2,1,0:T(8,128)} %get-tuple-element.25.basis_ref, ...), custom_call_target="tpu_custom_call" | custom-call | tf_op jit(solution)/shard_map/pallas_call | solution.py:332
Async XLA Ops:
  1.5 5.3 %collective-permute-start = (f32[2,4,16,128]{3,2,1,0:T(8,128)S(1)}, f32[2,4,16,128]{3,2,1,0:T(8,128)S(1)}, u32[]{:S(2)}, u32[]{:S(2)}) collective-permute-start(f32[2,4,16,128]{3,2,1,0:T(8,128)S(1)} %fusion.1), channel_id=1, source_target_pairs={{0,1},{1,0},{2,3},{3,2},{4,5},{5,4},{6,7},{7,6},{8,9},{9,8},{10,11... | collective-permute-start | bytes 196616 | tf_op jit(solution)/shard_map/ppermute | solution.py:321
  7.7 12.7 %copy-start = (f32[2,4,16,384]{3,2,1,0:T(8,128)}, f32[2,4,16,384]{3,2,1,0:T(8,128)S(1)}, u32[]{:S(2)}) copy-start(f32[2,4,16,384]{3,2,1,0:T(8,128)S(1)} %pad_maximum_fusion.own_ref) | copy-start | bytes 589828
  7.7 8.5 %collective-permute-start.2 = (f32[2,4,16,384]{3,2,1,0:T(8,128)S(1)}, f32[2,4,16,384]{3,2,1,0:T(8,128)S(1)}, u32[]{:S(2)}, u32[]{:S(2)}) collective-permute-start(f32[2,4,16,384]{3,2,1,0:T(8,128)S(1)} %pad_maximum_fusion.own_ref), channel_id=1, source_target_pairs={{2,0},{4,2},{6,4},{8,6},{10,8},{12,10},{14,12},{16,14},{18,16},{20... | collective-permute-start | bytes 589832 | tf_op jit(solution)/shard_map/ppermute | solution.py:328
  11.0 9.3 %collective-permute-start.1 = (f32[2,4,16,384]{3,2,1,0:T(8,128)S(1)}, f32[2,4,16,384]{3,2,1,0:T(8,128)S(1)}, u32[]{:S(2)}, u32[]{:S(2)}) collective-permute-start(f32[2,4,16,384]{3,2,1,0:T(8,128)S(1)} %pad_maximum_fusion.own_ref), channel_id=1, source_target_pairs={{0,2},{2,4},{4,6},{6,8},{8,10},{10,12},{12,14},{14,16},{16,18},{18... | collective-permute-start | bytes 589832 | tf_op jit(solution)/shard_map/ppermute | solution.py:327
  16.2 4.2 %copy-start.1 = (f32[2,4,16,384]{3,2,1,0:T(8,128)}, f32[2,4,16,384]{3,2,1,0:T(8,128)S(1)}, u32[]{:S(2)}) copy-start(f32[2,4,16,384]{3,2,1,0:T(8,128)S(1)} %collective-permute-done.2.down_ref) | copy-start | bytes 589828
  20.4 0.7 copy-start.2

commit v2 on v1

--- a/solution.py
+++ b/solution.py
@@ -315,6 +315,7 @@
     lines = lax.axis_size("sub") * lax.axis_size("gx")
     sides = lax.axis_size("gy")
     f32 = functools.partial(jax.ShapeDtypeStruct, dtype=jnp.float32)
+    near = lambda shape: pltpu.VMEM(shape, jnp.float32)
     pair = jnp.stack([state, damping])
     head, tail = pair[..., :LANES], pair[..., body - LANES :]
     if sides == 2:
@@ -329,22 +330,24 @@
 
     def call(body_fn, outs, *args, smem=(), scratch=()):
         specs = [pl.BlockSpec(memory_space=pltpu.SMEM) if k in smem else VMEM for k in range(len(args))]
+        args = [a if k in smem else pltpu.with_memory_space_constraint(a, pltpu.VMEM) for k, a in enumerate(args)]
         return pl.pallas_call(
             body_fn,
             out_shape=outs,
             in_specs=specs,
             out_specs=[VMEM] * len(outs),
             scratch_shapes=list(scratch),
+            compiler_params=pltpu.CompilerParams(vmem_limit_bytes=16 * 2**20),
         )(*args)
 
     table = pltpu.VMEM((LANES, LANES), jnp.float32)
-    send_shape = f32((devices, 1, LANES))
-    small_shape = f32((2, SLOTS, LANES))
+    send_shape = near((devices, 1, LANES))
+    small_shape = near((2, SLOTS, LANES))
     tall = height + 2 * HALO
     short = height + HALO
     basis, drag, send = call(
         first_kernel,
-        [f32((STEPS + 1, fields, tall, columns)), f32((fields, tall, columns)), send_shape],
+        [near((STEPS + 1, fields, tall, columns)), near((fields, tall, columns)), send_shape],
         own,
         up,
         down,
@@ -358,8 +361,8 @@
         basis, kept, small, send = call(
             functools.partial(next_kernel, first),
             [
-                f32((STEPS + 1, fields, short, columns)),
-                f32((first + STEPS, fields, short, columns)),
+                near((STEPS + 1, fields, short, columns)),
+                near((first + STEPS, fields, short, columns)),
                 small_shape,
                 send_shape,
             ],
@@ -375,7 +378,7 @@
     peak_rows = fields * (body // LANES)
     small, peaks = call(
         functools.partial(last_kernel, first),
-        [f32((3, SLOTS, LANES)), f32((lines, peak_rows, LANES))],
+        [near((3, SLOTS, LANES)), near((lines, peak_rows, LANES))],
         received,
         small,
         kept,

time: 87 us -> 70 us (0.80)
  Pallas kernels: 22.4 us -> 11.4 us
  blocking collectives: 42.3 us -> 37.8 us
  local copies, waits for them, and re-layouts: 1.29 us -> 0.02 us
    pallas_call x5, Pallas kernels: 22.4 us -> 11.4 us  [call(): pl.pallas_call(body_fn, out_shape=outs, in_specs=specs, out_specs=[VMEM]...]
    all_to_all x4, blocking collectives: 42.3 us -> 37.8 us  [shards(): exchange = lambda x, axes: lax.all_to_all(x, axes, 0, 0)]
where the time goes in v2:
time: 70 us; the launch traced here: 69.6 us
  blocking collectives  37.8 us (54%)
  waiting for transfers between devices  11.6 us (17%)
  Pallas kernels  11.4 us (16%)
  starting transfers between devices  6.44 us (9%)
  other arithmetic  1.71 us (2%)
  between operations  0.72 us (1%)
    all_to_all x4, blocking collectives, shards(): exchange = lambda x, axes: lax.all_to_all(x, axes, 0, 0)  37.8 us
    pallas_call x5, Pallas kernels, call(): pl.pallas_call(body_fn, out_shape=outs, in_specs=specs, out_specs=[VMEM]...  11.4 us
    ppermute x1, waiting for transfers between devices, shards(): lax.ppermute(own[:, :, :HALO], ROWS, [((i + 1) % lines, i) for i in range...  5.13 us
    ppermute x1, waiting for transfers between devices, shards(): lax.ppermute(own[:, :, height - HALO:], ROWS, [(i, (i + 1) % lines) for i...  4.21 us
    ppermute x1, starting transfers between devices, shards(): lax.ppermute(own[:, :, :HALO], ROWS, [((i + 1) % lines, i) for i in range...  3.38 us
    ppermute x1, starting transfers between devices, shards(): lax.ppermute(jnp.where(lax.axis_index('gy') == 0, tail, head), 'gy', [(0,...  3.06 us
    ppermute x1, waiting for transfers between devices, shards(): lax.ppermute(jnp.where(lax.axis_index('gy') == 0, tail, head), 'gy', [(0,...  2.25 us
  transfers between devices with their start and end apart: 3, of which 3 were waited for; matrix products, arithmetic and copies ran while one was open for 0% of the time, Pallas kernels for 0%

profile of v2, /device:TPU:0, one launch (start us, length us, event | category | flops | bytes accessed | tf_op | source)
XLA Modules:
  0.0 69.6 jit_solution(1644297475418927202)
XLA Ops:
  0.6 0.8 %fusion.1 = f32[2,4,16,128]{3,2,1,0:T(8,128)S(1)} fusion(f32[1,4,16,256]{3,2,1,0:T(8,128)} %bitcast.2, f32[1,4,16,256]{3,2,1,0:T(8,128)} %bitcast.4, pred[]{:T(512)S(6)} %eq.3), kind=kLoop, calls=%fused_computation.4 | loop fusion | flops 49152 | bytes 196609 | tf_op jit(solution)/shard_map/jit(_where)/select_n | solution.py:322
  1.5 3.1 %collective-permute-start = (f32[2,4,16,128]{3,2,1,0:T(8,128)S(1)}, f32[2,4,16,128]{3,2,1,0:T(8,128)S(1)}, u32[]{:S(2)}, u32[]{:S(2)}) collective-permute-start(f32[2,4,16,128]{3,2,1,0:T(8,128)S(1)} %fusion.1), channel_id=1, source_target_pairs={{0,1},{1,0},{2,3},{3,2},{4,5},{5,4},{6,7},{7,6},{8,9},{9,8},{10,11... | collective-permute-start | bytes 196616 | tf_op jit(solution)/shard_map/ppermute | solution.py:322
  4.5 2.2 %collective-permute-done = f32[2,4,16,128]{3,2,1,0:T(8,128)S(1)} collective-permute-done((f32[2,4,16,128]{3,2,1,0:T(8,128)S(1)}, f32[2,4,16,128]{3,2,1,0:T(8,128)S(1)}, u32[]{:S(2)}, u32[]{:S(2)}) %collective-permute-start) | collective-permute-done | bytes 65568 | tf_op jit(solution)/shard_map/ppermute | solution.py:322
  6.8 0.9 %pad_maximum_fusion.own_ref = f32[2,4,16,384]{3,2,1,0:T(8,128)S(1)} fusion(f32[2,4,16,128]{3,2,1,0:T(8,128)S(1)} %collective-permute-done, f32[1,4,16,256]{3,2,1,0:T(8,128)} %bitcast.5, f32[1,4,16,256]{3,2,1,0:T(8,128)} %bitcast.3), kind=kLoop, calls=%fused_computation | loop fusion | flops 98304 | bytes 393216 | tf_op jit(solution)/shard_map/concatenate | solution.py:327
  7.7 3.4 %collective-permute-start.2 = (f32[2,4,16,384]{3,2,1,0:T(8,128)S(1)}, f32[2,4,16,384]{3,2,1,0:T(8,128)S(1)}, u32[]{:S(2)}, u32[]{:S(2)}) collective-permute-start(f32[2,4,16,384]{3,2,1,0:T(8,128)S(1)} %pad_maximum_fusion.own_ref), channel_id=1, source_target_pairs={{2,0},{4,2},{6,4},{8,6},{10,8},{12,10},{14,12},{16,14},{18,16},{20... | collective-permute-start | bytes 589832 | tf_op jit(solution)/shard_map/ppermute | solution.py:329
  11.0 0.0 collective-permute-start.1
  11.0 5.1 %collective-permute-done.2.down_ref = f32[2,4,16,384]{3,2,1,0:T(8,128)S(1)} collective-permute-done((f32[2,4,16,384]{3,2,1,0:T(8,128)S(1)}, f32[2,4,16,384]{3,2,1,0:T(8,128)S(1)}, u32[]{:S(2)}, u32[]{:S(2)}) %collective-permute-start.2) | collective-permute-done | bytes 196640 | tf_op jit(solution)/shard_map/ppermute | solution.py:329
  16.2 4.2 %collective-permute-done.1.up_ref = f32[2,4,16,384]{3,2,1,0:T(8,128)S(1)} collective-permute-done((f32[2,4,16,384]{3,2,1,0:T(8,128)S(1)}, f32[2,4,16,384]{3,2,1,0:T(8,128)S(1)}, u32[]{:S(2)}, u32[]{:S(2)}) %collective-permute-start.1) | collective-permute-done | bytes 196640 | tf_op jit(solution)/shard_map/ppermute | solution.py:328
  20.4 0.7 %shard_map.50 = (f32[5,4,48,384]{3,2,1,0:T(8,128)S(1)}, f32[4,48,384]{2,1,0:T(8,128)S(1)}, f32[32,1,128]{2,1,0:T(1,128)S(1)}) custom-call(f32[2,4,16,384]{3,2,1,0:T(8,128)S(1)} %pad_maximum_fusion.own_ref, f32[2,4,16,384]{3,2,1,0:T(8,128)S(1)} %collective-permute-done.1.up_ref, f32[2,4,16,384]{3,2,1,0:T(8,128)S(1)} %collective-permute-done.2.down_ref), custom_call_target="tpu_custom_call" | custom-call | tf_op jit(solution)/shard_map/pallas_call | solution.py:334
  21.1 10.8 %all_to_all.20.received_ref = f32[32,1,128]{2,1,0:T(1,128)S(1)} all-to-all(f32[32,1,128]{2,1,0:T(1,128)S(1)} %get-tuple-element.15), channel_id=1, replica_groups=mesh['sub'=4,'gx'=4,'gy'=2] {'sub','gx','gy'}, dimensions={0} | all-to-all | bytes 32768 | tf_op jit(solution)/shard_map/all_to_all | solution.py:356
  31.9 2.0 %shard_map.51 = (f32[5,4,32,384]{3,2,1,0:T(8,128)S(1)}, f32[4,4,32,384]{3,2,1,0:T(8,128)S(1)}, f32[2,16,128]{2,1,0:T(8,128)S(1)}, f32[32,1,128]{2,1,0:T(1,128)S(1)}) custom-call(f32[32,1,128]{2,1,0:T(1,128)S(1)} %all_to_all.20.received_ref, f32[2,16,128]{2,1,0:T(8,128)S(1)} %broadcast_in_dim.3.small_ref, ...), custom_call_target="tpu_custom_call" | custom-call | tf_op jit(solution)/shard_map/pallas_call | solution.py:334
  33.9 8.8 %all_to_all.21.received_ref = f32[32,1,128]{2,1,0:T(1,128)S(1)} all-to-all(f32[32,1,128]{2,1,0:T(1,128)S(1)} %get-tuple-element.18), channel_id=1, replica_groups=mesh['sub'=4,'gx'=4,'gy'=2] {'sub','gx','gy'}, dimensions={0} | all-to-all | bytes 32768 | tf_op jit(solution)/shard_map/all_to_all | solution.py:356
  42.7 2.3 %shard_map.52 = (f32[5,4,32,384]{3,2,1,0:T(8,128)S(1)}, f32[8,4,32,384]{3,2,1,0:T(8,128)S(1)}, f32[2,16,128]{2,1,0:T(8,128)S(1)}, f32[32,1,128]{2,1,0:T(1,128)S(1)}) custom-call(f32[32,1,128]{2,1,0:T(1,128)S(1)} %all_to_all.21.received_ref, f32[2,16,128]{2,1,0:T(8,128)S(1)} %get-tuple-element.19.small_ref, ...), custom_call_target="tpu_custom_call" | custom-call | tf_op jit(solution)/shard_map/pallas_call | solution.py:334
  45.0 0.0 copy-start
  45.0 0.0 copy-start.1
  45.0 9.0 %all_to_all.22.received_ref = f32[32,1,128]{2,1,0:T(1,128)S(1)} all-to-all(f32[32,1,128]{2,1,0:T(1,128)S(1)} %get-tuple-element.22), channel_id=1, replica_groups=mesh['sub'=4,'gx'=4,'gy'=2] {'sub','gx','gy'}, dimensions={0} | all-to-all | bytes 32768 | tf_op jit(solution)/shard_map/all_to_all | solution.py:356
  54.0 1.2 %shard_map.53 = (f32[3,16,128]{2,1,0:T(8,128)S(1)}, f32[16,8,128]{2,1,0:T(8,128)S(1)}) custom-call(f32[32,1,128]{2,1,0:T(1,128)S(1)} %all_to_all.22.received_ref, f32[2,16,128]{2,1,0:T(8,128)S(1)} %get-tuple-element.23.small_ref, f32[8,4,32,384]{3,2,1,0:T(8,128)S(1)} %get-tuple-element.24.old_ref, f32[5,4,32,384]{3,2,1,0:T(8,128)S(1)} %get-tuple-element.25.basis_ref), custom_call_target="tpu_custom_call" | custom-call | tf_op jit(solution)/shard_map/pallas_call | solution.py:334
  55.3 9.2 %all_to_all.23.peaks_ref = f32[16,8,128]{2,1,0:T(8,128)S(1)} all-to-all(f32[16,8,128]{2,1,0:T(8,128)S(1)} %get-tuple-element.27), channel_id=1, replica_groups=mesh['sub'=4,'gx'=4,'gy'=2] {'sub','gx'}, dimensions={0} | all-to-all | bytes 131072 | tf_op jit(solution)/shard_map/all_to_all | solution.py:356
  64.4 0.0 copy-done
  64.5 0.0 copy-done.1
  64.5 5.1 %shard_map.54 = (f32[4,16,256]{2,1,0:T(8,128)}, f32[4,256]{1,0:T(4,128)}) custom-call(f32[4]{0:T(128)S(1)} %copy-done.1, f32[3,16,128]{2,1,0:T(8,128)S(1)} %get-tuple-element.26.small_ref, f32[4,16,256]{2,1,0:T(8,128)S(1)} %copy-done, f32[8,4,32,384]{3,2,1,0:T(8,128)S(1)} %get-tuple-element.24.old_ref, f32[5,4,32,384]{3,2,1,0:T(8,128)S(1)} %get-tuple-element.25.basis_ref, ...), custom_call_target="tpu_custom_call" | custom-call | tf_op jit(solution)/shard_map/pallas_call | solution.py:334
  (1 shorter events, 0.0 us)
Async XLA Ops:
  1.5 5.3 %collective-permute-start = (f32[2,4,16,128]{3,2,1,0:T(8,128)S(1)}, f32[2,4,16,128]{3,2,1,0:T(8,128)S(1)}, u32[]{:S(2)}, u32[]{:S(2)}) collective-permute-start(f32[2,4,16,128]{3,2,1,0:T(8,128)S(1)} %fusion.1), channel_id=1, source_target_pairs={{0,1},{1,0},{2,3},{3,2},{4,5},{5,4},{6,7},{7,6},{8,9},{9,8},{10,11... | collective-permute-start | bytes 196616 | tf_op jit(solution)/shard_map/ppermute | solution.py:322
  7.7 8.5 %collective-permute-start.2 = (f32[2,4,16,384]{3,2,1,0:T(8,128)S(1)}, f32[2,4,16,384]{3,2,1,0:T(8,128)S(1)}, u32[]{:S(2)}, u32[]{:S(2)}) collective-permute-start(f32[2,4,16,384]{3,2,1,0:T(8,128)S(1)} %pad_maximum_fusion.own_ref), channel_id=1, source_target_pairs={{2,0},{4,2},{6,4},{8,6},{10,8},{12,10},{14,12},{16,14},{18,16},{20... | collective-permute-start | bytes 589832 | tf_op jit(solution)/shard_map/ppermute | solution.py:329
  11.0 9.3 %collective-permute-start.1 = (f32[2,4,16,384]{3,2,1,0:T(8,128)S(1)}, f32[2,4,16,384]{3,2,1,0:T(8,128)S(1)}, u32[]{:S(2)}, u32[]{:S(2)}) collective-permute-start(f32[2,4,16,384]{3,2,1,0:T(8,128)S(1)} %pad_maximum_fusion.own_ref), channel_id=1, source_target_pairs={{0,2},{2,4},{4,6},{6,8},{8,10},{10,12},{12,14},{14,16},{16,18},{18... | collective-permute-start | bytes 589832 | tf_op jit(solution)/shard_map/ppermute | solution.py:328
  45.0 19.4 %copy-start = (f32[4,16,256]{2,1,0:T(8,128)S(1)}, f32[4,16,256]{2,1,0:T(8,128)}, u32[]{:S(2)}) copy-start(f32[4,16,256]{2,1,0:T(8,128)} %state_ref.1) | copy-start | bytes 196612
  45.0 19.4 %copy-start.1 = (f32[4]{0:T(128)S(1)}, f32[4]{0:T(128)}, u32[]{:S(2)}) copy-start(f32[4]{0:T(128)} %weights_ref.1) | copy-start | bytes 52

commit v3 on v2

v3 whole, which is shorter than its diff:
```python
import functools
import math

import jax
import jax.numpy as jnp
from jax import lax
from jax.experimental import pallas as pl
from jax.experimental.pallas import tpu as pltpu
from jax.sharding import PartitionSpec as P

KRYLOV = 12
SUBSTEPS = 4
BLOCKS = (5, 7)
HALO = 16
LANES = 128
SLOTS = 16
EDGE = 16

dt_total = 4.0
buoyancy_sq = 0.5
norm_eps = 1e-06
taylor_degree = 12
squarings = 8
SHIFT = -2.0
RADIUS = 4.0

ROWS = ("sub", "gx")
ALL = ("sub", "gx", "gy")
HIGH = lax.Precision.HIGHEST
VMEM = pl.BlockSpec(memory_space=pltpu.VMEM)


def iota(shape, dim):
    return lax.broadcasted_iota(jnp.int32, shape, dim)


def rise_rows(x):
    return pltpu.roll(x, x.shape[0] - 1, 0) - pltpu.roll(x, 1, 0)


def rise_columns(x):
    return pltpu.roll(x, x.shape[1] - 1, 1) - pltpu.roll(x, 1, 1)


def grid_mask(rows, columns, halo_rows):
    line, lane = iota((rows, columns), 0), iota((rows, columns), 1)
    place = lax.axis_index("sub") * lax.axis_size("gx") + lax.axis_index("gx")
    last = lax.axis_size("sub") * lax.axis_size("gx") - 1
    side = lax.axis_index("gy")
    first_line = jnp.where(place > 0, 0, halo_rows)
    end_line = jnp.where(place < last, rows, rows - halo_rows)
    body = columns - LANES
    right_end = jnp.where(side < lax.axis_size("gy") - 1, body + EDGE, body)
    left_start = jnp.where(side > 0, columns - EDGE, columns)
    inside = (line >= first_line) & (line < end_line) & ((lane < right_end) | (lane >= left_start))
    return jnp.where(inside, 1.0, 0.0)


def power_step(fields, drag, half):
    vx, vy, b, p = fields
    quarter = dt_total / RADIUS
    return (
        -half * rise_rows(p) - drag[0] * vx,
        -half * rise_columns(p) + quarter * b - drag[1] * vy,
        (-buoyancy_sq * quarter) * vy - drag[2] * b,
        -half * (rise_rows(vx) + rise_columns(vy)) - drag[3] * p,
    )


def two_sum(a, b):
    total = a + b
    part = total - a
    return total, (a - (total - part)) + (b - part)


def pair_sum(one, two):
    total, error = two_sum(one[0], two[0])
    return total, one[1] + two[1] + error


def split(a):
    scaled = 4097.0 * a
    high = scaled - (scaled - a)
    return high, a - high


def add_product(total, a, b, b_parts):
    product = a * b
    a_high, a_low = split(a)
    error = ((a_high * b_parts[0] - product) + a_high * b_parts[1] + a_low * b_parts[0]) + a_low * b_parts[1]
    high, rest = two_sum(total[0], product)
    return high, total[1] + (rest + error)


def tree_sum(tiles):
    while len(tiles) > 1:
        tiles = [pair_sum(tiles[k], tiles[k + 1]) for k in range(0, len(tiles) - 1, 2)] + tiles[len(tiles) // 2 * 2 :]
    total = tiles[0]
    for shift in (4, 2, 1):
        total = pair_sum(total, (pltpu.roll(total[0], shift, 0), pltpu.roll(total[1], shift, 0)))
    return total


def pair_rows(one, two):
    total = None
    for f in range(4):
        prod = one[f] * two[f]
        part = None
        for r in range(0, prod.shape[0], 8):
            for c in range(0, prod.shape[1], LANES):
                tile = prod[r : r + 8, c : c + LANES]
                part = tile if part is None else part + tile
        total = part if total is None else total + part
    return jnp.sum(total, axis=0, keepdims=True)


def gram_out(old, new, table_ref, send_ref):
    first = len(old)
    table_ref[...] = jnp.zeros_like(table_ref)
    for j in range(len(new)):
        for i in range(first):
            table_ref[j * SLOTS + i : j * SLOTS + i + 1, :] = pair_rows(old[i](), new[j]())
        for i in range(j + 1):
            row = pair_rows(new[i](), new[j]())
            table_ref[j * SLOTS + first + i : j * SLOTS + first + i + 1, :] = row
            if i != j:
                table_ref[i * SLOTS + first + j : i * SLOTS + first + j + 1, :] = row
    turned = jnp.transpose(table_ref[...])
    zero = jnp.zeros((8, LANES), jnp.float32)
    high, low = tree_sum([(turned[r : r + 8], zero) for r in range(0, LANES, 8)])
    for d in range(send_ref.shape[0]):
        send_ref[d, 0:1] = high[0:1]
        send_ref[d, 1:2] = low[0:1]


def edge_kernel(state_ref, damping_ref, *edge_refs):
    width = state_ref.shape[2]
    lane = iota((state_ref.shape[1], LANES), 1)

    def packed(pick):
        total = None
        for k in range(8):
            ref = state_ref if k < 4 else damping_ref
            head, tail = ref[k % 4, :, :LANES], ref[k % 4, :, width - LANES :]
            tile = pltpu.roll(pick(head, pltpu.roll(tail, EDGE, 1)), k * EDGE, 1) if k else pick(head, pltpu.roll(tail, EDGE, 1))
            total = tile if total is None else jnp.where(lane // EDGE == k, tile, total)
        return total

    if len(edge_refs) == 1:
        left = lax.axis_index("gy") == 0
        edge_refs[0][...] = packed(lambda head, tail: jnp.where(left, tail, head))
    else:
        edge_refs[0][...] = packed(lambda head, tail: head)
        edge_refs[1][...] = packed(lambda head, tail: tail)


def pack_kernel(count, state_ref, damping_ref, *refs):
    halo_refs, out_refs = refs[:count], refs[count:]
    height, width = state_ref.shape[1:]
    for out_ref, start in zip(out_refs, (height - HALO, 0)):
        lines = slice(start, start + HALO)
        at = 0
        for k in range(8):
            ref = state_ref if k < 4 else damping_ref
            for c in range(0, width, LANES):
                out_ref[at : at + HALO] = ref[k % 4, lines, c : c + LANES]
                at += HALO
        for halo_ref in halo_refs:
            out_ref[at : at + HALO] = halo_ref[lines]
            at += HALO


def first_kernel(count, state_ref, damping_ref, *refs):
    halo_refs = refs[:count]
    up_ref, down_ref, basis_ref, drag_ref, send_ref, table_ref = refs[count:]
    height, width = state_ref.shape[1:]
    rows, columns = height + 2 * HALO, width + LANES
    tiles = width // LANES
    mask = grid_mask(rows, columns, HALO)

    def side_tile(k, right, left):
        lane = iota(right.shape, 1)
        right = pltpu.roll(right, LANES - k * EDGE, 1) if k else right
        return jnp.where(lane < LANES // 2, right, pltpu.roll(left, LANES - (k + 1) * EDGE, 1) if k < 7 else left)

    def neighbour(ref, k):
        parts = [ref[(k * tiles + t) * HALO : (k * tiles + t + 1) * HALO] for t in range(tiles)]
        at = 8 * tiles * HALO
        ends = [ref[at + c * HALO : at + (c + 1) * HALO] for c in range(count)]
        return jnp.concatenate(parts + [side_tile(k, ends[0], ends[-1])], axis=1)

    def whole(k):
        ref = state_ref if k < 4 else damping_ref
        own = jnp.concatenate([ref[k % 4], side_tile(k, halo_refs[0][...], halo_refs[-1][...])], axis=1)
        joined = jnp.concatenate([neighbour(up_ref, k), own, neighbour(down_ref, k)], axis=0)
        return jnp.where(mask > 0, joined, 0.0)

    state = [whole(f) for f in range(4)]
    damping = [whole(4 + f) for f in range(4)]
    vx, vy, b, p = state
    half = 0.5 * mask
    linear = (
        -half * rise_rows(p),
        -half * rise_columns(p) + b,
        -buoyancy_sq * vy,
        -half * (rise_rows(vx) + rise_columns(vy)),
    )
    for f in range(4):
        square = damping[f] * state[f] * state[f]
        basis_ref[0, f] = linear[f] - square * state[f]
        drag_ref[f] = (3.0 * dt_total / RADIUS) * square
    half = (0.5 * dt_total / RADIUS) * mask
    drag = [drag_ref[f] + SHIFT / RADIUS for f in range(4)]
    steps = BLOCKS[0]
    for step in range(steps):
        current = [basis_ref[step, f] for f in range(4)]
        for f, value in enumerate(power_step(current, drag, half)):
            basis_ref[step + 1, f] = value

    def interior(j):
        return lambda: [basis_ref[j, f, HALO : rows - HALO, :width] for f in range(4)]

    gram_out([], [interior(j) for j in range(steps + 1)], table_ref, send_ref)


dot = functools.partial(jnp.dot, precision=HIGH, preferred_element_type=jnp.float32)
TILE = (SLOTS, LANES)


def tall(x):
    return jnp.concatenate([x, jnp.zeros((LANES - x.shape[0], LANES), jnp.float32)], axis=0)


def down_sum(x):
    return jnp.sum(x, axis=0, keepdims=True)


def across_sum(x):
    return jnp.sum(x, axis=1, keepdims=True)


def gram_matrix(received_ref, first):
    devices = received_ref.shape[0]
    parts = [(received_ref[d : d + 8, 0, :], received_ref[d : d + 8, 1, :]) for d in range(0, devices, 8)]
    packed = jnp.concatenate([jnp.concatenate([part, part], axis=0) for part in tree_sum(parts)], axis=0)
    row, lane = iota((2 * SLOTS, LANES), 0) % SLOTS, iota((2 * SLOTS, LANES), 1)
    tall_row, tall_lane = iota((LANES, LANES), 0), iota((LANES, LANES), 1)
    by_row = jnp.where(lane % SLOTS == row, packed, 0.0)
    right = dot(by_row, jnp.where(tall_row // SLOTS == tall_lane - first, 1.0, 0.0))
    by_column = jnp.where(lane // SLOTS == row - first, packed, 0.0)
    below = dot(by_column, jnp.where((tall_row % SLOTS == tall_lane) & (tall_lane < SLOTS), 1.0, 0.0))
    both = jnp.where(lane >= first, right, jnp.where(row >= first, below, 0.0))
    return both[:SLOTS] + old_unit(first), both[SLOTS:]


def old_unit(first):
    row, lane = iota(TILE, 0), iota(TILE, 1)
    return jnp.where((row == lane) & (row < first), 1.0, 0.0)


def gram_schmidt(gram, steps, start, hess, first, count):
    row, lane = iota(TILE, 0), iota(TILE, 1)
    unit = jnp.where(row == lane, 1.0, 0.0)
    scale = jnp.where(row == first, start, jnp.where(row < first, 1.0, 0.0))
    coefs = unit * scale
    images = gram * scale
    column = jnp.where(row[:, 0:1] == first, start, 0.0)
    for c in range(first, first + count):
        z = down_sum(steps * column)
        products = across_sum(images * z)
        z = z - down_sum(coefs * products)
        column = across_sum(unit * z)
        image = across_sum(gram * z)
        length = jnp.sqrt(jnp.maximum(down_sum(column * image), 0.0) + norm_eps)
        inverse = 1.0 / length
        hess_row = down_sum(unit * products) + jnp.where(lane[0:1] == c + 1, length, 0.0)
        hess = jnp.where(row == c, hess_row, hess)
        coefs = jnp.where(row == c + 1, z * inverse, coefs)
        images = jnp.where(row == c + 1, down_sum(gram * column) * inverse, images)
        column = column * inverse
    return coefs, hess


def refined_gram(coefs, gram, gram_low, first, count):
    row, lane = iota(TILE, 0), iota(TILE, 1)
    slots = range(first + count + 1)
    gram_parts = split(gram)
    zero = jnp.zeros(TILE, jnp.float32)
    image = (zero, zero)
    for j in slots:
        line = slice(j, j + 1)
        column = coefs[:, line]
        image = add_product(image, column, gram[line], [part[line] for part in gram_parts])
        image = image[0], image[1] + column * gram_low[line]
    turned = dot(jnp.where(row == lane, 1.0, 0.0), jnp.transpose(tall(coefs)))
    turned_parts = split(turned)
    result = (zero, zero)
    for i in slots:
        line = slice(i, i + 1)
        result = add_product(result, image[0][:, line], turned[line], [part[line] for part in turned_parts])
        result = result[0], result[1] + image[1][:, line] * turned[line]
    inner = (row < first) & (lane < first)
    return jnp.where(inner, old_unit(first), result[0] + result[1])


def basis_terms(hess, first):
    if first == 0:
        return jnp.full((1, 1), SHIFT, jnp.float32), jnp.zeros((1, 1), jnp.float32)
    c = first - 1
    shift = 0.5 * (hess[c - 1 : c, c - 1 : c] + hess[c : c + 1, c : c + 1])
    return shift, hess[c : c + 1, c - 1 : c]


def orthogonalize(received_ref, hess, first, count):
    gram, gram_low = gram_matrix(received_ref, first)
    row, lane = iota(TILE, 0), iota(TILE, 1)
    shift, back = basis_terms(hess, first)
    fresh = (row >= first) & (row < first + count)
    chain = jnp.where(lane == row, shift, 0.0) + jnp.where(lane == row + 1, RADIUS, 0.0)
    chain = chain + jnp.where((lane == row - 1) & (row > first), back, 0.0)
    steps = hess + jnp.where(fresh, chain, 0.0)
    one = jnp.ones((1, 1), jnp.float32)
    beta = jnp.sqrt(gram[0:1, 0:1] + norm_eps)
    coefs, image = gram_schmidt(gram, steps, one if first else 1.0 / beta, hess, first, count)
    gram = refined_gram(coefs, gram, gram_low, first, count)
    again, hess = gram_schmidt(gram, image, one, hess, first, count)
    return dot(again, tall(coefs)), hess, beta


def combine(coefs, c, parts):
    total = None
    for i, part in parts:
        term = coefs[c : c + 1, i : i + 1] * part()
        total = term if total is None else total + term
    return total


def middle_kernel(received_ref, drag_in_ref, basis_in_ref, basis_ref, kept_ref, small_ref, send_ref, table_ref):
    first, count = BLOCKS
    rows, columns = basis_ref.shape[2:]
    edge = (basis_in_ref.shape[2] - rows) // 2
    halo = HALO - edge
    body = columns - LANES
    coefs, hess, beta = orthogonalize(received_ref, jnp.zeros(TILE, jnp.float32), 0, first)
    small_ref[0] = hess
    small_ref[1] = jnp.broadcast_to(beta, TILE)
    for f in range(4):
        inner = [(j, lambda j=j: basis_in_ref[j, f, HALO : edge + rows - halo, :body]) for j in range(first + 1)]
        for c in range(first):
            kept_ref[c, f] = combine(coefs, c, inner[: c + 1])
        outer = [(j, lambda j=j: basis_in_ref[j, f, edge : edge + rows]) for j in range(first + 1)]
        basis_ref[0, f] = combine(coefs, first, outer)
    shift, back = basis_terms(hess, first)
    back = back * (1.0 / RADIUS)
    half = (0.5 * dt_total / RADIUS) * grid_mask(rows, columns, halo)
    drag = [drag_in_ref[f, edge : edge + rows] + shift * (1.0 / RADIUS) for f in range(4)]
    for step in range(count):
        current = [basis_ref[step, f] for f in range(4)]
        for f, value in enumerate(power_step(current, drag, half)):
            basis_ref[step + 1, f] = value - back * basis_ref[step - 1, f] if step else value

    def interior(ref, j, lines):
        return lambda: [ref[j, f, lines, :body] for f in range(4)]

    gram_out(
        [interior(kept_ref, i, slice(None)) for i in range(first)],
        [interior(basis_ref, j, slice(halo, rows - halo)) for j in range(count + 1)],
        table_ref,
        send_ref,
    )


def block_parts(kept_ref, basis_ref, f):
    first, count = BLOCKS
    height, body = kept_ref.shape[2:]
    halo = (basis_ref.shape[2] - height) // 2
    parts = [(i, lambda i=i: kept_ref[i, f]) for i in range(first)]
    return parts + [(first + j, lambda j=j: basis_ref[j, f, halo : halo + height, :body]) for j in range(count + 1)]


def last_kernel(received_ref, small_ref, kept_ref, basis_ref, small_out_ref, peak_ref):
    body = kept_ref.shape[3]
    coefs, hess, _ = orthogonalize(received_ref, small_ref[0], *BLOCKS)
    small_out_ref[0] = hess
    small_out_ref[1] = small_ref[1]
    small_out_ref[2] = coefs
    tiles = body // LANES
    for f in range(4):
        peak = jnp.max(jnp.abs(combine(coefs, KRYLOV, block_parts(kept_ref, basis_ref, f))), axis=0, keepdims=True)
        for d in range(peak_ref.shape[0]):
            for t in range(tiles):
                peak_ref[d, f * tiles + t : f * tiles + t + 1, :] = peak[:, t * LANES : (t + 1) * LANES]


def finish_kernel(weights_ref, small_ref, state_ref, kept_ref, basis_ref, peaks_ref, combined_ref, error_ref):
    body = kept_ref.shape[3]
    hess, beta, coefs = small_ref[0], small_ref[1, 0:1, 0:1], small_ref[2]
    size = SUBSTEPS * SLOTS
    row, lane = iota((size, LANES), 0), iota((size, LANES), 1)
    row_in, lane_in = row % SLOTS, lane % SLOTS
    same = (row // SLOTS == lane // SLOTS) & (lane < size)
    lower = jnp.where((row_in < KRYLOV) & (lane < KRYLOV), jnp.concatenate([hess] * SUBSTEPS, axis=0), 0.0)
    wide = lower
    for k in range(1, SUBSTEPS):
        wide = jnp.where(lane // SLOTS == k, pltpu.roll(lower, k * SLOTS, 1), wide)
    fraction = ((row // SLOTS) + 1).astype(jnp.float32) * (1.0 / SUBSTEPS)
    scaled = jnp.where(same, wide * fraction, 0.0)
    scaled = scaled + jnp.where(same & (row_in == KRYLOV) & (lane_in == 0), 1.0, 0.0)
    scaled = scaled * (1.0 / 2.0**squarings)
    unit = jnp.where(row == lane, 1.0, 0.0)

    def times(a, b):
        return dot(a, tall(b))

    power = [unit, scaled, times(scaled, scaled)]
    power += [times(power[2], scaled), times(power[2], power[2])]

    def group(k, count):
        total = None
        for i in range(count):
            term = power[i] * (1.0 / math.factorial(k + i))
            total = term if total is None else total + term
        return total

    top = taylor_degree - 4
    result = group(top, 5)
    while top > 0:
        top -= 4
        result = times(result, power[4]) + group(top, 4)
    for _ in range(squarings):
        result = times(result, result)
    mixing = jnp.zeros((1, LANES), jnp.float32)
    highest = jnp.zeros((1, 1), jnp.float32)
    for k in range(SUBSTEPS):
        tau = (k + 1) / SUBSTEPS
        factor = dt_total * tau
        g = result[k * SLOTS + KRYLOV : k * SLOTS + KRYLOV + 1, :]
        g = pltpu.roll(g, LANES - k * SLOTS, 1) if k else g
        mixing = mixing + weights_ref[k] * factor * beta * g
        estimate = (factor * tau) * beta * hess[KRYLOV - 1 : KRYLOV, KRYLOV : KRYLOV + 1] * jnp.abs(g[:, KRYLOV - 1 : KRYLOV])
        highest = jnp.maximum(highest, estimate)
    mixing = jnp.where(lane[0:8] < KRYLOV, jnp.broadcast_to(mixing, (8, LANES)), 0.0)
    share = dot(mixing, tall(coefs))
    for f in range(4):
        combined_ref[f] = state_ref[f] + combine(share, 0, block_parts(kept_ref, basis_ref, f))
    peak = jnp.max(peaks_ref[...], axis=0) * highest
    tiles = body // LANES
    for f in range(4):
        for t in range(tiles):
            error_ref[f : f + 1, t * LANES : (t + 1) * LANES] = peak[f * tiles + t : f * tiles + t + 1]


def shards(state, damping, weights):
    fields, height, width = state.shape
    columns = width + LANES
    lines = lax.axis_size("sub") * lax.axis_size("gx")
    sides = lax.axis_size("gy")
    devices = lines * sides
    f32 = lambda *shape: jax.ShapeDtypeStruct(shape, jnp.float32)
    near = lambda *shape: pltpu.VMEM(shape, jnp.float32)

    def call(kernel, outs, *args, smem=(), scratch=()):
        specs = [pl.BlockSpec(memory_space=pltpu.SMEM) if k in smem else VMEM for k in range(len(args))]
        args = [a if k in smem else pltpu.with_memory_space_constraint(a, pltpu.VMEM) for k, a in enumerate(args)]
        return pl.pallas_call(
            kernel,
            out_shape=outs,
            in_specs=specs,
            out_specs=[VMEM] * len(outs),
            scratch_shapes=list(scratch),
            compiler_params=pltpu.CompilerParams(vmem_limit_bytes=16 * 2**20),
        )(*args)

    exchange = lambda x, axes: lax.all_to_all(x, axes, 0, 0)
    table = near(LANES, LANES)
    send_shape = near(devices, 2, LANES)
    short = height + HALO
    first, count = BLOCKS

    edges = call(edge_kernel, [near(height, LANES)] * (1 if sides == 2 else 2), state, damping)
    if sides == 2:
        halos = [lax.ppermute(edges[0], "gy", [(0, 1), (1, 0)])]
    else:
        halos = [
            lax.ppermute(edges[0], "gy", [((i + 1) % sides, i) for i in range(sides)]),
            lax.ppermute(edges[1], "gy", [(i, (i + 1) % sides) for i in range(sides)]),
        ]
    number = len(halos)
    stack = (8 * (width // LANES) + number) * HALO
    packs = call(
        functools.partial(pack_kernel, number),
        [near(stack, LANES)] * (1 if height == HALO else 2),
        state,
        damping,
        *halos,
    )
    up = lax.ppermute(packs[0], ROWS, [(i, (i + 1) % lines) for i in range(lines)])
    down = lax.ppermute(packs[-1], ROWS, [((i + 1) % lines, i) for i in range(lines)])
    tall_rows = height + 2 * HALO
    basis, drag, send = call(
        functools.partial(first_kernel, number),
        [near(first + 1, fields, tall_rows, columns), near(fields, tall_rows, columns), send_shape],
        state,
        damping,
        *halos,
        up,
        down,
        scratch=[table],
    )
    basis, kept, small, send = call(
        middle_kernel,
        [near(count + 1, fields, short, columns), near(first, fields, height, width), near(2, *TILE), send_shape],
        exchange(send, ALL),
        drag,
        basis,
        scratch=[table],
    )
    small, peaks = call(
        last_kernel,
        [near(3, *TILE), near(lines, fields * (width // LANES), LANES)],
        exchange(send, ALL),
        small,
        kept,
        basis,
    )
    combined, column_error = call(
        finish_kernel,
        [f32(fields, height, width), f32(fields, width)],
        weights,
        small,
        state,
        kept,
        basis,
        exchange(peaks, ROWS),
        smem=(0,),
    )
    return combined, column_error


def solution(mesh):
    return jax.shard_map(
        shards,
        mesh=mesh,
        in_specs=(P(None, ROWS, "gy"), P(None, ROWS, "gy"), P()),
        out_specs=(P(None, ROWS, "gy"), P(None, "gy")),
        check_vma=False,
    )
```

time: 70 us -> 59.6 us (0.85)
  blocking collectives: 37.8 us -> 28.7 us
  waiting for transfers between devices: 11.6 us -> 9.19 us
  other arithmetic: 1.71 us -> 0 us
  local copies, waits for them, and re-layouts: 0.02 us -> 1.68 us
  Pallas kernels: 11.4 us -> 12.7 us
    all_to_all x4 -> x3, blocking collectives: 37.8 us -> 28.7 us  [shards(): exchange = lambda x, axes: lax.all_to_all(x, axes, 0, 0)]
    ppermute x3, waiting for transfers between devices: 11.6 us -> 9.19 us  [the longest x1 3.9 us: shards(): lax.ppermute(packs[-1], ROWS, [((i + 1) % lines, i) for i in range(lines)])]
    unnamed x4 -> x6, local copies, waits for them, and re-layouts: 0.01 us -> 1.68 us
    pallas_call x5 -> x6, Pallas kernels: 11.4 us -> 12.7 us  [call(): pl.pallas_call(kernel, out_shape=outs, in_specs=specs, out_specs=[VMEM] *...]
    concatenate x1 -> x0, other arithmetic: 0.89 us -> none  [shards(): own = jnp.concatenate([pair, halo], axis=-1)]
    select_n x1 -> x0, other arithmetic: 0.82 us -> none  [shards(): jnp.where(lax.axis_index('gy') == 0, tail, head)]
where the time goes in v3:
time: 59.6 us; the launch traced here: 59.3 us
  blocking collectives  28.7 us (48%)
  Pallas kernels  12.7 us (21%)
  waiting for transfers between devices  9.19 us (15%)
  starting transfers between devices  6.43 us (11%)
  local copies, waits for them, and re-layouts  1.68 us (3%)
  between operations  0.67 us (1%)
    all_to_all x3, blocking collectives, shards(): exchange = lambda x, axes: lax.all_to_all(x, axes, 0, 0)  28.7 us
    pallas_call x6, Pallas kernels, call(): pl.pallas_call(kernel, out_shape=outs, in_specs=specs, out_specs=[VMEM] *...  12.7 us
    ppermute x1, waiting for transfers between devices, shards(): lax.ppermute(packs[-1], ROWS, [((i + 1) % lines, i) for i in range(lines)])  3.9 us
    ppermute x1, waiting for transfers between devices, shards(): lax.ppermute(packs[0], ROWS, [(i, (i + 1) % lines) for i in range(lines)])  3.66 us
    ppermute x1, starting transfers between devices, shards(): lax.ppermute(packs[-1], ROWS, [((i + 1) % lines, i) for i in range(lines)])  3.38 us
    ppermute x1, starting transfers between devices, shards(): halos = [lax.ppermute(edges[0], 'gy', [(0, 1), (1, 0)])]  3.05 us
    unnamed x6, local copies, waits for them, and re-layouts  1.68 us
    ppermute x1, waiting for transfers between devices, shards(): halos = [lax.ppermute(edges[0], 'gy', [(0, 1), (1, 0)])]  1.63 us
  transfers between devices with their start and end apart: 3, of which 3 were waited for; matrix products, arithmetic and copies ran while one was open for 0% of the time, Pallas kernels for 0%

profile of v3, /device:TPU:0, one launch (start us, length us, event | category | flops | bytes accessed | tf_op | source)
XLA Modules:
  0.0 59.3 jit_solution(2308896743655765875)
XLA Ops:
  0.6 0.0 copy-start
  0.6 0.8 %copy-done = f32[4,16,256]{2,1,0:T(8,128)S(1)} copy-done((f32[4,16,256]{2,1,0:T(8,128)S(1)}, f32[4,16,256]{2,1,0:T(8,128)}, u32[]{:S(2)}) %copy-start) | copy-done | bytes 65560
  1.5 0.0 copy-start.1
  1.5 0.8 %copy-done.1 = f32[4,16,256]{2,1,0:T(8,128)S(1)} copy-done((f32[4,16,256]{2,1,0:T(8,128)S(1)}, f32[4,16,256]{2,1,0:T(8,128)}, u32[]{:S(2)}) %copy-start.1) | copy-done | bytes 65560
  2.3 0.1 shard_map.50
  2.5 3.1 %collective-permute-start = (f32[16,128]{1,0:T(8,128)S(1)}, f32[16,128]{1,0:T(8,128)S(1)}, u32[]{:S(2)}, u32[]{:S(2)}) collective-permute-start(f32[16,128]{1,0:T(8,128)S(1)} %shard_map.50), channel_id=1, source_target_pairs={{0,1},{1,0},{2,3},{3,2},{4,5},{5,4},{6,7},{7,6},{8,9},{9,8},{10,11... | collective-permute-start | bytes 24584 | tf_op jit(solution)/shard_map/ppermute | solution.py:482
  5.5 1.6 %collective-permute-done.refs_0_ = f32[16,128]{1,0:T(8,128)S(1)} collective-permute-done((f32[16,128]{1,0:T(8,128)S(1)}, f32[16,128]{1,0:T(8,128)S(1)}, u32[]{:S(2)}, u32[]{:S(2)}) %collective-permute-start) | collective-permute-done | bytes 8224 | tf_op jit(solution)/shard_map/ppermute | solution.py:482
  7.2 3.4 %collective-permute-start.2 = (f32[272,128]{1,0:T(8,128)S(1)}, f32[272,128]{1,0:T(8,128)S(1)}, u32[]{:S(2)}, u32[]{:S(2)}) collective-permute-start(f32[272,128]{1,0:T(8,128)S(1)} %shard_map.51), channel_id=1, source_target_pairs={{2,0},{4,2},{6,4},{8,6},{10,8},{12,10},{14,12},{16,14},{18,16},{20... | collective-permute-start | bytes 417800 | tf_op jit(solution)/shard_map/ppermute | solution.py:498
  10.5 0.0 collective-permute-start.1
  10.5 3.9 %collective-permute-done.2.refs_2_ = f32[272,128]{1,0:T(8,128)S(1)} collective-permute-done((f32[272,128]{1,0:T(8,128)S(1)}, f32[272,128]{1,0:T(8,128)S(1)}, u32[]{:S(2)}, u32[]{:S(2)}) %collective-permute-start.2) | collective-permute-done | bytes 139296 | tf_op jit(solution)/shard_map/ppermute | solution.py:498
  14.4 3.7 %collective-permute-done.1.refs_1_ = f32[272,128]{1,0:T(8,128)S(1)} collective-permute-done((f32[272,128]{1,0:T(8,128)S(1)}, f32[272,128]{1,0:T(8,128)S(1)}, u32[]{:S(2)}, u32[]{:S(2)}) %collective-permute-start.1) | collective-permute-done | bytes 139296 | tf_op jit(solution)/shard_map/ppermute | solution.py:497
  18.1 1.1 %shard_map.52 = (f32[6,4,48,384]{3,2,1,0:T(8,128)S(1)}, f32[4,48,384]{2,1,0:T(8,128)S(1)}, f32[32,2,128]{2,1,0:T(2,128)S(1)}) custom-call(f32[4,16,256]{2,1,0:T(8,128)S(1)} %copy-done, f32[4,16,256]{2,1,0:T(8,128)S(1)} %copy-done.1, f32[16,128]{1,0:T(8,128)S(1)} %collective-permute-done.refs_0_, f32[272,128]{1,0:T(8,128)S(1)} %collective-permute-done.1.refs_1_, ...), custom_call_target="tpu_custom_call" | custom-call | tf_op jit(solution)/shard_map/pallas_call | solution.py:465
  19.2 10.6 %all_to_all.15.received_ref = f32[32,2,128]{2,1,0:T(2,128)S(1)} all-to-all(f32[32,2,128]{2,1,0:T(2,128)S(1)} %get-tuple-element.11), channel_id=1, replica_groups=mesh['sub'=4,'gx'=4,'gy'=2] {'sub','gx','gy'}, dimensions={0} | all-to-all | bytes 65536 | tf_op jit(solution)/shard_map/all_to_all | solution.py:474
  29.7 0.0 copy-start.2
  29.7 4.0 %shard_map.53 = (f32[8,4,32,384]{3,2,1,0:T(8,128)S(1)}, f32[5,4,16,256]{3,2,1,0:T(8,128)S(1)}, f32[2,16,128]{2,1,0:T(8,128)S(1)}, f32[32,2,128]{2,1,0:T(2,128)S(1)}) custom-call(f32[32,2,128]{2,1,0:T(2,128)S(1)} %all_to_all.15.received_ref, f32[4,48,384]{2,1,0:T(8,128)S(1)} %get-tuple-element.12.drag_in_ref, f32[6,4,48,384]{3,2,1,0:T(8,128)S(1)} %get-tuple-element.13.basis_in_ref), custom_call_target="tpu_custom_call" | custom-call | tf_op jit(solution)/shard_map/pallas_call | solution.py:465
  33.7 8.9 %all_to_all.16.received_ref = f32[32,2,128]{2,1,0:T(2,128)S(1)} all-to-all(f32[32,2,128]{2,1,0:T(2,128)S(1)} %get-tuple-element.14), channel_id=1, replica_groups=mesh['sub'=4,'gx'=4,'gy'=2] {'sub','gx','gy'}, dimensions={0} | all-to-all | bytes 65536 | tf_op jit(solution)/shard_map/all_to_all | solution.py:474
  42.6 3.8 %shard_map.54 = (f32[3,16,128]{2,1,0:T(8,128)S(1)}, f32[16,8,128]{2,1,0:T(8,128)S(1)}) custom-call(f32[32,2,128]{2,1,0:T(2,128)S(1)} %all_to_all.16.received_ref, f32[2,16,128]{2,1,0:T(8,128)S(1)} %get-tuple-element.15.small_ref, f32[5,4,16,256]{3,2,1,0:T(8,128)S(1)} %get-tuple-element.16.kept_ref, f32[8,4,32,384]{3,2,1,0:T(8,128)S(1)} %get-tuple-element.17.basis_ref), custom_call_target="tpu_custom_call" | custom-call | tf_op jit(solution)/shard_map/pallas_call | solution.py:465
  46.4 9.2 %all_to_all.17.peaks_ref = f32[16,8,128]{2,1,0:T(8,128)S(1)} all-to-all(f32[16,8,128]{2,1,0:T(8,128)S(1)} %get-tuple-element.19), channel_id=1, replica_groups=mesh['sub'=4,'gx'=4,'gy'=2] {'sub','gx'}, dimensions={0} | all-to-all | bytes 131072 | tf_op jit(solution)/shard_map/all_to_all | solution.py:474
  55.6 0.0 copy-done.2
  55.6 3.7 %shard_map.55 = (f32[4,16,256]{2,1,0:T(8,128)}, f32[4,256]{1,0:T(4,128)}) custom-call(f32[4]{0:T(128)S(1)} %copy-done.2, f32[3,16,128]{2,1,0:T(8,128)S(1)} %get-tuple-element.18.small_ref, f32[4,16,256]{2,1,0:T(8,128)S(1)} %copy-done, f32[5,4,16,256]{3,2,1,0:T(8,128)S(1)} %get-tuple-element.16.kept_ref, f32[8,4,32,384]{3,2,1,0:T(8,128)S(1)} %get-tuple-element.17.basis_ref, ...), custom_call_target="tpu_custom_call" | custom-call | tf_op jit(solution)/shard_map/pallas_call | solution.py:465
  (1 shorter events, 0.0 us)
Async XLA Ops:
  0.6 0.8 %copy-start = (f32[4,16,256]{2,1,0:T(8,128)S(1)}, f32[4,16,256]{2,1,0:T(8,128)}, u32[]{:S(2)}) copy-start(f32[4,16,256]{2,1,0:T(8,128)} %state_ref.7) | copy-start | bytes 196612
  1.5 0.8 %copy-start.1 = (f32[4,16,256]{2,1,0:T(8,128)S(1)}, f32[4,16,256]{2,1,0:T(8,128)}, u32[]{:S(2)}) copy-start(f32[4,16,256]{2,1,0:T(8,128)} %damping_ref.5) | copy-start | bytes 196612
  2.5 4.7 %collective-permute-start = (f32[16,128]{1,0:T(8,128)S(1)}, f32[16,128]{1,0:T(8,128)S(1)}, u32[]{:S(2)}, u32[]{:S(2)}) collective-permute-start(f32[16,128]{1,0:T(8,128)S(1)} %shard_map.50), channel_id=1, source_target_pairs={{0,1},{1,0},{2,3},{3,2},{4,5},{5,4},{6,7},{7,6},{8,9},{9,8},{10,11... | collective-permute-start | bytes 24584 | tf_op jit(solution)/shard_map/ppermute | solution.py:482
  7.2 7.3 %collective-permute-start.2 = (f32[272,128]{1,0:T(8,128)S(1)}, f32[272,128]{1,0:T(8,128)S(1)}, u32[]{:S(2)}, u32[]{:S(2)}) collective-permute-start(f32[272,128]{1,0:T(8,128)S(1)} %shard_map.51), channel_id=1, source_target_pairs={{2,0},{4,2},{6,4},{8,6},{10,8},{12,10},{14,12},{16,14},{18,16},{20... | collective-permute-start | bytes 417800 | tf_op jit(solution)/shard_map/ppermute | solution.py:498
  10.5 7.6 %collective-permute-start.1 = (f32[272,128]{1,0:T(8,128)S(1)}, f32[272,128]{1,0:T(8,128)S(1)}, u32[]{:S(2)}, u32[]{:S(2)}) collective-permute-start(f32[272,128]{1,0:T(8,128)S(1)} %shard_map.51), channel_id=1, source_target_pairs={{0,2},{2,4},{4,6},{6,8},{8,10},{10,12},{12,14},{14,16},{16,18},{18... | collective-permute-start | bytes 417800 | tf_op jit(solution)/shard_map/ppermute | solution.py:497
  29.7 25.9 %copy-start.2 = (f32[4]{0:T(128)S(1)}, f32[4]{0:T(128)}, u32[]{:S(2)}) copy-start(f32[4]{0:T(128)} %weights_ref.1) | copy-start | bytes 52

commit v4 on v3

--- a/solution.py
+++ b/solution.py
@@ -10,7 +10,7 @@
 
 KRYLOV = 12
 SUBSTEPS = 4
-BLOCKS = (5, 7)
+BLOCKS = (6, 6)
 HALO = 16
 LANES = 128
 SLOTS = 16
@@ -133,7 +133,16 @@
         send_ref[d, 1:2] = low[0:1]
 
 
-def edge_kernel(state_ref, damping_ref, *edge_refs):
+def edge_kernel(far_state_ref, far_damping_ref, state_ref, damping_ref, *refs):
+    edge_refs, semaphores = refs[:-1], refs[-1]
+    copies = [
+        pltpu.make_async_copy(far_state_ref, state_ref, semaphores.at[0]),
+        pltpu.make_async_copy(far_damping_ref, damping_ref, semaphores.at[1]),
+    ]
+    for copy in copies:
+        copy.start()
+    for copy in copies:
+        copy.wait()
     width = state_ref.shape[2]
     lane = iota((state_ref.shape[1], LANES), 1)
 
@@ -213,9 +222,11 @@
     drag = [drag_ref[f] + SHIFT / RADIUS for f in range(4)]
     steps = BLOCKS[0]
     for step in range(steps):
-        current = [basis_ref[step, f] for f in range(4)]
-        for f, value in enumerate(power_step(current, drag, half)):
-            basis_ref[step + 1, f] = value
+        skip = (HALO - (KRYLOV - step)) // 8 * 8 if step else 0
+        lines = slice(skip, rows - skip)
+        current = [basis_ref[step, f, lines] for f in range(4)]
+        for f, value in enumerate(power_step(current, [d[lines] for d in drag], half[lines])):
+            basis_ref[step + 1, f, lines] = value
 
     def interior(j):
         return lambda: [basis_ref[j, f, HALO : rows - HALO, :width] for f in range(4)]
@@ -239,18 +250,18 @@
     return jnp.sum(x, axis=1, keepdims=True)
 
 
-def gram_matrix(received_ref, first):
+def gram_matrix(received_ref, first, count):
     devices = received_ref.shape[0]
-    parts = [(received_ref[d : d + 8, 0, :], received_ref[d : d + 8, 1, :]) for d in range(0, devices, 8)]
-    packed = jnp.concatenate([jnp.concatenate([part, part], axis=0) for part in tree_sum(parts)], axis=0)
-    row, lane = iota((2 * SLOTS, LANES), 0) % SLOTS, iota((2 * SLOTS, LANES), 1)
-    tall_row, tall_lane = iota((LANES, LANES), 0), iota((LANES, LANES), 1)
-    by_row = jnp.where(lane % SLOTS == row, packed, 0.0)
-    right = dot(by_row, jnp.where(tall_row // SLOTS == tall_lane - first, 1.0, 0.0))
-    by_column = jnp.where(lane // SLOTS == row - first, packed, 0.0)
-    below = dot(by_column, jnp.where((tall_row % SLOTS == tall_lane) & (tall_lane < SLOTS), 1.0, 0.0))
-    both = jnp.where(lane >= first, right, jnp.where(row >= first, below, 0.0))
-    return both[:SLOTS] + old_unit(first), both[SLOTS:]
+    row, lane = iota(TILE, 0), iota(TILE, 1)
+    parts = []
+    for packed in tree_sum([(received_ref[d : d + 8, 0, :], received_ref[d : d + 8, 1, :]) for d in range(0, devices, 8)]):
+        packed = jnp.concatenate([packed, packed], axis=0)
+        below = jnp.zeros(TILE, jnp.float32)
+        for j in range(count + 1):
+            line = pltpu.roll(packed, LANES - j * SLOTS, 1) if j else packed
+            below = jnp.where((row == first + j) & (lane < SLOTS), line, below)
+        parts.append(jnp.where(row >= first, below, jnp.where(lane >= first, flip(below), 0.0)))
+    return parts[0] + old_unit(first), parts[1]
 
 
 def old_unit(first):
@@ -258,26 +269,41 @@
     return jnp.where((row == lane) & (row < first), 1.0, 0.0)
 
 
+def flip(x):
+    return jnp.transpose(tall(x))[:SLOTS]
+
+
+def small_dot(a, b):
+    terms = [a[:, k : k + 1] * b[k : k + 1] for k in range(KRYLOV + 1)]
+    while len(terms) > 1:
+        terms = [terms[k] + terms[k + 1] for k in range(0, len(terms) - 1, 2)] + terms[len(terms) // 2 * 2 :]
+    return terms[0]
+
+
 def gram_schmidt(gram, steps, start, hess, first, count):
     row, lane = iota(TILE, 0), iota(TILE, 1)
     unit = jnp.where(row == lane, 1.0, 0.0)
+    turned = flip(steps)
+    pull = small_dot(gram, turned)
     scale = jnp.where(row == first, start, jnp.where(row < first, 1.0, 0.0))
     coefs = unit * scale
-    images = gram * scale
-    column = jnp.where(row[:, 0:1] == first, start, 0.0)
+    tests = pull * scale
+    products = across_sum(tests * jnp.where(lane[0:1] == first, start, 0.0))
+    z = down_sum(steps * jnp.where(row[:, 0:1] == first, start, 0.0)) - down_sum(coefs * products)
     for c in range(first, first + count):
-        z = down_sum(steps * column)
-        products = across_sum(images * z)
-        z = z - down_sum(coefs * products)
-        column = across_sum(unit * z)
-        image = across_sum(gram * z)
-        length = jnp.sqrt(jnp.maximum(down_sum(column * image), 0.0) + norm_eps)
-        inverse = 1.0 / length
-        hess_row = down_sum(unit * products) + jnp.where(lane[0:1] == c + 1, length, 0.0)
+        column, image = across_sum(unit * z), across_sum(gram * z)
+        square = jnp.maximum(down_sum(column * image), 0.0) + norm_eps
+        inverse = lax.rsqrt(square)
+        inverse = inverse * (1.5 - 0.5 * square * inverse * inverse)
+        hess_row = down_sum(unit * products) + jnp.where(lane[0:1] == c + 1, square * inverse, 0.0)
         hess = jnp.where(row == c, hess_row, hess)
         coefs = jnp.where(row == c + 1, z * inverse, coefs)
-        images = jnp.where(row == c + 1, down_sum(gram * column) * inverse, images)
-        column = column * inverse
+        if c + 1 < first + count:
+            moved, older = across_sum(turned * z), across_sum(tests * z)
+            own = down_sum(image * moved) * inverse * inverse
+            products = older * inverse + jnp.where(row[:, 0:1] == c + 1, own, 0.0)
+            tests = jnp.where(row == c + 1, down_sum(pull * column) * inverse, tests)
+            z = down_sum(steps * column) * inverse - down_sum(coefs * products)
     return coefs, hess
 
 
@@ -292,7 +318,7 @@
         column = coefs[:, line]
         image = add_product(image, column, gram[line], [part[line] for part in gram_parts])
         image = image[0], image[1] + column * gram_low[line]
-    turned = dot(jnp.where(row == lane, 1.0, 0.0), jnp.transpose(tall(coefs)))
+    turned = flip(coefs)
     turned_parts = split(turned)
     result = (zero, zero)
     for i in slots:
@@ -312,7 +338,7 @@
 
 
 def orthogonalize(received_ref, hess, first, count):
-    gram, gram_low = gram_matrix(received_ref, first)
+    gram, gram_low = gram_matrix(received_ref, first, count)
     row, lane = iota(TILE, 0), iota(TILE, 1)
     shift, back = basis_terms(hess, first)
     fresh = (row >= first) & (row < first + count)
@@ -322,9 +348,11 @@
     one = jnp.ones((1, 1), jnp.float32)
     beta = jnp.sqrt(gram[0:1, 0:1] + norm_eps)
     coefs, image = gram_schmidt(gram, steps, one if first else 1.0 / beta, hess, first, count)
+    if first:
+        return coefs, image, beta
     gram = refined_gram(coefs, gram, gram_low, first, count)
     again, hess = gram_schmidt(gram, image, one, hess, first, count)
-    return dot(again, tall(coefs)), hess, beta
+    return small_dot(again, coefs), hess, beta
 
 
 def combine(coefs, c, parts):
@@ -379,21 +407,17 @@
 
 
 def last_kernel(received_ref, small_ref, kept_ref, basis_ref, small_out_ref, peak_ref):
-    body = kept_ref.shape[3]
     coefs, hess, _ = orthogonalize(received_ref, small_ref[0], *BLOCKS)
     small_out_ref[0] = hess
     small_out_ref[1] = small_ref[1]
     small_out_ref[2] = coefs
-    tiles = body // LANES
     for f in range(4):
         peak = jnp.max(jnp.abs(combine(coefs, KRYLOV, block_parts(kept_ref, basis_ref, f))), axis=0, keepdims=True)
         for d in range(peak_ref.shape[0]):
-            for t in range(tiles):
-                peak_ref[d, f * tiles + t : f * tiles + t + 1, :] = peak[:, t * LANES : (t + 1) * LANES]
-
-
-def finish_kernel(weights_ref, small_ref, state_ref, kept_ref, basis_ref, peaks_ref, combined_ref, error_ref):
-    body = kept_ref.shape[3]
+            peak_ref[d, f : f + 1] = peak
+
+
+def exp_kernel(weights_ref, small_ref, state_ref, kept_ref, basis_ref, combined_ref, highest_ref):
     hess, beta, coefs = small_ref[0], small_ref[1, 0:1, 0:1], small_ref[2]
     size = SUBSTEPS * SLOTS
     row, lane = iota((size, LANES), 0), iota((size, LANES), 1)
@@ -443,11 +467,11 @@
     share = dot(mixing, tall(coefs))
     for f in range(4):
         combined_ref[f] = state_ref[f] + combine(share, 0, block_parts(kept_ref, basis_ref, f))
-    peak = jnp.max(peaks_ref[...], axis=0) * highest
-    tiles = body // LANES
-    for f in range(4):
-        for t in range(tiles):
-            error_ref[f : f + 1, t * LANES : (t + 1) * LANES] = peak[f * tiles + t : f * tiles + t + 1]
+    highest_ref[...] = jnp.broadcast_to(highest, highest_ref.shape)
+
+
+def finish_kernel(highest_ref, peaks_ref, error_ref):
+    error_ref[...] = jnp.max(peaks_ref[...], axis=0) * highest_ref[0:1, 0:1]
 
 
 def shards(state, damping, weights):
@@ -459,9 +483,10 @@
     f32 = lambda *shape: jax.ShapeDtypeStruct(shape, jnp.float32)
     near = lambda *shape: pltpu.VMEM(shape, jnp.float32)
 
-    def call(kernel, outs, *args, smem=(), scratch=()):
-        specs = [pl.BlockSpec(memory_space=pltpu.SMEM) if k in smem else VMEM for k in range(len(args))]
-        args = [a if k in smem else pltpu.with_memory_space_constraint(a, pltpu.VMEM) for k, a in enumerate(args)]
+    def call(kernel, outs, *args, smem=(), far=(), scratch=()):
+        space = lambda k: pltpu.SMEM if k in smem else pltpu.HBM if k in far else pltpu.VMEM
+        specs = [pl.BlockSpec(memory_space=space(k)) for k in range(len(args))]
+        args = [a if k in smem else pltpu.with_memory_space_constraint(a, space(k)) for k, a in enumerate(args)]
         return pl.pallas_call(
             kernel,
             out_shape=outs,
@@ -477,7 +502,15 @@
     short = height + HALO
     first, count = BLOCKS
 
-    edges = call(edge_kernel, [near(height, LANES)] * (1 if sides == 2 else 2), state, damping)
+    whole = near(fields, height, width)
+    state, damping, *edges = call(
+        edge_kernel,
+        [whole, whole] + [near(height, LANES)] * (1 if sides == 2 else 2),
+        state,
+        damping,
+        far=(0, 1),
+        scratch=[pltpu.SemaphoreType.DMA((2,))],
+    )
     if sides == 2:
         halos = [lax.ppermute(edges[0], "gy", [(0, 1), (1, 0)])]
     else:
@@ -517,23 +550,23 @@
     )
     small, peaks = call(
         last_kernel,
-        [near(3, *TILE), near(lines, fields * (width // LANES), LANES)],
+        [near(3, *TILE), near(lines, fields, width)],
         exchange(send, ALL),
         small,
         kept,
         basis,
     )
-    combined, column_error = call(
-        finish_kernel,
-        [f32(fields, height, width), f32(fields, width)],
+    combined, highest = call(
+        exp_kernel,
+        [f32(fields, height, width), near(8, LANES)],
         weights,
         small,
         state,
         kept,
         basis,
-        exchange(peaks, ROWS),
         smem=(0,),
     )
+    (column_error,) = call(finish_kernel, [f32(fields, width)], highest, exchange(peaks, ROWS))
     return combined, column_error
 
 

time: 59.6 us -> 54.1 us (0.908)
  blocking collectives: 28.7 us -> 19.5 us
  starting transfers between devices: 6.43 us -> 9.93 us
  waiting for transfers between devices: 9.19 us -> 12.1 us
  local copies, waits for them, and re-layouts: 1.68 us -> 0.01 us
  Pallas kernels: 12.7 us -> 11.6 us
    all_to_all x3 -> x2, blocking collectives: 28.7 us -> 19.5 us  [shards(): exchange = lambda x, axes: lax.all_to_all(x, axes, 0, 0)]
    all_to_all x0 -> x1, starting transfers between devices: none -> 3.49 us  [shards(): exchange = lambda x, axes: lax.all_to_all(x, axes, 0, 0)]
    all_to_all x0 -> x1, waiting for transfers between devices: none -> 2.91 us  [shards(): exchange = lambda x, axes: lax.all_to_all(x, axes, 0, 0)]
    unnamed x6 -> x2, local copies, waits for them, and re-layouts: 1.68 us -> 0.01 us
    pallas_call x6 -> x7, Pallas kernels: 12.7 us -> 11.6 us  [call(): pl.pallas_call(kernel, out_shape=outs, in_specs=specs, out_specs=[VMEM] *...]
  transfers between devices with their start and end apart: 3 -> 4, of which waited for: 3 -> 4; matrix products, arithmetic and copies ran while one was open for 0% -> 0% of each run, Pallas kernels for 0% -> 7%
where the time goes in v4:
time: 54.1 us; the launch traced here: 53.8 us
  blocking collectives  19.5 us (36%)
  waiting for transfers between devices  12.1 us (22%)
  Pallas kernels  11.6 us (21%)
  starting transfers between devices  9.93 us (18%)
  between operations  0.68 us (1%)
    all_to_all x2, blocking collectives, shards(): exchange = lambda x, axes: lax.all_to_all(x, axes, 0, 0)  19.5 us
    pallas_call x7, Pallas kernels, call(): pl.pallas_call(kernel, out_shape=outs, in_specs=specs, out_specs=[VMEM] *...  11.6 us
    ppermute x1, waiting for transfers between devices, shards(): lax.ppermute(packs[-1], ROWS, [((i + 1) % lines, i) for i in range(lines)])  3.9 us
    ppermute x1, waiting for transfers between devices, shards(): lax.ppermute(packs[0], ROWS, [(i, (i + 1) % lines) for i in range(lines)])  3.66 us
    all_to_all x1, starting transfers between devices, shards(): exchange = lambda x, axes: lax.all_to_all(x, axes, 0, 0)  3.49 us
    ppermute x1, starting transfers between devices, shards(): lax.ppermute(packs[-1], ROWS, [((i + 1) % lines, i) for i in range(lines)])  3.38 us
    ppermute x1, starting transfers between devices, shards(): halos = [lax.ppermute(edges[0], 'gy', [(0, 1), (1, 0)])]  3.06 us
    all_to_all x1, waiting for transfers between devices, shards(): exchange = lambda x, axes: lax.all_to_all(x, axes, 0, 0)  2.91 us
  transfers between devices with their start and end apart: 4, of which 4 were waited for; matrix products, arithmetic and copies ran while one was open for 0% of the time, Pallas kernels for 7%

profile of v4, /device:TPU:0, one launch (start us, length us, event | category | flops | bytes accessed | tf_op | source)
XLA Modules:
  0.0 53.8 jit_solution(8929167611866050451)
XLA Ops:
  0.6 1.0 %shard_map.50 = (f32[4,16,256]{2,1,0:T(8,128)S(1)}, f32[4,16,256]{2,1,0:T(8,128)S(1)}, f32[16,128]{1,0:T(8,128)S(1)}) custom-call(f32[4,16,256]{2,1,0:T(8,128)} %far_state_ref.1, f32[4,16,256]{2,1,0:T(8,128)} %far_damping_ref.1), custom_call_target="tpu_custom_call" | custom-call | tf_op jit(solution)/shard_map/pallas_call | solution.py:490
  1.7 3.1 %collective-permute-start = (f32[16,128]{1,0:T(8,128)S(1)}, f32[16,128]{1,0:T(8,128)S(1)}, u32[]{:S(2)}, u32[]{:S(2)}) collective-permute-start(f32[16,128]{1,0:T(8,128)S(1)} %get-tuple-element.18), channel_id=1, source_target_pairs={{0,1},{1,0},{2,3},{3,2},{4,5},{5,4},{6,7},{7,6},{8,9},{9,8},{10,11... | collective-permute-start | bytes 24584 | tf_op jit(solution)/shard_map/ppermute | solution.py:515
  4.7 1.6 %collective-permute-done.refs_0_ = f32[16,128]{1,0:T(8,128)S(1)} collective-permute-done((f32[16,128]{1,0:T(8,128)S(1)}, f32[16,128]{1,0:T(8,128)S(1)}, u32[]{:S(2)}, u32[]{:S(2)}) %collective-permute-start) | collective-permute-done | bytes 8224 | tf_op jit(solution)/shard_map/ppermute | solution.py:515
  6.4 3.4 %collective-permute-start.2 = (f32[272,128]{1,0:T(8,128)S(1)}, f32[272,128]{1,0:T(8,128)S(1)}, u32[]{:S(2)}, u32[]{:S(2)}) collective-permute-start(f32[272,128]{1,0:T(8,128)S(1)} %shard_map.51), channel_id=1, source_target_pairs={{2,0},{4,2},{6,4},{8,6},{10,8},{12,10},{14,12},{16,14},{18,16},{20... | collective-permute-start | bytes 417800 | tf_op jit(solution)/shard_map/ppermute | solution.py:531
  9.8 0.0 collective-permute-start.1
  9.8 3.9 %collective-permute-done.2.refs_2_ = f32[272,128]{1,0:T(8,128)S(1)} collective-permute-done((f32[272,128]{1,0:T(8,128)S(1)}, f32[272,128]{1,0:T(8,128)S(1)}, u32[]{:S(2)}, u32[]{:S(2)}) %collective-permute-start.2) | collective-permute-done | bytes 139296 | tf_op jit(solution)/shard_map/ppermute | solution.py:531
  13.7 3.7 %collective-permute-done.1.refs_1_ = f32[272,128]{1,0:T(8,128)S(1)} collective-permute-done((f32[272,128]{1,0:T(8,128)S(1)}, f32[272,128]{1,0:T(8,128)S(1)}, u32[]{:S(2)}, u32[]{:S(2)}) %collective-permute-start.1) | collective-permute-done | bytes 139296 | tf_op jit(solution)/shard_map/ppermute | solution.py:530
  17.3 1.1 %shard_map.52 = (f32[7,4,48,384]{3,2,1,0:T(8,128)S(1)}, f32[4,48,384]{2,1,0:T(8,128)S(1)}, f32[32,2,128]{2,1,0:T(2,128)S(1)}) custom-call(f32[4,16,256]{2,1,0:T(8,128)S(1)} %get-tuple-element.16.state_ref, f32[4,16,256]{2,1,0:T(8,128)S(1)} %get-tuple-element.17.damping_ref, f32[16,128]{1,0:T(8,128)S(1)} %collective-permute-done.refs_0_, ...), custom_call_target="tpu_custom_call" | custom-call | tf_op jit(solution)/shard_map/pallas_call | solution.py:490
  18.4 10.6 %all_to_all.15.received_ref = f32[32,2,128]{2,1,0:T(2,128)S(1)} all-to-all(f32[32,2,128]{2,1,0:T(2,128)S(1)} %get-tuple-element.19), channel_id=1, replica_groups=mesh['sub'=4,'gx'=4,'gy'=2] {'sub','gx','gy'}, dimensions={0} | all-to-all | bytes 65536 | tf_op jit(solution)/shard_map/all_to_all | solution.py:499
  29.0 0.0 copy-start
  29.0 3.3 %shard_map.53 = (f32[7,4,32,384]{3,2,1,0:T(8,128)S(1)}, f32[6,4,16,256]{3,2,1,0:T(8,128)S(1)}, f32[2,16,128]{2,1,0:T(8,128)S(1)}, f32[32,2,128]{2,1,0:T(2,128)S(1)}) custom-call(f32[32,2,128]{2,1,0:T(2,128)S(1)} %all_to_all.15.received_ref, f32[4,48,384]{2,1,0:T(8,128)S(1)} %get-tuple-element.20.drag_in_ref, f32[7,4,48,384]{3,2,1,0:T(8,128)S(1)} %get-tuple-element.21.basis_in_ref), custom_call_target="tpu_custom_call" | custom-call | tf_op jit(solution)/shard_map/pallas_call | solution.py:490
  32.4 8.9 %all_to_all.16.received_ref = f32[32,2,128]{2,1,0:T(2,128)S(1)} all-to-all(f32[32,2,128]{2,1,0:T(2,128)S(1)} %get-tuple-element.22), channel_id=1, replica_groups=mesh['sub'=4,'gx'=4,'gy'=2] {'sub','gx','gy'}, dimensions={0} | all-to-all | bytes 65536 | tf_op jit(solution)/shard_map/all_to_all | solution.py:499
  41.2 1.8 %shard_map.54 = (f32[3,16,128]{2,1,0:T(8,128)S(1)}, f32[16,4,256]{2,1,0:T(4,128)}) custom-call(f32[32,2,128]{2,1,0:T(2,128)S(1)} %all_to_all.16.received_ref, f32[2,16,128]{2,1,0:T(8,128)S(1)} %get-tuple-element.23.small_ref, f32[6,4,16,256]{3,2,1,0:T(8,128)S(1)} %get-tuple-element.24.kept_ref, f32[7,4,32,384]{3,2,1,0:T(8,128)S(1)} %get-tuple-element.25.basis_ref), custom_call_target="tpu_custom_call" | custom-call | tf_op jit(solution)/shard_map/pallas_call | solution.py:490
  43.1 3.5 %all-to-all-start.2 = ((f32[16,4,256]{2,1,0:T(4,128)}), f32[16,4,256]{2,1,0:T(4,128)S(1)}, u32[]{:S(2)}, u32[]{:S(2)}) async-start(f32[16,4,256]{2,1,0:T(4,128)} %get-tuple-element.29), calls=%async_computation.2 | async-start | bytes 131072 | tf_op jit(solution)/shard_map/all_to_all | solution.py:499
  46.6 0.0 copy-done
  46.6 3.7 %shard_map.55 = (f32[4,16,256]{2,1,0:T(8,128)}, f32[8,128]{1,0:T(8,128)S(1)}) custom-call(f32[4]{0:T(128)S(1)} %copy-done, f32[3,16,128]{2,1,0:T(8,128)S(1)} %get-tuple-element.26.small_ref, f32[4,16,256]{2,1,0:T(8,128)S(1)} %get-tuple-element.16.state_ref, f32[6,4,16,256]{3,2,1,0:T(8,128)S(1)} %get-tuple-element.24.kept_ref, ...), custom_call_target="tpu_custom_call" | custom-call | tf_op jit(solution)/shard_map/pallas_call | solution.py:490
  50.3 2.9 %all-to-all-done.2.peaks_ref = f32[16,4,256]{2,1,0:T(4,128)S(1)} async-done(((f32[16,4,256]{2,1,0:T(4,128)}), f32[16,4,256]{2,1,0:T(4,128)S(1)}, u32[]{:S(2)}, u32[]{:S(2)}) %all-to-all-start.2) | async-done | bytes 65568 | tf_op jit(solution)/shard_map/all_to_all | solution.py:499
  53.2 0.6 %shard_map.56 = f32[4,256]{1,0:T(4,128)} custom-call(f32[8,128]{1,0:T(8,128)S(1)} %get-tuple-element.28.highest_ref, f32[16,4,256]{2,1,0:T(4,128)S(1)} %all-to-all-done.2.peaks_ref), custom_call_target="tpu_custom_call" | custom-call | tf_op jit(solution)/shard_map/pallas_call | solution.py:490
  (1 shorter events, 0.0 us)
Async XLA Ops:
  1.7 4.7 %collective-permute-start = (f32[16,128]{1,0:T(8,128)S(1)}, f32[16,128]{1,0:T(8,128)S(1)}, u32[]{:S(2)}, u32[]{:S(2)}) collective-permute-start(f32[16,128]{1,0:T(8,128)S(1)} %get-tuple-element.18), channel_id=1, source_target_pairs={{0,1},{1,0},{2,3},{3,2},{4,5},{5,4},{6,7},{7,6},{8,9},{9,8},{10,11... | collective-permute-start | bytes 24584 | tf_op jit(solution)/shard_map/ppermute | solution.py:515
  6.4 7.3 %collective-permute-start.2 = (f32[272,128]{1,0:T(8,128)S(1)}, f32[272,128]{1,0:T(8,128)S(1)}, u32[]{:S(2)}, u32[]{:S(2)}) collective-permute-start(f32[272,128]{1,0:T(8,128)S(1)} %shard_map.51), channel_id=1, source_target_pairs={{2,0},{4,2},{6,4},{8,6},{10,8},{12,10},{14,12},{16,14},{18,16},{20... | collective-permute-start | bytes 417800 | tf_op jit(solution)/shard_map/ppermute | solution.py:531
  9.8 7.6 %collective-permute-start.1 = (f32[272,128]{1,0:T(8,128)S(1)}, f32[272,128]{1,0:T(8,128)S(1)}, u32[]{:S(2)}, u32[]{:S(2)}) collective-permute-start(f32[272,128]{1,0:T(8,128)S(1)} %shard_map.51), channel_id=1, source_target_pairs={{0,2},{2,4},{4,6},{6,8},{8,10},{10,12},{12,14},{14,16},{16,18},{18... | collective-permute-start | bytes 417800 | tf_op jit(solution)/shard_map/ppermute | solution.py:530
  29.0 17.6 %copy-start = (f32[4]{0:T(128)S(1)}, f32[4]{0:T(128)}, u32[]{:S(2)}) copy-start(f32[4]{0:T(128)} %weights_ref.1) | copy-start | bytes 52
  43.1 10.1 %all-to-all-start.2 = ((f32[16,4,256]{2,1,0:T(4,128)}), f32[16,4,256]{2,1,0:T(4,128)S(1)}, u32[]{:S(2)}, u32[]{:S(2)}) async-start(f32[16,4,256]{2,1,0:T(4,128)} %get-tuple-element.29), calls=%async_computation.2 | async-start | bytes 131072 | tf_op jit(solution)/shard_map/all_to_all | solution.py:499

commit v5 on v4

--- a/solution.py
+++ b/solution.py
@@ -238,6 +238,10 @@
 TILE = (SLOTS, LANES)
 
 
+def block_tile(first, count):
+    return (-(-(first + count + 1) // 8) * 8, LANES)
+
+
 def tall(x):
     return jnp.concatenate([x, jnp.zeros((LANES - x.shape[0], LANES), jnp.float32)], axis=0)
 
@@ -252,114 +256,162 @@
 
 def gram_matrix(received_ref, first, count):
     devices = received_ref.shape[0]
-    row, lane = iota(TILE, 0), iota(TILE, 1)
+    tile = block_tile(first, count)
+    row, lane = iota(tile, 0), iota(tile, 1)
     parts = []
     for packed in tree_sum([(received_ref[d : d + 8, 0, :], received_ref[d : d + 8, 1, :]) for d in range(0, devices, 8)]):
-        packed = jnp.concatenate([packed, packed], axis=0)
-        below = jnp.zeros(TILE, jnp.float32)
+        packed = jnp.concatenate([packed] * (tile[0] // 8), axis=0)
+        below = jnp.zeros(tile, jnp.float32)
         for j in range(count + 1):
             line = pltpu.roll(packed, LANES - j * SLOTS, 1) if j else packed
             below = jnp.where((row == first + j) & (lane < SLOTS), line, below)
         parts.append(jnp.where(row >= first, below, jnp.where(lane >= first, flip(below), 0.0)))
-    return parts[0] + old_unit(first), parts[1]
-
-
-def old_unit(first):
-    row, lane = iota(TILE, 0), iota(TILE, 1)
+    return parts[0] + old_unit(first, tile), parts[1]
+
+
+def old_unit(first, tile):
+    row, lane = iota(tile, 0), iota(tile, 1)
     return jnp.where((row == lane) & (row < first), 1.0, 0.0)
 
 
 def flip(x):
-    return jnp.transpose(tall(x))[:SLOTS]
-
-
-def small_dot(a, b):
-    terms = [a[:, k : k + 1] * b[k : k + 1] for k in range(KRYLOV + 1)]
+    return jnp.transpose(tall(x))[: x.shape[0]]
+
+
+def added(terms):
     while len(terms) > 1:
         terms = [terms[k] + terms[k + 1] for k in range(0, len(terms) - 1, 2)] + terms[len(terms) // 2 * 2 :]
     return terms[0]
 
 
-def gram_schmidt(gram, steps, start, hess, first, count):
-    row, lane = iota(TILE, 0), iota(TILE, 1)
-    unit = jnp.where(row == lane, 1.0, 0.0)
-    turned = flip(steps)
-    pull = small_dot(gram, turned)
-    scale = jnp.where(row == first, start, jnp.where(row < first, 1.0, 0.0))
-    coefs = unit * scale
-    tests = pull * scale
-    products = across_sum(tests * jnp.where(lane[0:1] == first, start, 0.0))
-    z = down_sum(steps * jnp.where(row[:, 0:1] == first, start, 0.0)) - down_sum(coefs * products)
+def columns_of(matrix, count):
+    return [jnp.broadcast_to(matrix[:, a : a + 1], matrix.shape) for a in range(count)]
+
+
+def weighted(columns, x):
+    return added([x[a : a + 1] * column for a, column in enumerate(columns)])
+
+
+def gram_matrix(received_ref, first, count):
+    devices = received_ref.shape[0]
+    tile = block_tile(first, count)
+    row, lane = iota(tile, 0), iota(tile, 1)
+    parts = []
+    for packed in tree_sum([(received_ref[d : d + 8, 0, :], received_ref[d : d + 8, 1, :]) for d in range(0, devices, 8)]):
+        packed = jnp.concatenate([packed] * (tile[0] // 8), axis=0)
+        below = jnp.zeros(tile, jnp.float32)
+        for j in range(count + 1):
+            line = pltpu.roll(packed, LANES - j * SLOTS, 1) if j else packed
+            below = jnp.where((row == first + j) & (lane < SLOTS), line, below)
+        parts.append(jnp.where(row >= first, below, jnp.where(lane >= first, flip(below), 0.0)))
+    return parts[0] + old_unit(first, tile), parts[1]
+
+
+def old_unit(first, tile):
+    row, lane = iota(tile, 0), iota(tile, 1)
+    return jnp.where((row == lane) & (row < first), 1.0, 0.0)
+
+
+def flip(x):
+    return jnp.transpose(tall(x))[: x.shape[0]]
+
+
+def small_dot(a, b):
+    terms = [a[:, k : k + 1] * b[k : k + 1] for k in range(min(KRYLOV + 1, b.shape[0]))]
+    while len(terms) > 1:
+        terms = [terms[k] + terms[k + 1] for k in range(0, len(terms) - 1, 2)] + terms[len(terms) // 2 * 2 :]
+    return terms[0]
+
+
+def gram_schmidt(gram, image_of, start, first, count):
+    row = iota(gram[0].shape, 0)
+    vector = jnp.where(row == first, start, 0.0)
+    raw, raw_image, inverse = vector, gram[first] * start, 1.0
+    vectors, images, hess = [vector], [], []
     for c in range(first, first + count):
-        column, image = across_sum(unit * z), across_sum(gram * z)
-        square = jnp.maximum(down_sum(column * image), 0.0) + norm_eps
+        moved = image_of(raw, c)
+        products = [down_sum(image * moved) for image in images]
+        own = down_sum(raw_image * moved) * (inverse * inverse)
+        images.append(raw_image * inverse)
+        rest = added([moved] + [-product * other for product, other in zip(products, vectors)])
+        seen = added([jnp.where(row == first + k, product, 0.0) for k, product in enumerate(products)] + [jnp.zeros_like(moved)])
+        if first:
+            older = jnp.where(row < first, weighted(gram[: c + 2], moved), 0.0)
+            rest, seen = rest - older, seen + older
+        raw = rest * inverse - own * vectors[-1]
+        column = seen * inverse + jnp.where(row == c, own, 0.0)
+        raw_image = weighted(gram[: c + 2], raw)
+        square = jnp.maximum(down_sum(raw * raw_image), 0.0) + norm_eps
         inverse = lax.rsqrt(square)
         inverse = inverse * (1.5 - 0.5 * square * inverse * inverse)
-        hess_row = down_sum(unit * products) + jnp.where(lane[0:1] == c + 1, square * inverse, 0.0)
-        hess = jnp.where(row == c, hess_row, hess)
-        coefs = jnp.where(row == c + 1, z * inverse, coefs)
-        if c + 1 < first + count:
-            moved, older = across_sum(turned * z), across_sum(tests * z)
-            own = down_sum(image * moved) * inverse * inverse
-            products = older * inverse + jnp.where(row[:, 0:1] == c + 1, own, 0.0)
-            tests = jnp.where(row == c + 1, down_sum(pull * column) * inverse, tests)
-            z = down_sum(steps * column) * inverse - down_sum(coefs * products)
-    return coefs, hess
-
-
-def refined_gram(coefs, gram, gram_low, first, count):
-    row, lane = iota(TILE, 0), iota(TILE, 1)
-    slots = range(first + count + 1)
-    gram_parts = split(gram)
-    zero = jnp.zeros(TILE, jnp.float32)
+        vectors.append(raw * inverse)
+        hess.append(column + jnp.where(row == c + 1, square * inverse, 0.0))
+    return vectors, hess
+
+
+def by_lane(columns, first, matrix):
+    lane = iota(matrix.shape, 1)
+    for k, column in enumerate(columns):
+        matrix = jnp.where(lane == first + k, column, matrix)
+    return matrix
+
+
+def refined_gram(vectors, gram, gram_low):
+    row = iota(gram[0].shape, 0)
+    zero = jnp.zeros_like(gram[0])
+    turned = by_lane(vectors, 0, zero)
+    parts = split(turned)
     image = (zero, zero)
-    for j in slots:
+    for j, (column, low) in enumerate(zip(gram, gram_low)):
         line = slice(j, j + 1)
-        column = coefs[:, line]
-        image = add_product(image, column, gram[line], [part[line] for part in gram_parts])
-        image = image[0], image[1] + column * gram_low[line]
-    turned = flip(coefs)
-    turned_parts = split(turned)
-    result = (zero, zero)
-    for i in slots:
-        line = slice(i, i + 1)
-        result = add_product(result, image[0][:, line], turned[line], [part[line] for part in turned_parts])
-        result = result[0], result[1] + image[1][:, line] * turned[line]
-    inner = (row < first) & (lane < first)
-    return jnp.where(inner, old_unit(first), result[0] + result[1])
+        image = add_product(image, column, turned[line], [part[line] for part in parts])
+        image = image[0], image[1] + low * turned[line]
+    image_parts = split(image[0])
+    result = zero
+    for c, vector in enumerate(vectors):
+        high, low = add_product((zero, zero), vector, image[0], image_parts)
+        high, low = tree_sum([(high, low + vector * image[1])])
+        result = jnp.where(row == c, high + low, result)
+    return result
 
 
 def basis_terms(hess, first):
-    if first == 0:
-        return jnp.full((1, 1), SHIFT, jnp.float32), jnp.zeros((1, 1), jnp.float32)
     c = first - 1
-    shift = 0.5 * (hess[c - 1 : c, c - 1 : c] + hess[c : c + 1, c : c + 1])
-    return shift, hess[c : c + 1, c - 1 : c]
+    shift = 0.5 * (hess[c - 1][c - 1 : c] + hess[c][c : c + 1])
+    return shift, hess[c][c - 1 : c]
 
 
 def orthogonalize(received_ref, hess, first, count):
     gram, gram_low = gram_matrix(received_ref, first, count)
-    row, lane = iota(TILE, 0), iota(TILE, 1)
-    shift, back = basis_terms(hess, first)
-    fresh = (row >= first) & (row < first + count)
-    chain = jnp.where(lane == row, shift, 0.0) + jnp.where(lane == row + 1, RADIUS, 0.0)
-    chain = chain + jnp.where((lane == row - 1) & (row > first), back, 0.0)
-    steps = hess + jnp.where(fresh, chain, 0.0)
-    one = jnp.ones((1, 1), jnp.float32)
-    beta = jnp.sqrt(gram[0:1, 0:1] + norm_eps)
-    coefs, image = gram_schmidt(gram, steps, one if first else 1.0 / beta, hess, first, count)
+    slots = first + count + 1
+    gram = columns_of(gram, slots)
+    row = iota(gram[0].shape, 0)
+
+    def basis_image(x, c):
+        fresh = jnp.where(row >= first, x, 0.0)
+        if not first:
+            return RADIUS * pltpu.roll(fresh, 1, 0) + SHIFT * fresh
+        shift, back = basis_terms(hess, first)
+        image = RADIUS * pltpu.roll(fresh, 1, 0) + shift * fresh
+        image = image + jnp.where(row >= first, back * pltpu.roll(fresh, row.shape[0] - 1, 0), 0.0)
+        return image + weighted(hess, x)
+
     if first:
-        return coefs, image, beta
-    gram = refined_gram(coefs, gram, gram_low, first, count)
-    again, hess = gram_schmidt(gram, image, one, hess, first, count)
-    return small_dot(again, coefs), hess, beta
-
-
-def combine(coefs, c, parts):
+        return *gram_schmidt(gram, basis_image, 1.0, first, count), None
+    square = gram[0][0:1] + norm_eps
+    beta = jnp.sqrt(square)
+    vectors, image = gram_schmidt(gram, basis_image, 1.0 / beta, first, count)
+    gram = columns_of(refined_gram(vectors, gram, columns_of(gram_low, slots)), slots)
+    again, hess = gram_schmidt(gram, lambda x, c: weighted(image[: c + 1], x), 1.0, first, count)
+    return [weighted(vectors[: c + 1], x) for c, x in enumerate(again)], hess, beta
+
+
+def combine(weights, parts):
     total = None
     for i, part in parts:
-        term = coefs[c : c + 1, i : i + 1] * part()
-        total = term if total is None else total + term
+        value = part()
+        scale = jnp.concatenate([weights[i : i + 1]] * (value.shape[1] // LANES), axis=1)
+        total = scale * value if total is None else total + scale * value
     return total
 
 
@@ -369,19 +421,20 @@
     edge = (basis_in_ref.shape[2] - rows) // 2
     halo = HALO - edge
     body = columns - LANES
-    coefs, hess, beta = orthogonalize(received_ref, jnp.zeros(TILE, jnp.float32), 0, first)
-    small_ref[0] = hess
+    vectors, hess, beta = orthogonalize(received_ref, [], 0, first)
+    small_ref[0] = jnp.zeros(TILE, jnp.float32)
+    small_ref[0, : hess[0].shape[0]] = by_lane(hess, 0, jnp.zeros_like(hess[0]))
     small_ref[1] = jnp.broadcast_to(beta, TILE)
     for f in range(4):
         inner = [(j, lambda j=j: basis_in_ref[j, f, HALO : edge + rows - halo, :body]) for j in range(first + 1)]
         for c in range(first):
-            kept_ref[c, f] = combine(coefs, c, inner[: c + 1])
+            kept_ref[c, f] = combine(vectors[c], inner[: c + 1])
         outer = [(j, lambda j=j: basis_in_ref[j, f, edge : edge + rows]) for j in range(first + 1)]
-        basis_ref[0, f] = combine(coefs, first, outer)
-    shift, back = basis_terms(hess, first)
-    back = back * (1.0 / RADIUS)
+        basis_ref[0, f] = combine(vectors[first], outer)
+    wide = lambda x: jnp.concatenate([x * (1.0 / RADIUS)] * (columns // LANES), axis=1)
+    shift, back = map(wide, basis_terms(hess, first))
     half = (0.5 * dt_total / RADIUS) * grid_mask(rows, columns, halo)
-    drag = [drag_in_ref[f, edge : edge + rows] + shift * (1.0 / RADIUS) for f in range(4)]
+    drag = [drag_in_ref[f, edge : edge + rows] + shift for f in range(4)]
     for step in range(count):
         current = [basis_ref[step, f] for f in range(4)]
         for f, value in enumerate(power_step(current, drag, half)):
@@ -407,18 +460,20 @@
 
 
 def last_kernel(received_ref, small_ref, kept_ref, basis_ref, small_out_ref, peak_ref):
-    coefs, hess, _ = orthogonalize(received_ref, small_ref[0], *BLOCKS)
-    small_out_ref[0] = hess
+    first, count = BLOCKS
+    old = small_ref[0]
+    vectors, hess, _ = orthogonalize(received_ref, columns_of(old, first), first, count)
+    small_out_ref[0] = by_lane(hess, first, old)
     small_out_ref[1] = small_ref[1]
-    small_out_ref[2] = coefs
+    small_out_ref[2] = by_lane(vectors, first, old_unit(first, TILE))
     for f in range(4):
-        peak = jnp.max(jnp.abs(combine(coefs, KRYLOV, block_parts(kept_ref, basis_ref, f))), axis=0, keepdims=True)
+        peak = jnp.max(jnp.abs(combine(vectors[count], block_parts(kept_ref, basis_ref, f))), axis=0, keepdims=True)
         for d in range(peak_ref.shape[0]):
             peak_ref[d, f : f + 1] = peak
 
 
 def exp_kernel(weights_ref, small_ref, state_ref, kept_ref, basis_ref, combined_ref, highest_ref):
-    hess, beta, coefs = small_ref[0], small_ref[1, 0:1, 0:1], small_ref[2]
+    hess, beta, vectors = flip(small_ref[0]), small_ref[1, 0:1, 0:1], small_ref[2]
     size = SUBSTEPS * SLOTS
     row, lane = iota((size, LANES), 0), iota((size, LANES), 1)
     row_in, lane_in = row % SLOTS, lane % SLOTS
@@ -463,10 +518,10 @@
         mixing = mixing + weights_ref[k] * factor * beta * g
         estimate = (factor * tau) * beta * hess[KRYLOV - 1 : KRYLOV, KRYLOV : KRYLOV + 1] * jnp.abs(g[:, KRYLOV - 1 : KRYLOV])
         highest = jnp.maximum(highest, estimate)
-    mixing = jnp.where(lane[0:8] < KRYLOV, jnp.broadcast_to(mixing, (8, LANES)), 0.0)
-    share = dot(mixing, tall(coefs))
+    mixing = jnp.where(lane[0:1] < KRYLOV, mixing, 0.0)
+    share = jnp.broadcast_to(across_sum(vectors * mixing), TILE)
     for f in range(4):
-        combined_ref[f] = state_ref[f] + combine(share, 0, block_parts(kept_ref, basis_ref, f))
+        combined_ref[f] = state_ref[f] + combine(share, block_parts(kept_ref, basis_ref, f))
     highest_ref[...] = jnp.broadcast_to(highest, highest_ref.shape)
 
 

time: 54.1 us -> 51.8 us (0.957)
  Pallas kernels: 11.6 us -> 9.32 us
    pallas_call x7, Pallas kernels: 11.6 us -> 9.32 us  [call(): pl.pallas_call(kernel, out_shape=outs, in_specs=specs, out_specs=[VMEM] *...]
where the time goes in v5:
time: 51.8 us; the launch traced here: 51.6 us
  blocking collectives  19.5 us (38%)
  waiting for transfers between devices  12.2 us (24%)
  starting transfers between devices  9.93 us (19%)
  Pallas kernels  9.32 us (18%)
  between operations  0.68 us (1%)
    all_to_all x2, blocking collectives, shards(): exchange = lambda x, axes: lax.all_to_all(x, axes, 0, 0)  19.5 us
    pallas_call x7, Pallas kernels, call(): pl.pallas_call(kernel, out_shape=outs, in_specs=specs, out_specs=[VMEM] *...  9.32 us
    ppermute x1, waiting for transfers between devices, shards(): lax.ppermute(packs[-1], ROWS, [((i + 1) % lines, i) for i in range(lines)])  3.9 us
    ppermute x1, waiting for transfers between devices, shards(): lax.ppermute(packs[0], ROWS, [(i, (i + 1) % lines) for i in range(lines)])  3.66 us
    all_to_all x1, starting transfers between devices, shards(): exchange = lambda x, axes: lax.all_to_all(x, axes, 0, 0)  3.49 us
    ppermute x1, starting transfers between devices, shards(): lax.ppermute(packs[-1], ROWS, [((i + 1) % lines, i) for i in range(lines)])  3.38 us
    ppermute x1, starting transfers between devices, shards(): halos = [lax.ppermute(edges[0], 'gy', [(0, 1), (1, 0)])]  3.06 us
    all_to_all x1, waiting for transfers between devices, shards(): exchange = lambda x, axes: lax.all_to_all(x, axes, 0, 0)  2.98 us
  transfers between devices with their start and end apart: 4, of which 4 were waited for; matrix products, arithmetic and copies ran while one was open for 0% of the time, Pallas kernels for 7%

profile of v5, /device:TPU:0, one launch (start us, length us, event | category | flops | bytes accessed | tf_op | source)
XLA Modules:
  0.0 51.6 jit_solution(14663100105928297649)
XLA Ops:
  0.6 1.0 %shard_map.50 = (f32[4,16,256]{2,1,0:T(8,128)S(1)}, f32[4,16,256]{2,1,0:T(8,128)S(1)}, f32[16,128]{1,0:T(8,128)S(1)}) custom-call(f32[4,16,256]{2,1,0:T(8,128)} %far_state_ref.1, f32[4,16,256]{2,1,0:T(8,128)} %far_damping_ref.1), custom_call_target="tpu_custom_call" | custom-call | tf_op jit(solution)/shard_map/pallas_call | solution.py:545
  1.7 3.1 %collective-permute-start = (f32[16,128]{1,0:T(8,128)S(1)}, f32[16,128]{1,0:T(8,128)S(1)}, u32[]{:S(2)}, u32[]{:S(2)}) collective-permute-start(f32[16,128]{1,0:T(8,128)S(1)} %get-tuple-element.18), channel_id=1, source_target_pairs={{0,1},{1,0},{2,3},{3,2},{4,5},{5,4},{6,7},{7,6},{8,9},{9,8},{10,11... | collective-permute-start | bytes 24584 | tf_op jit(solution)/shard_map/ppermute | solution.py:570
  4.7 1.6 %collective-permute-done.refs_0_ = f32[16,128]{1,0:T(8,128)S(1)} collective-permute-done((f32[16,128]{1,0:T(8,128)S(1)}, f32[16,128]{1,0:T(8,128)S(1)}, u32[]{:S(2)}, u32[]{:S(2)}) %collective-permute-start) | collective-permute-done | bytes 8224 | tf_op jit(solution)/shard_map/ppermute | solution.py:570
  6.4 3.4 %collective-permute-start.2 = (f32[272,128]{1,0:T(8,128)S(1)}, f32[272,128]{1,0:T(8,128)S(1)}, u32[]{:S(2)}, u32[]{:S(2)}) collective-permute-start(f32[272,128]{1,0:T(8,128)S(1)} %shard_map.51), channel_id=1, source_target_pairs={{2,0},{4,2},{6,4},{8,6},{10,8},{12,10},{14,12},{16,14},{18,16},{20... | collective-permute-start | bytes 417800 | tf_op jit(solution)/shard_map/ppermute | solution.py:586
  9.8 0.0 collective-permute-start.1
  9.8 3.9 %collective-permute-done.2.refs_2_ = f32[272,128]{1,0:T(8,128)S(1)} collective-permute-done((f32[272,128]{1,0:T(8,128)S(1)}, f32[272,128]{1,0:T(8,128)S(1)}, u32[]{:S(2)}, u32[]{:S(2)}) %collective-permute-start.2) | collective-permute-done | bytes 139296 | tf_op jit(solution)/shard_map/ppermute | solution.py:586
  13.7 3.7 %collective-permute-done.1.refs_1_ = f32[272,128]{1,0:T(8,128)S(1)} collective-permute-done((f32[272,128]{1,0:T(8,128)S(1)}, f32[272,128]{1,0:T(8,128)S(1)}, u32[]{:S(2)}, u32[]{:S(2)}) %collective-permute-start.1) | collective-permute-done | bytes 139296 | tf_op jit(solution)/shard_map/ppermute | solution.py:585
  17.3 1.1 %shard_map.52 = (f32[7,4,48,384]{3,2,1,0:T(8,128)S(1)}, f32[4,48,384]{2,1,0:T(8,128)S(1)}, f32[32,2,128]{2,1,0:T(2,128)S(1)}) custom-call(f32[4,16,256]{2,1,0:T(8,128)S(1)} %get-tuple-element.16.state_ref, f32[4,16,256]{2,1,0:T(8,128)S(1)} %get-tuple-element.17.damping_ref, f32[16,128]{1,0:T(8,128)S(1)} %collective-permute-done.refs_0_, ...), custom_call_target="tpu_custom_call" | custom-call | tf_op jit(solution)/shard_map/pallas_call | solution.py:545
  18.4 10.6 %all_to_all.15.received_ref = f32[32,2,128]{2,1,0:T(2,128)S(1)} all-to-all(f32[32,2,128]{2,1,0:T(2,128)S(1)} %get-tuple-element.19), channel_id=1, replica_groups=mesh['sub'=4,'gx'=4,'gy'=2] {'sub','gx','gy'}, dimensions={0} | all-to-all | bytes 65536 | tf_op jit(solution)/shard_map/all_to_all | solution.py:554
  29.0 0.0 copy-start
  29.0 1.8 %shard_map.53 = (f32[7,4,32,384]{3,2,1,0:T(8,128)S(1)}, f32[6,4,16,256]{3,2,1,0:T(8,128)S(1)}, f32[2,16,128]{2,1,0:T(8,128)S(1)}, f32[32,2,128]{2,1,0:T(2,128)S(1)}) custom-call(f32[32,2,128]{2,1,0:T(2,128)S(1)} %all_to_all.15.received_ref, f32[4,48,384]{2,1,0:T(8,128)S(1)} %get-tuple-element.20.drag_in_ref, f32[7,4,48,384]{3,2,1,0:T(8,128)S(1)} %get-tuple-element.21.basis_in_ref), custom_call_target="tpu_custom_call" | custom-call | tf_op jit(solution)/shard_map/pallas_call | solution.py:545
  30.8 8.9 %all_to_all.16.received_ref = f32[32,2,128]{2,1,0:T(2,128)S(1)} all-to-all(f32[32,2,128]{2,1,0:T(2,128)S(1)} %get-tuple-element.22), channel_id=1, replica_groups=mesh['sub'=4,'gx'=4,'gy'=2] {'sub','gx','gy'}, dimensions={0} | all-to-all | bytes 65536 | tf_op jit(solution)/shard_map/all_to_all | solution.py:554
  39.7 1.2 %shard_map.54 = (f32[3,16,128]{2,1,0:T(8,128)S(1)}, f32[16,4,256]{2,1,0:T(4,128)}) custom-call(f32[32,2,128]{2,1,0:T(2,128)S(1)} %all_to_all.16.received_ref, f32[2,16,128]{2,1,0:T(8,128)S(1)} %get-tuple-element.23.small_ref, f32[6,4,16,256]{3,2,1,0:T(8,128)S(1)} %get-tuple-element.24.kept_ref, f32[7,4,32,384]{3,2,1,0:T(8,128)S(1)} %get-tuple-element.25.basis_ref), custom_call_target="tpu_custom_call" | custom-call | tf_op jit(solution)/shard_map/pallas_call | solution.py:545
  40.9 3.5 %all-to-all-start.2 = ((f32[16,4,256]{2,1,0:T(4,128)}), f32[16,4,256]{2,1,0:T(4,128)S(1)}, u32[]{:S(2)}, u32[]{:S(2)}) async-start(f32[16,4,256]{2,1,0:T(4,128)} %get-tuple-element.29), calls=%async_computation.2 | async-start | bytes 131072 | tf_op jit(solution)/shard_map/all_to_all | solution.py:554
  44.4 0.0 copy-done
  44.4 3.6 %shard_map.55 = (f32[4,16,256]{2,1,0:T(8,128)}, f32[8,128]{1,0:T(8,128)S(1)}) custom-call(f32[4]{0:T(128)S(1)} %copy-done, f32[3,16,128]{2,1,0:T(8,128)S(1)} %get-tuple-element.26.small_ref, f32[4,16,256]{2,1,0:T(8,128)S(1)} %get-tuple-element.16.state_ref, f32[6,4,16,256]{3,2,1,0:T(8,128)S(1)} %get-tuple-element.24.kept_ref, ...), custom_call_target="tpu_custom_call" | custom-call | tf_op jit(solution)/shard_map/pallas_call | solution.py:545
  48.0 3.0 %all-to-all-done.2.peaks_ref = f32[16,4,256]{2,1,0:T(4,128)S(1)} async-done(((f32[16,4,256]{2,1,0:T(4,128)}), f32[16,4,256]{2,1,0:T(4,128)S(1)}, u32[]{:S(2)}, u32[]{:S(2)}) %all-to-all-start.2) | async-done | bytes 65568 | tf_op jit(solution)/shard_map/all_to_all | solution.py:554
  50.9 0.6 %shard_map.56 = f32[4,256]{1,0:T(4,128)} custom-call(f32[8,128]{1,0:T(8,128)S(1)} %get-tuple-element.28.highest_ref, f32[16,4,256]{2,1,0:T(4,128)S(1)} %all-to-all-done.2.peaks_ref), custom_call_target="tpu_custom_call" | custom-call | tf_op jit(solution)/shard_map/pallas_call | solution.py:545
  (1 shorter events, 0.0 us)
Async XLA Ops:
  1.7 4.7 %collective-permute-start = (f32[16,128]{1,0:T(8,128)S(1)}, f32[16,128]{1,0:T(8,128)S(1)}, u32[]{:S(2)}, u32[]{:S(2)}) collective-permute-start(f32[16,128]{1,0:T(8,128)S(1)} %get-tuple-element.18), channel_id=1, source_target_pairs={{0,1},{1,0},{2,3},{3,2},{4,5},{5,4},{6,7},{7,6},{8,9},{9,8},{10,11... | collective-permute-start | bytes 24584 | tf_op jit(solution)/shard_map/ppermute | solution.py:570
  6.4 7.3 %collective-permute-start.2 = (f32[272,128]{1,0:T(8,128)S(1)}, f32[272,128]{1,0:T(8,128)S(1)}, u32[]{:S(2)}, u32[]{:S(2)}) collective-permute-start(f32[272,128]{1,0:T(8,128)S(1)} %shard_map.51), channel_id=1, source_target_pairs={{2,0},{4,2},{6,4},{8,6},{10,8},{12,10},{14,12},{16,14},{18,16},{20... | collective-permute-start | bytes 417800 | tf_op jit(solution)/shard_map/ppermute | solution.py:586
  9.8 7.6 %collective-permute-start.1 = (f32[272,128]{1,0:T(8,128)S(1)}, f32[272,128]{1,0:T(8,128)S(1)}, u32[]{:S(2)}, u32[]{:S(2)}) collective-permute-start(f32[272,128]{1,0:T(8,128)S(1)} %shard_map.51), channel_id=1, source_target_pairs={{0,2},{2,4},{4,6},{6,8},{8,10},{10,12},{12,14},{14,16},{16,18},{18... | collective-permute-start | bytes 417800 | tf_op jit(solution)/shard_map/ppermute | solution.py:585
  29.0 15.3 %copy-start = (f32[4]{0:T(128)S(1)}, f32[4]{0:T(128)}, u32[]{:S(2)}) copy-start(f32[4]{0:T(128)} %weights_ref.1) | copy-start | bytes 52
  40.9 10.1 %all-to-all-start.2 = ((f32[16,4,256]{2,1,0:T(4,128)}), f32[16,4,256]{2,1,0:T(4,128)S(1)}, u32[]{:S(2)}, u32[]{:S(2)}) async-start(f32[16,4,256]{2,1,0:T(4,128)} %get-tuple-element.29), calls=%async_computation.2 | async-start | bytes 131072 | tf_op jit(solution)/shard_map/all_to_all | solution.py:554

commit v6 on v5

--- a/solution.py
+++ b/solution.py
@@ -10,7 +10,7 @@
 
 KRYLOV = 12
 SUBSTEPS = 4
-BLOCKS = (6, 6)
+GUESS = 6
 HALO = 16
 LANES = 128
 SLOTS = 16
@@ -56,15 +56,26 @@
     return jnp.where(inside, 1.0, 0.0)
 
 
-def power_step(fields, drag, half):
+def shifted(fields, drag, double, rows_of=rise_rows, columns_of=rise_columns):
     vx, vy, b, p = fields
-    quarter = dt_total / RADIUS
     return (
-        -half * rise_rows(p) - drag[0] * vx,
-        -half * rise_columns(p) + quarter * b - drag[1] * vy,
-        (-buoyancy_sq * quarter) * vy - drag[2] * b,
-        -half * (rise_rows(vx) + rise_columns(vy)) - drag[3] * p,
-    )
+        -double * rows_of(p) - drag[0] * vx,
+        -double * columns_of(p) + dt_total * b - drag[1] * vy,
+        (-buoyancy_sq * dt_total) * vy - drag[2] * b,
+        -double * (rows_of(vx) + columns_of(vy)) - drag[3] * p,
+    )
+
+
+def forcing_of(state, damping, half, rows_of=rise_rows, columns_of=rise_columns):
+    vx, vy, b, p = state
+    linear = (
+        -half * rows_of(p),
+        -half * columns_of(p) + b,
+        -buoyancy_sq * vy,
+        -half * (rows_of(vx) + columns_of(vy)),
+    )
+    square = [damping[f] * state[f] * state[f] for f in range(4)]
+    return [linear[f] - square[f] * state[f] for f in range(4)], [(3.0 * dt_total) * x for x in square]
 
 
 def two_sum(a, b):
@@ -114,23 +125,21 @@
     return jnp.sum(total, axis=0, keepdims=True)
 
 
-def gram_out(old, new, table_ref, send_ref):
-    first = len(old)
+GROUP = LANES // SLOTS
+
+
+def gram_out(vectors, table_ref, send_ref):
     table_ref[...] = jnp.zeros_like(table_ref)
-    for j in range(len(new)):
-        for i in range(first):
-            table_ref[j * SLOTS + i : j * SLOTS + i + 1, :] = pair_rows(old[i](), new[j]())
+    for j in range(len(vectors)):
         for i in range(j + 1):
-            row = pair_rows(new[i](), new[j]())
-            table_ref[j * SLOTS + first + i : j * SLOTS + first + i + 1, :] = row
-            if i != j:
-                table_ref[i * SLOTS + first + j : i * SLOTS + first + j + 1, :] = row
-    turned = jnp.transpose(table_ref[...])
+            table_ref[j * SLOTS + i : j * SLOTS + i + 1, :] = pair_rows(vectors[i](), vectors[j]())
     zero = jnp.zeros((8, LANES), jnp.float32)
-    high, low = tree_sum([(turned[r : r + 8], zero) for r in range(0, LANES, 8)])
-    for d in range(send_ref.shape[0]):
-        send_ref[d, 0:1] = high[0:1]
-        send_ref[d, 1:2] = low[0:1]
+    for g in range(table_ref.shape[0] // LANES):
+        turned = jnp.transpose(table_ref[g * LANES : (g + 1) * LANES])
+        high, low = tree_sum([(turned[r : r + 8], zero) for r in range(0, LANES, 8)])
+        for d in range(send_ref.shape[0]):
+            send_ref[d, 2 * g : 2 * g + 1] = high[0:1]
+            send_ref[d, 2 * g + 1 : 2 * g + 2] = low[0:1]
 
 
 def edge_kernel(far_state_ref, far_damping_ref, state_ref, damping_ref, *refs):
@@ -181,7 +190,7 @@
 
 def first_kernel(count, state_ref, damping_ref, *refs):
     halo_refs = refs[:count]
-    up_ref, down_ref, basis_ref, drag_ref, send_ref, table_ref = refs[count:]
+    up_ref, down_ref, guess_ref, inner_ref, small_ref, send_ref, basis_ref, drag_ref, table_ref = refs[count:]
     height, width = state_ref.shape[1:]
     rows, columns = height + 2 * HALO, width + LANES
     tiles = width // LANES
@@ -206,42 +215,62 @@
 
     state = [whole(f) for f in range(4)]
     damping = [whole(4 + f) for f in range(4)]
-    vx, vy, b, p = state
-    half = 0.5 * mask
-    linear = (
-        -half * rise_rows(p),
-        -half * rise_columns(p) + b,
-        -buoyancy_sq * vy,
-        -half * (rise_rows(vx) + rise_columns(vy)),
-    )
+    forcing, drag = forcing_of(state, damping, 0.5 * mask)
+    guess, scale = guessed(guess_ref)
+    steps = basis_columns(guess)
+    small_ref[0] = by_lane(steps, 0, jnp.zeros(TILE, jnp.float32))
+    small_ref[1] = jnp.broadcast_to(scale, TILE)
+    wide = lambda x: jnp.concatenate([x] * (columns // LANES), axis=1)
+    start = wide(1.0 / scale)
     for f in range(4):
-        square = damping[f] * state[f] * state[f]
-        basis_ref[0, f] = linear[f] - square * state[f]
-        drag_ref[f] = (3.0 * dt_total / RADIUS) * square
-    half = (0.5 * dt_total / RADIUS) * mask
-    drag = [drag_ref[f] + SHIFT / RADIUS for f in range(4)]
-    steps = BLOCKS[0]
-    for step in range(steps):
-        skip = (HALO - (KRYLOV - step)) // 8 * 8 if step else 0
+        basis_ref[0, f] = forcing[f] * start
+        drag_ref[f] = drag[f]
+    double = (0.5 * dt_total) * mask
+    for c, column in enumerate(steps):
+        skip = (HALO - (KRYLOV - c)) // 8 * 8 if c else 0
         lines = slice(skip, rows - skip)
-        current = [basis_ref[step, f, lines] for f in range(4)]
-        for f, value in enumerate(power_step(current, [d[lines] for d in drag], half[lines])):
-            basis_ref[step + 1, f, lines] = value
-
-    def interior(j):
-        return lambda: [basis_ref[j, f, HALO : rows - HALO, :width] for f in range(4)]
-
-    gram_out([], [interior(j) for j in range(steps + 1)], table_ref, send_ref)
+        entry = lambda i: wide(column[i : i + 1])
+        shift, inverse = entry(c), wide(1.0 / column[c + 1 : c + 2])
+        current = [basis_ref[c, f, lines] for f in range(4)]
+        image = shifted(current, [drag_ref[f, lines] + shift for f in range(4)], double[lines])
+        for f in range(4):
+            value = image[f]
+            for i in range(0 if c < GUESS else c - 1, c):
+                value = value - entry(i) * basis_ref[i, f, lines]
+            basis_ref[c + 1, f, lines] = value * inverse
+
+    for j in range(KRYLOV + 1):
+        for f in range(4):
+            inner_ref[j, f] = basis_ref[j, f, HALO : rows - HALO, :width]
+    gram_out([lambda j=j: [inner_ref[j, f] for f in range(4)] for j in range(KRYLOV + 1)], table_ref, send_ref)
+
+
+def guess_kernel(state_ref, damping_ref, send_ref, basis_ref, table_ref):
+    height, width = state_ref.shape[1:]
+    line, lane = iota((height, width), 0), iota((height, width), 1)
+
+    def rows_of(x):
+        return jnp.where(line < height - 1, pltpu.roll(x, height - 1, 0), 0.0) - jnp.where(line > 0, pltpu.roll(x, 1, 0), 0.0)
+
+    def columns_of(x):
+        return jnp.where(lane < width - 1, pltpu.roll(x, width - 1, 1), 0.0) - jnp.where(lane > 0, pltpu.roll(x, 1, 1), 0.0)
+
+    state, damping = [state_ref[f] for f in range(4)], [damping_ref[f] for f in range(4)]
+    forcing, drag = forcing_of(state, damping, 0.5, rows_of, columns_of)
+    drag = [x + SHIFT for x in drag]
+    for f in range(4):
+        basis_ref[0, f] = forcing[f]
+    for c in range(GUESS):
+        image = shifted([basis_ref[c, f] for f in range(4)], drag, 0.5 * dt_total, rows_of, columns_of)
+        for f in range(4):
+            basis_ref[c + 1, f] = image[f] * (1.0 / RADIUS)
+    gram_out([lambda j=j: [basis_ref[j, f] for f in range(4)] for j in range(GUESS + 1)], table_ref, send_ref)
 
 
 dot = functools.partial(jnp.dot, precision=HIGH, preferred_element_type=jnp.float32)
 TILE = (SLOTS, LANES)
 
 
-def block_tile(first, count):
-    return (-(-(first + count + 1) // 8) * 8, LANES)
-
-
 def tall(x):
     return jnp.concatenate([x, jnp.zeros((LANES - x.shape[0], LANES), jnp.float32)], axis=0)
 
@@ -254,24 +283,20 @@
     return jnp.sum(x, axis=1, keepdims=True)
 
 
-def gram_matrix(received_ref, first, count):
+def gram_matrix(received_ref, count):
     devices = received_ref.shape[0]
-    tile = block_tile(first, count)
+    tile = (-(-count // 8) * 8, LANES)
     row, lane = iota(tile, 0), iota(tile, 1)
-    parts = []
-    for packed in tree_sum([(received_ref[d : d + 8, 0, :], received_ref[d : d + 8, 1, :]) for d in range(0, devices, 8)]):
-        packed = jnp.concatenate([packed] * (tile[0] // 8), axis=0)
-        below = jnp.zeros(tile, jnp.float32)
-        for j in range(count + 1):
-            line = pltpu.roll(packed, LANES - j * SLOTS, 1) if j else packed
-            below = jnp.where((row == first + j) & (lane < SLOTS), line, below)
-        parts.append(jnp.where(row >= first, below, jnp.where(lane >= first, flip(below), 0.0)))
-    return parts[0] + old_unit(first, tile), parts[1]
-
-
-def old_unit(first, tile):
-    row, lane = iota(tile, 0), iota(tile, 1)
-    return jnp.where((row == lane) & (row < first), 1.0, 0.0)
+    below = [jnp.zeros(tile, jnp.float32)] * 2
+    for g in range(0, count, GROUP):
+        at = g // GROUP * 2
+        tiles = [(received_ref[d : d + 8, at, :], received_ref[d : d + 8, at + 1, :]) for d in range(0, devices, 8)]
+        for part, packed in enumerate(tree_sum(tiles)):
+            packed = jnp.concatenate([packed] * (tile[0] // 8), axis=0)
+            for j in range(g, min(g + GROUP, count)):
+                turned = pltpu.roll(packed, LANES - (j - g) * SLOTS, 1) if j > g else packed
+                below[part] = jnp.where((row == j) & (lane < SLOTS), turned, below[part])
+    return [jnp.where(lane <= row, x, flip(x)) for x in below]
 
 
 def flip(x):
@@ -292,52 +317,17 @@
     return added([x[a : a + 1] * column for a, column in enumerate(columns)])
 
 
-def gram_matrix(received_ref, first, count):
-    devices = received_ref.shape[0]
-    tile = block_tile(first, count)
-    row, lane = iota(tile, 0), iota(tile, 1)
-    parts = []
-    for packed in tree_sum([(received_ref[d : d + 8, 0, :], received_ref[d : d + 8, 1, :]) for d in range(0, devices, 8)]):
-        packed = jnp.concatenate([packed] * (tile[0] // 8), axis=0)
-        below = jnp.zeros(tile, jnp.float32)
-        for j in range(count + 1):
-            line = pltpu.roll(packed, LANES - j * SLOTS, 1) if j else packed
-            below = jnp.where((row == first + j) & (lane < SLOTS), line, below)
-        parts.append(jnp.where(row >= first, below, jnp.where(lane >= first, flip(below), 0.0)))
-    return parts[0] + old_unit(first, tile), parts[1]
-
-
-def old_unit(first, tile):
-    row, lane = iota(tile, 0), iota(tile, 1)
-    return jnp.where((row == lane) & (row < first), 1.0, 0.0)
-
-
-def flip(x):
-    return jnp.transpose(tall(x))[: x.shape[0]]
-
-
-def small_dot(a, b):
-    terms = [a[:, k : k + 1] * b[k : k + 1] for k in range(min(KRYLOV + 1, b.shape[0]))]
-    while len(terms) > 1:
-        terms = [terms[k] + terms[k + 1] for k in range(0, len(terms) - 1, 2)] + terms[len(terms) // 2 * 2 :]
-    return terms[0]
-
-
-def gram_schmidt(gram, image_of, start, first, count):
+def gram_schmidt(gram, image_of, start, count):
     row = iota(gram[0].shape, 0)
-    vector = jnp.where(row == first, start, 0.0)
-    raw, raw_image, inverse = vector, gram[first] * start, 1.0
-    vectors, images, hess = [vector], [], []
-    for c in range(first, first + count):
+    raw, raw_image, inverse = jnp.where(row == 0, start, 0.0), gram[0] * start, 1.0
+    vectors, images, hess = [raw], [], []
+    for c in range(count):
         moved = image_of(raw, c)
         products = [down_sum(image * moved) for image in images]
         own = down_sum(raw_image * moved) * (inverse * inverse)
         images.append(raw_image * inverse)
         rest = added([moved] + [-product * other for product, other in zip(products, vectors)])
-        seen = added([jnp.where(row == first + k, product, 0.0) for k, product in enumerate(products)] + [jnp.zeros_like(moved)])
-        if first:
-            older = jnp.where(row < first, weighted(gram[: c + 2], moved), 0.0)
-            rest, seen = rest - older, seen + older
+        seen = added([jnp.where(row == k, product, 0.0) for k, product in enumerate(products)] + [jnp.zeros_like(moved)])
         raw = rest * inverse - own * vectors[-1]
         column = seen * inverse + jnp.where(row == c, own, 0.0)
         raw_image = weighted(gram[: c + 2], raw)
@@ -370,39 +360,46 @@
     result = zero
     for c, vector in enumerate(vectors):
         high, low = add_product((zero, zero), vector, image[0], image_parts)
-        high, low = tree_sum([(high, low + vector * image[1])])
-        result = jnp.where(row == c, high + low, result)
+        low = low + vector * image[1]
+        high, low = tree_sum([(high[r : r + 8], low[r : r + 8]) for r in range(0, row.shape[0], 8)])
+        result = jnp.where(row == c, (high + low)[0:1], result)
     return result
 
 
-def basis_terms(hess, first):
-    c = first - 1
-    shift = 0.5 * (hess[c - 1][c - 1 : c] + hess[c][c : c + 1])
-    return shift, hess[c][c - 1 : c]
-
-
-def orthogonalize(received_ref, hess, first, count):
-    gram, gram_low = gram_matrix(received_ref, first, count)
-    slots = first + count + 1
-    gram = columns_of(gram, slots)
-    row = iota(gram[0].shape, 0)
-
-    def basis_image(x, c):
-        fresh = jnp.where(row >= first, x, 0.0)
-        if not first:
-            return RADIUS * pltpu.roll(fresh, 1, 0) + SHIFT * fresh
-        shift, back = basis_terms(hess, first)
-        image = RADIUS * pltpu.roll(fresh, 1, 0) + shift * fresh
-        image = image + jnp.where(row >= first, back * pltpu.roll(fresh, row.shape[0] - 1, 0), 0.0)
-        return image + weighted(hess, x)
-
-    if first:
-        return *gram_schmidt(gram, basis_image, 1.0, first, count), None
-    square = gram[0][0:1] + norm_eps
-    beta = jnp.sqrt(square)
-    vectors, image = gram_schmidt(gram, basis_image, 1.0 / beta, first, count)
-    gram = columns_of(refined_gram(vectors, gram, columns_of(gram_low, slots)), slots)
-    again, hess = gram_schmidt(gram, lambda x, c: weighted(image[: c + 1], x), 1.0, first, count)
+def guessed(received_ref):
+    gram = columns_of(gram_matrix(received_ref, GUESS + 1)[0], GUESS + 1)
+    beta = jnp.sqrt(gram[0][0:1] + norm_eps)
+
+    def image_of(x, c):
+        return RADIUS * pltpu.roll(x, 1, 0) + SHIFT * x
+
+    return gram_schmidt(gram, image_of, 1.0 / beta, GUESS)[1], beta
+
+
+def basis_columns(guess):
+    row = iota(TILE, 0)
+    more = jnp.zeros((SLOTS - guess[0].shape[0], LANES), jnp.float32)
+    columns = []
+    for c, column in enumerate(guess):
+        length = jnp.maximum(column[c + 1 : c + 2], 0.5 * RADIUS)
+        columns.append(jnp.where(row == c + 1, length, jnp.concatenate([column, more], axis=0)))
+    c = GUESS - 1
+    shift = 0.5 * (guess[c - 1][c - 1 : c] + guess[c][c : c + 1])
+    length = jnp.maximum(0.5 * (guess[c - 1][c : c + 1] + guess[c][c + 1 : c + 2]), 0.5 * RADIUS)
+    back = guess[c][c - 1 : c]
+    for c in range(GUESS, KRYLOV):
+        column = jnp.where(row == c, shift, jnp.where(row == c + 1, length, 0.0))
+        columns.append(jnp.where(row == c - 1, back, column))
+    return columns
+
+
+def orthogonalize(received_ref, steps, scale):
+    slots = KRYLOV + 1
+    gram, gram_low = [columns_of(x, slots) for x in gram_matrix(received_ref, slots)]
+    beta = jnp.sqrt(scale * scale * gram[0][0:1] + norm_eps)
+    vectors, image = gram_schmidt(gram, lambda x, c: weighted(steps[: c + 1], x), scale / beta, KRYLOV)
+    gram = columns_of(refined_gram(vectors, gram, gram_low), slots)
+    again, hess = gram_schmidt(gram, lambda x, c: weighted(image[: c + 1], x), 1.0, KRYLOV)
     return [weighted(vectors[: c + 1], x) for c, x in enumerate(again)], hess, beta
 
 
@@ -415,64 +412,24 @@
     return total
 
 
-def middle_kernel(received_ref, drag_in_ref, basis_in_ref, basis_ref, kept_ref, small_ref, send_ref, table_ref):
-    first, count = BLOCKS
-    rows, columns = basis_ref.shape[2:]
-    edge = (basis_in_ref.shape[2] - rows) // 2
-    halo = HALO - edge
-    body = columns - LANES
-    vectors, hess, beta = orthogonalize(received_ref, [], 0, first)
-    small_ref[0] = jnp.zeros(TILE, jnp.float32)
-    small_ref[0, : hess[0].shape[0]] = by_lane(hess, 0, jnp.zeros_like(hess[0]))
-    small_ref[1] = jnp.broadcast_to(beta, TILE)
+def block_parts(basis_ref, f):
+    return [(j, lambda j=j: basis_ref[j, f]) for j in range(KRYLOV + 1)]
+
+
+def last_kernel(received_ref, small_ref, basis_ref, small_out_ref, peak_ref):
+    steps = columns_of(small_ref[0], KRYLOV)
+    vectors, hess, beta = orthogonalize(received_ref, steps, small_ref[1, 0:1])
+    zero = jnp.zeros(TILE, jnp.float32)
+    small_out_ref[0] = by_lane(hess, 0, zero)
+    small_out_ref[1] = jnp.broadcast_to(beta, TILE)
+    small_out_ref[2] = by_lane(vectors, 0, zero)
     for f in range(4):
-        inner = [(j, lambda j=j: basis_in_ref[j, f, HALO : edge + rows - halo, :body]) for j in range(first + 1)]
-        for c in range(first):
-            kept_ref[c, f] = combine(vectors[c], inner[: c + 1])
-        outer = [(j, lambda j=j: basis_in_ref[j, f, edge : edge + rows]) for j in range(first + 1)]
-        basis_ref[0, f] = combine(vectors[first], outer)
-    wide = lambda x: jnp.concatenate([x * (1.0 / RADIUS)] * (columns // LANES), axis=1)
-    shift, back = map(wide, basis_terms(hess, first))
-    half = (0.5 * dt_total / RADIUS) * grid_mask(rows, columns, halo)
-    drag = [drag_in_ref[f, edge : edge + rows] + shift for f in range(4)]
-    for step in range(count):
-        current = [basis_ref[step, f] for f in range(4)]
-        for f, value in enumerate(power_step(current, drag, half)):
-            basis_ref[step + 1, f] = value - back * basis_ref[step - 1, f] if step else value
-
-    def interior(ref, j, lines):
-        return lambda: [ref[j, f, lines, :body] for f in range(4)]
-
-    gram_out(
-        [interior(kept_ref, i, slice(None)) for i in range(first)],
-        [interior(basis_ref, j, slice(halo, rows - halo)) for j in range(count + 1)],
-        table_ref,
-        send_ref,
-    )
-
-
-def block_parts(kept_ref, basis_ref, f):
-    first, count = BLOCKS
-    height, body = kept_ref.shape[2:]
-    halo = (basis_ref.shape[2] - height) // 2
-    parts = [(i, lambda i=i: kept_ref[i, f]) for i in range(first)]
-    return parts + [(first + j, lambda j=j: basis_ref[j, f, halo : halo + height, :body]) for j in range(count + 1)]
-
-
-def last_kernel(received_ref, small_ref, kept_ref, basis_ref, small_out_ref, peak_ref):
-    first, count = BLOCKS
-    old = small_ref[0]
-    vectors, hess, _ = orthogonalize(received_ref, columns_of(old, first), first, count)
-    small_out_ref[0] = by_lane(hess, first, old)
-    small_out_ref[1] = small_ref[1]
-    small_out_ref[2] = by_lane(vectors, first, old_unit(first, TILE))
-    for f in range(4):
-        peak = jnp.max(jnp.abs(combine(vectors[count], block_parts(kept_ref, basis_ref, f))), axis=0, keepdims=True)
+        peak = jnp.max(jnp.abs(combine(vectors[KRYLOV], block_parts(basis_ref, f))), axis=0, keepdims=True)
         for d in range(peak_ref.shape[0]):
             peak_ref[d, f : f + 1] = peak
 
 
-def exp_kernel(weights_ref, small_ref, state_ref, kept_ref, basis_ref, combined_ref, highest_ref):
+def exp_kernel(weights_ref, small_ref, state_ref, basis_ref, combined_ref, highest_ref):
     hess, beta, vectors = flip(small_ref[0]), small_ref[1, 0:1, 0:1], small_ref[2]
     size = SUBSTEPS * SLOTS
     row, lane = iota((size, LANES), 0), iota((size, LANES), 1)
@@ -521,7 +478,7 @@
     mixing = jnp.where(lane[0:1] < KRYLOV, mixing, 0.0)
     share = jnp.broadcast_to(across_sum(vectors * mixing), TILE)
     for f in range(4):
-        combined_ref[f] = state_ref[f] + combine(share, block_parts(kept_ref, basis_ref, f))
+        combined_ref[f] = state_ref[f] + combine(share, block_parts(basis_ref, f))
     highest_ref[...] = jnp.broadcast_to(highest, highest_ref.shape)
 
 
@@ -552,11 +509,8 @@
         )(*args)
 
     exchange = lambda x, axes: lax.all_to_all(x, axes, 0, 0)
-    table = near(LANES, LANES)
-    send_shape = near(devices, 2, LANES)
-    short = height + HALO
-    first, count = BLOCKS
-
+    table = lambda count: near(-(-count * SLOTS // LANES) * LANES, LANES)
+    sends = lambda count: near(devices, -(-count // GROUP) * 2, LANES)
     whole = near(fields, height, width)
     state, damping, *edges = call(
         edge_kernel,
@@ -573,6 +527,14 @@
             lax.ppermute(edges[0], "gy", [((i + 1) % sides, i) for i in range(sides)]),
             lax.ppermute(edges[1], "gy", [(i, (i + 1) % sides) for i in range(sides)]),
         ]
+    (send,) = call(
+        guess_kernel,
+        [sends(GUESS + 1)],
+        state,
+        damping,
+        scratch=[near(GUESS + 1, fields, height, width), table(GUESS + 1)],
+    )
+    guess = exchange(send, ALL)
     number = len(halos)
     stack = (8 * (width // LANES) + number) * HALO
     packs = call(
@@ -585,30 +547,26 @@
     up = lax.ppermute(packs[0], ROWS, [(i, (i + 1) % lines) for i in range(lines)])
     down = lax.ppermute(packs[-1], ROWS, [((i + 1) % lines, i) for i in range(lines)])
     tall_rows = height + 2 * HALO
-    basis, drag, send = call(
+    basis, small, send = call(
         functools.partial(first_kernel, number),
-        [near(first + 1, fields, tall_rows, columns), near(fields, tall_rows, columns), send_shape],
+        [near(KRYLOV + 1, fields, height, width), near(2, *TILE), sends(KRYLOV + 1)],
         state,
         damping,
         *halos,
         up,
         down,
-        scratch=[table],
-    )
-    basis, kept, small, send = call(
-        middle_kernel,
-        [near(count + 1, fields, short, columns), near(first, fields, height, width), near(2, *TILE), send_shape],
-        exchange(send, ALL),
-        drag,
-        basis,
-        scratch=[table],
+        guess,
+        scratch=[
+            near(KRYLOV + 1, fields, tall_rows, columns),
+            near(fields, tall_rows, columns),
+            table(KRYLOV + 1),
+        ],
     )
     small, peaks = call(
         last_kernel,
         [near(3, *TILE), near(lines, fields, width)],
         exchange(send, ALL),
         small,
-        kept,
         basis,
     )
     combined, highest = call(
@@ -617,7 +575,6 @@
         weights,
         small,
         state,
-        kept,
         basis,
         smem=(0,),
     )

time: 51.8 us -> 48.6 us (0.938)
  waiting for transfers between devices: 12.2 us -> 3.97 us
  blocking collectives: 19.5 us -> 22.5 us
  Pallas kernels: 9.32 us -> 10.6 us
  local copies, waits for them, and re-layouts: 0.01 us -> 0.65 us
    ppermute x1, waiting for transfers between devices: 3.9 us -> 0.01 us  [shards(): lax.ppermute(packs[-1], ROWS, [((i + 1) % lines, i) for i in range(lines)])]
    ppermute x1, waiting for transfers between devices: 3.66 us -> 0.01 us  [shards(): lax.ppermute(packs[0], ROWS, [(i, (i + 1) % lines) for i in range(lines)])]
    all_to_all x2, blocking collectives: 19.5 us -> 22.5 us  [shards(): exchange = lambda x, axes: lax.all_to_all(x, axes, 0, 0)]
    pallas_call x7, Pallas kernels: 9.32 us -> 10.6 us  [call(): pl.pallas_call(kernel, out_shape=outs, in_specs=specs, out_specs=[VMEM] *...]
    unnamed x2, local copies, waits for them, and re-layouts: 0.01 us -> 0.65 us
    all_to_all x1, waiting for transfers between devices: 2.98 us -> 2.33 us  [shards(): exchange = lambda x, axes: lax.all_to_all(x, axes, 0, 0)]
  transfers between devices with their start and end apart: 4 -> 4, of which waited for: 4 -> 2; matrix products, arithmetic and copies ran while one was open for 0% -> 0% of each run, Pallas kernels for 7% -> 9%
where the time goes in v6:
time: 48.6 us; the launch traced here: 48.3 us
  blocking collectives  22.5 us (46%)
  Pallas kernels  10.6 us (22%)
  starting transfers between devices  9.92 us (20%)
  waiting for transfers between devices  3.97 us (8%)
  between operations  0.68 us (1%)
  local copies, waits for them, and re-layouts  0.65 us (1%)
    all_to_all x2, blocking collectives, shards(): exchange = lambda x, axes: lax.all_to_all(x, axes, 0, 0)  22.5 us
    pallas_call x7, Pallas kernels, call(): pl.pallas_call(kernel, out_shape=outs, in_specs=specs, out_specs=[VMEM] *...  10.6 us
    all_to_all x1, starting transfers between devices, shards(): exchange = lambda x, axes: lax.all_to_all(x, axes, 0, 0)  3.48 us
    ppermute x1, starting transfers between devices, shards(): lax.ppermute(packs[-1], ROWS, [((i + 1) % lines, i) for i in range(lines)])  3.38 us
    ppermute x1, starting transfers between devices, shards(): halos = [lax.ppermute(edges[0], 'gy', [(0, 1), (1, 0)])]  3.06 us
    all_to_all x1, waiting for transfers between devices, shards(): exchange = lambda x, axes: lax.all_to_all(x, axes, 0, 0)  2.33 us
    ppermute x1, waiting for transfers between devices, shards(): halos = [lax.ppermute(edges[0], 'gy', [(0, 1), (1, 0)])]  1.63 us
  transfers between devices with their start and end apart: 4, of which 2 were waited for; matrix products, arithmetic and copies ran while one was open for 0% of the time, Pallas kernels for 9%

profile of v6, /device:TPU:0, one launch (start us, length us, event | category | flops | bytes accessed | tf_op | source)
XLA Modules:
  0.0 48.3 jit_solution(10348688788025340956)
XLA Ops:
  0.6 1.0 %shard_map.50 = (f32[4,16,256]{2,1,0:T(8,128)S(1)}, f32[4,16,256]{2,1,0:T(8,128)S(1)}, f32[16,128]{1,0:T(8,128)S(1)}) custom-call(f32[4,16,256]{2,1,0:T(8,128)} %far_state_ref.1, f32[4,16,256]{2,1,0:T(8,128)} %far_damping_ref.1), custom_call_target="tpu_custom_call" | custom-call | tf_op jit(solution)/shard_map/pallas_call | solution.py:502
  1.7 3.1 %collective-permute-start = (f32[16,128]{1,0:T(8,128)S(1)}, f32[16,128]{1,0:T(8,128)S(1)}, u32[]{:S(2)}, u32[]{:S(2)}) collective-permute-start(f32[16,128]{1,0:T(8,128)S(1)} %get-tuple-element.14), channel_id=1, source_target_pairs={{0,1},{1,0},{2,3},{3,2},{4,5},{5,4},{6,7},{7,6},{8,9},{9,8},{10,11... | collective-permute-start | bytes 24584 | tf_op jit(solution)/shard_map/ppermute | solution.py:524
  4.7 1.6 %collective-permute-done.refs_0_ = f32[16,128]{1,0:T(8,128)S(1)} collective-permute-done((f32[16,128]{1,0:T(8,128)S(1)}, f32[16,128]{1,0:T(8,128)S(1)}, u32[]{:S(2)}, u32[]{:S(2)}) %collective-permute-start) | collective-permute-done | bytes 8224 | tf_op jit(solution)/shard_map/ppermute | solution.py:524
  6.4 3.4 %collective-permute-start.2 = (f32[272,128]{1,0:T(8,128)S(1)}, f32[272,128]{1,0:T(8,128)S(1)}, u32[]{:S(2)}, u32[]{:S(2)}) collective-permute-start(f32[272,128]{1,0:T(8,128)S(1)} %shard_map.51), channel_id=1, source_target_pairs={{2,0},{4,2},{6,4},{8,6},{10,8},{12,10},{14,12},{16,14},{18,16},{20... | collective-permute-start | bytes 417800 | tf_op jit(solution)/shard_map/ppermute | solution.py:548
  9.8 0.0 collective-permute-start.1
  9.8 0.7 %shard_map.52 = f32[32,2,128]{2,1,0:T(2,128)S(1)} custom-call(f32[4,16,256]{2,1,0:T(8,128)S(1)} %get-tuple-element.12.state_ref, f32[4,16,256]{2,1,0:T(8,128)S(1)} %get-tuple-element.13.damping_ref), custom_call_target="tpu_custom_call" | custom-call | tf_op jit(solution)/shard_map/pallas_call | solution.py:502
  10.4 13.6 %all_to_all.15.refs_3_ = f32[32,2,128]{2,1,0:T(2,128)S(1)} all-to-all(f32[32,2,128]{2,1,0:T(2,128)S(1)} %shard_map.52), channel_id=1, replica_groups=mesh['sub'=4,'gx'=4,'gy'=2] {'sub','gx','gy'}, dimensions={0} | all-to-all | bytes 65536 | tf_op jit(solution)/shard_map/all_to_all | solution.py:511
  24.0 0.0 collective-permute-done.2.refs_2_
  24.0 0.0 collective-permute-done.1.refs_1_
  24.0 2.4 %shard_map.53 = (f32[13,4,16,256]{3,2,1,0:T(8,128)S(1)}, f32[2,16,128]{2,1,0:T(8,128)S(1)}, f32[32,4,128]{2,1,0:T(4,128)S(1)}) custom-call(f32[4,16,256]{2,1,0:T(8,128)S(1)} %get-tuple-element.12.state_ref, f32[4,16,256]{2,1,0:T(8,128)S(1)} %get-tuple-element.13.damping_ref, f32[16,128]{1,0:T(8,128)S(1)} %collective-permute-done.refs_0_, ...), custom_call_target="tpu_custom_call" | custom-call | tf_op jit(solution)/shard_map/pallas_call | solution.py:502
  26.4 9.0 %all_to_all.16.received_ref = f32[32,4,128]{2,1,0:T(4,128)S(1)} all-to-all(f32[32,4,128]{2,1,0:T(4,128)S(1)} %get-tuple-element.15), channel_id=1, replica_groups=mesh['sub'=4,'gx'=4,'gy'=2] {'sub','gx','gy'}, dimensions={0} | all-to-all | bytes 131072 | tf_op jit(solution)/shard_map/all_to_all | solution.py:511
  35.4 2.2 %shard_map.54 = (f32[3,16,128]{2,1,0:T(8,128)S(1)}, f32[16,4,256]{2,1,0:T(4,128)}) custom-call(f32[32,4,128]{2,1,0:T(4,128)S(1)} %all_to_all.16.received_ref, f32[2,16,128]{2,1,0:T(8,128)S(1)} %get-tuple-element.16.small_ref, f32[13,4,16,256]{3,2,1,0:T(8,128)S(1)} %get-tuple-element.17.basis_ref), custom_call_target="tpu_custom_call" | custom-call | tf_op jit(solution)/shard_map/pallas_call | solution.py:502
  37.6 3.5 %all-to-all-start.2 = ((f32[16,4,256]{2,1,0:T(4,128)}), f32[16,4,256]{2,1,0:T(4,128)S(1)}, u32[]{:S(2)}, u32[]{:S(2)}) async-start(f32[16,4,256]{2,1,0:T(4,128)} %get-tuple-element.21), calls=%async_computation.2 | async-start | bytes 131072 | tf_op jit(solution)/shard_map/all_to_all | solution.py:511
  41.1 0.0 copy-start
  41.1 0.6 %copy-done = f32[4]{0:T(128)S(1)} copy-done((f32[4]{0:T(128)S(1)}, f32[4]{0:T(128)}, u32[]{:S(2)}) %copy-start) | copy-done | bytes 40
  41.8 3.6 %shard_map.55 = (f32[4,16,256]{2,1,0:T(8,128)}, f32[8,128]{1,0:T(8,128)S(1)}) custom-call(f32[4]{0:T(128)S(1)} %copy-done, f32[3,16,128]{2,1,0:T(8,128)S(1)} %get-tuple-element.18.small_ref, f32[4,16,256]{2,1,0:T(8,128)S(1)} %get-tuple-element.12.state_ref, f32[13,4,16,256]{3,2,1,0:T(8,128)S(1)} %get-tuple-element.17.basis_ref), custom_call_target="tpu_custom_call" | custom-call | tf_op jit(solution)/shard_map/pallas_call | solution.py:502
  45.4 2.3 %all-to-all-done.2.peaks_ref = f32[16,4,256]{2,1,0:T(4,128)S(1)} async-done(((f32[16,4,256]{2,1,0:T(4,128)}), f32[16,4,256]{2,1,0:T(4,128)S(1)}, u32[]{:S(2)}, u32[]{:S(2)}) %all-to-all-start.2) | async-done | bytes 65568 | tf_op jit(solution)/shard_map/all_to_all | solution.py:511
  47.7 0.6 %shard_map.56 = f32[4,256]{1,0:T(4,128)} custom-call(f32[8,128]{1,0:T(8,128)S(1)} %get-tuple-element.20.highest_ref, f32[16,4,256]{2,1,0:T(4,128)S(1)} %all-to-all-done.2.peaks_ref), custom_call_target="tpu_custom_call" | custom-call | tf_op jit(solution)/shard_map/pallas_call | solution.py:502
  (1 shorter events, 0.0 us)
Async XLA Ops:
  1.7 4.7 %collective-permute-start = (f32[16,128]{1,0:T(8,128)S(1)}, f32[16,128]{1,0:T(8,128)S(1)}, u32[]{:S(2)}, u32[]{:S(2)}) collective-permute-start(f32[16,128]{1,0:T(8,128)S(1)} %get-tuple-element.14), channel_id=1, source_target_pairs={{0,1},{1,0},{2,3},{3,2},{4,5},{5,4},{6,7},{7,6},{8,9},{9,8},{10,11... | collective-permute-start | bytes 24584 | tf_op jit(solution)/shard_map/ppermute | solution.py:524
  6.4 17.6 %collective-permute-start.2 = (f32[272,128]{1,0:T(8,128)S(1)}, f32[272,128]{1,0:T(8,128)S(1)}, u32[]{:S(2)}, u32[]{:S(2)}) collective-permute-start(f32[272,128]{1,0:T(8,128)S(1)} %shard_map.51), channel_id=1, source_target_pairs={{2,0},{4,2},{6,4},{8,6},{10,8},{12,10},{14,12},{16,14},{18,16},{20... | collective-permute-start | bytes 417800 | tf_op jit(solution)/shard_map/ppermute | solution.py:548
  9.8 14.3 %collective-permute-start.1 = (f32[272,128]{1,0:T(8,128)S(1)}, f32[272,128]{1,0:T(8,128)S(1)}, u32[]{:S(2)}, u32[]{:S(2)}) collective-permute-start(f32[272,128]{1,0:T(8,128)S(1)} %shard_map.51), channel_id=1, source_target_pairs={{0,2},{2,4},{4,6},{6,8},{8,10},{10,12},{12,14},{14,16},{16,18},{18... | collective-permute-start | bytes 417800 | tf_op jit(solution)/shard_map/ppermute | solution.py:547
  37.6 10.1 %all-to-all-start.2 = ((f32[16,4,256]{2,1,0:T(4,128)}), f32[16,4,256]{2,1,0:T(4,128)S(1)}, u32[]{:S(2)}, u32[]{:S(2)}) async-start(f32[16,4,256]{2,1,0:T(4,128)} %get-tuple-element.21), calls=%async_computation.2 | async-start | bytes 131072 | tf_op jit(solution)/shard_map/all_to_all | solution.py:511
  41.1 0.7 %copy-start = (f32[4]{0:T(128)S(1)}, f32[4]{0:T(128)}, u32[]{:S(2)}) copy-start(f32[4]{0:T(128)} %weights_ref.1) | copy-start | bytes 52

commit v7 on v6

--- a/solution.py
+++ b/solution.py
@@ -8,10 +8,12 @@
 from jax.experimental.pallas import tpu as pltpu
 from jax.sharding import PartitionSpec as P
 
+
 KRYLOV = 12
 SUBSTEPS = 4
 GUESS = 6
-HALO = 16
+REACH = KRYLOV + 1
+HALO = -(-REACH // 8) * 8
 LANES = 128
 SLOTS = 16
 EDGE = 16
@@ -175,17 +177,19 @@
 def pack_kernel(count, state_ref, damping_ref, *refs):
     halo_refs, out_refs = refs[:count], refs[count:]
     height, width = state_ref.shape[1:]
-    for out_ref, start in zip(out_refs, (height - HALO, 0)):
-        lines = slice(start, start + HALO)
+    for out_ref, start in zip(out_refs, (height - REACH, 0)):
+        lines = slice(start, start + REACH)
         at = 0
         for k in range(8):
             ref = state_ref if k < 4 else damping_ref
             for c in range(0, width, LANES):
-                out_ref[at : at + HALO] = ref[k % 4, lines, c : c + LANES]
-                at += HALO
+                out_ref[at : at + REACH] = ref[k % 4, lines, c : c + LANES]
+                at += REACH
         for halo_ref in halo_refs:
-            out_ref[at : at + HALO] = halo_ref[lines]
-            at += HALO
+            out_ref[at : at + REACH] = halo_ref[lines]
+            at += REACH
+        if at < out_ref.shape[0]:
+            out_ref[at:] = jnp.zeros((out_ref.shape[0] - at, LANES), jnp.float32)
 
 
 def first_kernel(count, state_ref, damping_ref, *refs):
@@ -201,16 +205,20 @@
         right = pltpu.roll(right, LANES - k * EDGE, 1) if k else right
         return jnp.where(lane < LANES // 2, right, pltpu.roll(left, LANES - (k + 1) * EDGE, 1) if k < 7 else left)
 
-    def neighbour(ref, k):
-        parts = [ref[(k * tiles + t) * HALO : (k * tiles + t + 1) * HALO] for t in range(tiles)]
-        at = 8 * tiles * HALO
-        ends = [ref[at + c * HALO : at + (c + 1) * HALO] for c in range(count)]
+    def neighbour(ref, k, above):
+        def piece(n):
+            lines = ref[n * REACH : (n + 1) * REACH]
+            blank = jnp.zeros((HALO - REACH, LANES), jnp.float32)
+            return jnp.concatenate([blank, lines] if above else [lines, blank], axis=0)
+
+        parts = [piece(k * tiles + t) for t in range(tiles)]
+        ends = [piece(8 * tiles + c) for c in range(count)]
         return jnp.concatenate(parts + [side_tile(k, ends[0], ends[-1])], axis=1)
 
     def whole(k):
         ref = state_ref if k < 4 else damping_ref
         own = jnp.concatenate([ref[k % 4], side_tile(k, halo_refs[0][...], halo_refs[-1][...])], axis=1)
-        joined = jnp.concatenate([neighbour(up_ref, k), own, neighbour(down_ref, k)], axis=0)
+        joined = jnp.concatenate([neighbour(up_ref, k, True), own, neighbour(down_ref, k, False)], axis=0)
         return jnp.where(mask > 0, joined, 0.0)
 
     state = [whole(f) for f in range(4)]
@@ -379,13 +387,15 @@
 def basis_columns(guess):
     row = iota(TILE, 0)
     more = jnp.zeros((SLOTS - guess[0].shape[0], LANES), jnp.float32)
-    columns = []
+    columns, lengths, top = [], [], 0.0
     for c, column in enumerate(guess):
-        length = jnp.maximum(column[c + 1 : c + 2], 0.5 * RADIUS)
+        top = jnp.maximum(column[c + 1 : c + 2], top)
+        length = jnp.maximum(column[c + 1 : c + 2], 0.125 * top)
+        lengths.append(length)
         columns.append(jnp.where(row == c + 1, length, jnp.concatenate([column, more], axis=0)))
     c = GUESS - 1
     shift = 0.5 * (guess[c - 1][c - 1 : c] + guess[c][c : c + 1])
-    length = jnp.maximum(0.5 * (guess[c - 1][c : c + 1] + guess[c][c + 1 : c + 2]), 0.5 * RADIUS)
+    length = 0.5 * (lengths[c - 1] + lengths[c])
     back = guess[c][c - 1 : c]
     for c in range(GUESS, KRYLOV):
         column = jnp.where(row == c, shift, jnp.where(row == c + 1, length, 0.0))
@@ -520,6 +530,14 @@
         far=(0, 1),
         scratch=[pltpu.SemaphoreType.DMA((2,))],
     )
+    (send,) = call(
+        guess_kernel,
+        [sends(GUESS + 1)],
+        state,
+        damping,
+        scratch=[near(GUESS + 1, fields, height, width), table(GUESS + 1)],
+    )
+    guess = exchange(send, ALL)
     if sides == 2:
         halos = [lax.ppermute(edges[0], "gy", [(0, 1), (1, 0)])]
     else:
@@ -527,19 +545,11 @@
             lax.ppermute(edges[0], "gy", [((i + 1) % sides, i) for i in range(sides)]),
             lax.ppermute(edges[1], "gy", [(i, (i + 1) % sides) for i in range(sides)]),
         ]
-    (send,) = call(
-        guess_kernel,
-        [sends(GUESS + 1)],
-        state,
-        damping,
-        scratch=[near(GUESS + 1, fields, height, width), table(GUESS + 1)],
-    )
-    guess = exchange(send, ALL)
     number = len(halos)
-    stack = (8 * (width // LANES) + number) * HALO
+    stack = -(-(8 * (width // LANES) + number) * REACH // 8) * 8
     packs = call(
         functools.partial(pack_kernel, number),
-        [near(stack, LANES)] * (1 if height == HALO else 2),
+        [near(stack, LANES)] * 2,
         state,
         damping,
         *halos,

time: 48.6 us -> 47.1 us (0.969)
  blocking collectives: 22.5 us -> 19.9 us
  starting transfers between devices: 9.92 us -> 11.1 us
    all_to_all x2, blocking collectives: 22.5 us -> 19.9 us  [shards(): exchange = lambda x, axes: lax.all_to_all(x, axes, 0, 0)]
    ppermute x1, starting transfers between devices: 0.01 us -> 2.14 us  [shards(): lax.ppermute(packs[0], ROWS, [(i, (i + 1) % lines) for i in range(lines)])]
    ppermute x1, starting transfers between devices: 3.38 us -> 2.37 us  [shards(): lax.ppermute(packs[-1], ROWS, [((i + 1) % lines, i) for i in range(lines)])]
where the time goes in v7:
time: 47.1 us; the launch traced here: 46.8 us
  blocking collectives  19.9 us (42%)
  starting transfers between devices  11.1 us (24%)
  Pallas kernels  10.6 us (23%)
  waiting for transfers between devices  3.97 us (8%)
  between operations  0.68 us (1%)
  local copies, waits for them, and re-layouts  0.65 us (1%)
    all_to_all x2, blocking collectives, shards(): exchange = lambda x, axes: lax.all_to_all(x, axes, 0, 0)  19.9 us
    pallas_call x7, Pallas kernels, call(): pl.pallas_call(kernel, out_shape=outs, in_specs=specs, out_specs=[VMEM] *...  10.6 us
    all_to_all x1, starting transfers between devices, shards(): exchange = lambda x, axes: lax.all_to_all(x, axes, 0, 0)  3.49 us
    ppermute x1, starting transfers between devices, shards(): halos = [lax.ppermute(edges[0], 'gy', [(0, 1), (1, 0)])]  3.06 us
    ppermute x1, starting transfers between devices, shards(): lax.ppermute(packs[-1], ROWS, [((i + 1) % lines, i) for i in range(lines)])  2.37 us
    all_to_all x1, waiting for transfers between devices, shards(): exchange = lambda x, axes: lax.all_to_all(x, axes, 0, 0)  2.34 us
    ppermute x1, starting transfers between devices, shards(): lax.ppermute(packs[0], ROWS, [(i, (i + 1) % lines) for i in range(lines)])  2.14 us
    ppermute x1, waiting for transfers between devices, shards(): halos = [lax.ppermute(edges[0], 'gy', [(0, 1), (1, 0)])]  1.63 us
  transfers between devices with their start and end apart: 4, of which 2 were waited for; matrix products, arithmetic and copies ran while one was open for 0% of the time, Pallas kernels for 9%

profile of v7, /device:TPU:0, one launch (start us, length us, event | category | flops | bytes accessed | tf_op | source)
XLA Modules:
  0.0 46.8 jit_solution(8686237083163067034)
XLA Ops:
  0.6 1.0 %shard_map.50 = (f32[4,16,256]{2,1,0:T(8,128)S(1)}, f32[4,16,256]{2,1,0:T(8,128)S(1)}, f32[16,128]{1,0:T(8,128)S(1)}) custom-call(f32[4,16,256]{2,1,0:T(8,128)} %far_state_ref.1, f32[4,16,256]{2,1,0:T(8,128)} %far_damping_ref.1), custom_call_target="tpu_custom_call" | custom-call | tf_op jit(solution)/shard_map/pallas_call | solution.py:512
  1.7 3.1 %collective-permute-start = (f32[16,128]{1,0:T(8,128)S(1)}, f32[16,128]{1,0:T(8,128)S(1)}, u32[]{:S(2)}, u32[]{:S(2)}) collective-permute-start(f32[16,128]{1,0:T(8,128)S(1)} %get-tuple-element.16), channel_id=1, source_target_pairs={{0,1},{1,0},{2,3},{3,2},{4,5},{5,4},{6,7},{7,6},{8,9},{9,8},{10,11... | collective-permute-start | bytes 24584 | tf_op jit(solution)/shard_map/ppermute | solution.py:542
  4.7 1.6 %collective-permute-done.refs_0_ = f32[16,128]{1,0:T(8,128)S(1)} collective-permute-done((f32[16,128]{1,0:T(8,128)S(1)}, f32[16,128]{1,0:T(8,128)S(1)}, u32[]{:S(2)}, u32[]{:S(2)}) %collective-permute-start) | collective-permute-done | bytes 8224 | tf_op jit(solution)/shard_map/ppermute | solution.py:542
  6.4 2.1 %collective-permute-start.1 = (f32[224,128]{1,0:T(8,128)S(1)}, f32[224,128]{1,0:T(8,128)S(1)}, u32[]{:S(2)}, u32[]{:S(2)}) collective-permute-start(f32[224,128]{1,0:T(8,128)S(1)} %get-tuple-element.17), channel_id=1, source_target_pairs={{0,2},{2,4},{4,6},{6,8},{8,10},{10,12},{12,14},{14,16},{16,18},{18... | collective-permute-start | bytes 344072 | tf_op jit(solution)/shard_map/ppermute | solution.py:557
  8.5 2.4 %collective-permute-start.2 = (f32[224,128]{1,0:T(8,128)S(1)}, f32[224,128]{1,0:T(8,128)S(1)}, u32[]{:S(2)}, u32[]{:S(2)}) collective-permute-start(f32[224,128]{1,0:T(8,128)S(1)} %get-tuple-element.18), channel_id=1, source_target_pairs={{2,0},{4,2},{6,4},{8,6},{10,8},{12,10},{14,12},{16,14},{18,16},{20... | collective-permute-start | bytes 344072 | tf_op jit(solution)/shard_map/ppermute | solution.py:558
  10.9 0.7 %shard_map.52 = f32[32,2,128]{2,1,0:T(2,128)S(1)} custom-call(f32[4,16,256]{2,1,0:T(8,128)S(1)} %get-tuple-element.14.state_ref, f32[4,16,256]{2,1,0:T(8,128)S(1)} %get-tuple-element.15.damping_ref), custom_call_target="tpu_custom_call" | custom-call | tf_op jit(solution)/shard_map/pallas_call | solution.py:512
  11.6 10.9 %all_to_all.15.refs_3_ = f32[32,2,128]{2,1,0:T(2,128)S(1)} all-to-all(f32[32,2,128]{2,1,0:T(2,128)S(1)} %shard_map.52), channel_id=1, replica_groups=mesh['sub'=4,'gx'=4,'gy'=2] {'sub','gx','gy'}, dimensions={0} | all-to-all | bytes 65536 | tf_op jit(solution)/shard_map/all_to_all | solution.py:521
  22.5 0.0 collective-permute-done.1.refs_1_
  22.5 0.0 collective-permute-done.2.refs_2_
  22.5 2.4 %shard_map.53 = (f32[13,4,16,256]{3,2,1,0:T(8,128)S(1)}, f32[2,16,128]{2,1,0:T(8,128)S(1)}, f32[32,4,128]{2,1,0:T(4,128)S(1)}) custom-call(f32[4,16,256]{2,1,0:T(8,128)S(1)} %get-tuple-element.14.state_ref, f32[4,16,256]{2,1,0:T(8,128)S(1)} %get-tuple-element.15.damping_ref, f32[16,128]{1,0:T(8,128)S(1)} %collective-permute-done.refs_0_, ...), custom_call_target="tpu_custom_call" | custom-call | tf_op jit(solution)/shard_map/pallas_call | solution.py:512
  24.9 9.0 %all_to_all.16.received_ref = f32[32,4,128]{2,1,0:T(4,128)S(1)} all-to-all(f32[32,4,128]{2,1,0:T(4,128)S(1)} %get-tuple-element.19), channel_id=1, replica_groups=mesh['sub'=4,'gx'=4,'gy'=2] {'sub','gx','gy'}, dimensions={0} | all-to-all | bytes 131072 | tf_op jit(solution)/shard_map/all_to_all | solution.py:521
  33.9 2.2 %shard_map.54 = (f32[3,16,128]{2,1,0:T(8,128)S(1)}, f32[16,4,256]{2,1,0:T(4,128)}) custom-call(f32[32,4,128]{2,1,0:T(4,128)S(1)} %all_to_all.16.received_ref, f32[2,16,128]{2,1,0:T(8,128)S(1)} %get-tuple-element.20.small_ref, f32[13,4,16,256]{3,2,1,0:T(8,128)S(1)} %get-tuple-element.21.basis_ref), custom_call_target="tpu_custom_call" | custom-call | tf_op jit(solution)/shard_map/pallas_call | solution.py:512
  36.1 3.5 %all-to-all-start.2 = ((f32[16,4,256]{2,1,0:T(4,128)}), f32[16,4,256]{2,1,0:T(4,128)S(1)}, u32[]{:S(2)}, u32[]{:S(2)}) async-start(f32[16,4,256]{2,1,0:T(4,128)} %get-tuple-element.25), calls=%async_computation.2 | async-start | bytes 131072 | tf_op jit(solution)/shard_map/all_to_all | solution.py:521
  39.6 0.0 copy-start
  39.6 0.6 %copy-done = f32[4]{0:T(128)S(1)} copy-done((f32[4]{0:T(128)S(1)}, f32[4]{0:T(128)}, u32[]{:S(2)}) %copy-start) | copy-done | bytes 40
  40.3 3.6 %shard_map.55 = (f32[4,16,256]{2,1,0:T(8,128)}, f32[8,128]{1,0:T(8,128)S(1)}) custom-call(f32[4]{0:T(128)S(1)} %copy-done, f32[3,16,128]{2,1,0:T(8,128)S(1)} %get-tuple-element.22.small_ref, f32[4,16,256]{2,1,0:T(8,128)S(1)} %get-tuple-element.14.state_ref, f32[13,4,16,256]{3,2,1,0:T(8,128)S(1)} %get-tuple-element.21.basis_ref), custom_call_target="tpu_custom_call" | custom-call | tf_op jit(solution)/shard_map/pallas_call | solution.py:512
  43.8 2.3 %all-to-all-done.2.peaks_ref = f32[16,4,256]{2,1,0:T(4,128)S(1)} async-done(((f32[16,4,256]{2,1,0:T(4,128)}), f32[16,4,256]{2,1,0:T(4,128)S(1)}, u32[]{:S(2)}, u32[]{:S(2)}) %all-to-all-start.2) | async-done | bytes 65568 | tf_op jit(solution)/shard_map/all_to_all | solution.py:521
  46.2 0.6 %shard_map.56 = f32[4,256]{1,0:T(4,128)} custom-call(f32[8,128]{1,0:T(8,128)S(1)} %get-tuple-element.24.highest_ref, f32[16,4,256]{2,1,0:T(4,128)S(1)} %all-to-all-done.2.peaks_ref), custom_call_target="tpu_custom_call" | custom-call | tf_op jit(solution)/shard_map/pallas_call | solution.py:512
  (1 shorter events, 0.0 us)
Async XLA Ops:
  1.7 4.7 %collective-permute-start = (f32[16,128]{1,0:T(8,128)S(1)}, f32[16,128]{1,0:T(8,128)S(1)}, u32[]{:S(2)}, u32[]{:S(2)}) collective-permute-start(f32[16,128]{1,0:T(8,128)S(1)} %get-tuple-element.16), channel_id=1, source_target_pairs={{0,1},{1,0},{2,3},{3,2},{4,5},{5,4},{6,7},{7,6},{8,9},{9,8},{10,11... | collective-permute-start | bytes 24584 | tf_op jit(solution)/shard_map/ppermute | solution.py:542
  6.4 16.1 %collective-permute-start.1 = (f32[224,128]{1,0:T(8,128)S(1)}, f32[224,128]{1,0:T(8,128)S(1)}, u32[]{:S(2)}, u32[]{:S(2)}) collective-permute-start(f32[224,128]{1,0:T(8,128)S(1)} %get-tuple-element.17), channel_id=1, source_target_pairs={{0,2},{2,4},{4,6},{6,8},{8,10},{10,12},{12,14},{14,16},{16,18},{18... | collective-permute-start | bytes 344072 | tf_op jit(solution)/shard_map/ppermute | solution.py:557
  8.5 14.0 %collective-permute-start.2 = (f32[224,128]{1,0:T(8,128)S(1)}, f32[224,128]{1,0:T(8,128)S(1)}, u32[]{:S(2)}, u32[]{:S(2)}) collective-permute-start(f32[224,128]{1,0:T(8,128)S(1)} %get-tuple-element.18), channel_id=1, source_target_pairs={{2,0},{4,2},{6,4},{8,6},{10,8},{12,10},{14,12},{16,14},{18,16},{20... | collective-permute-start | bytes 344072 | tf_op jit(solution)/shard_map/ppermute | solution.py:558
  36.1 10.1 %all-to-all-start.2 = ((f32[16,4,256]{2,1,0:T(4,128)}), f32[16,4,256]{2,1,0:T(4,128)S(1)}, u32[]{:S(2)}, u32[]{:S(2)}) async-start(f32[16,4,256]{2,1,0:T(4,128)} %get-tuple-element.25), calls=%async_computation.2 | async-start | bytes 131072 | tf_op jit(solution)/shard_map/all_to_all | solution.py:521
  39.6 0.7 %copy-start = (f32[4]{0:T(128)S(1)}, f32[4]{0:T(128)}, u32[]{:S(2)}) copy-start(f32[4]{0:T(128)} %weights_ref.1) | copy-start | bytes 52

commit v8 on v7

--- a/solution.py
+++ b/solution.py
@@ -11,7 +11,7 @@
 
 KRYLOV = 12
 SUBSTEPS = 4
-GUESS = 6
+GUESS = 5
 REACH = KRYLOV + 1
 HALO = -(-REACH // 8) * 8
 LANES = 128
@@ -194,7 +194,7 @@
 
 def first_kernel(count, state_ref, damping_ref, *refs):
     halo_refs = refs[:count]
-    up_ref, down_ref, guess_ref, inner_ref, small_ref, send_ref, basis_ref, drag_ref, table_ref = refs[count:]
+    up_ref, down_ref, small_ref, inner_ref, send_ref, basis_ref, drag_ref, table_ref = refs[count:]
     height, width = state_ref.shape[1:]
     rows, columns = height + 2 * HALO, width + LANES
     tiles = width // LANES
@@ -224,10 +224,7 @@
     state = [whole(f) for f in range(4)]
     damping = [whole(4 + f) for f in range(4)]
     forcing, drag = forcing_of(state, damping, 0.5 * mask)
-    guess, scale = guessed(guess_ref)
-    steps = basis_columns(guess)
-    small_ref[0] = by_lane(steps, 0, jnp.zeros(TILE, jnp.float32))
-    small_ref[1] = jnp.broadcast_to(scale, TILE)
+    steps, scale = columns_of(small_ref[0], KRYLOV), small_ref[1, 0:1]
     wide = lambda x: jnp.concatenate([x] * (columns // LANES), axis=1)
     start = wide(1.0 / scale)
     for f in range(4):
@@ -401,6 +398,12 @@
         column = jnp.where(row == c, shift, jnp.where(row == c + 1, length, 0.0))
         columns.append(jnp.where(row == c - 1, back, column))
     return columns
+
+
+def plan_kernel(guess_ref, small_ref):
+    guess, scale = guessed(guess_ref)
+    small_ref[0] = by_lane(basis_columns(guess), 0, jnp.zeros(TILE, jnp.float32))
+    small_ref[1] = jnp.broadcast_to(scale, TILE)
 
 
 def orthogonalize(received_ref, steps, scale):
@@ -557,15 +560,16 @@
     up = lax.ppermute(packs[0], ROWS, [(i, (i + 1) % lines) for i in range(lines)])
     down = lax.ppermute(packs[-1], ROWS, [((i + 1) % lines, i) for i in range(lines)])
     tall_rows = height + 2 * HALO
-    basis, small, send = call(
+    (small,) = call(plan_kernel, [near(2, *TILE)], guess)
+    basis, send = call(
         functools.partial(first_kernel, number),
-        [near(KRYLOV + 1, fields, height, width), near(2, *TILE), sends(KRYLOV + 1)],
+        [near(KRYLOV + 1, fields, height, width), sends(KRYLOV + 1)],
         state,
         damping,
         *halos,
         up,
         down,
-        guess,
+        small,
         scratch=[
             near(KRYLOV + 1, fields, tall_rows, columns),
             near(fields, tall_rows, columns),

time: 47.1 us -> 47.2 us (level)
    pallas_call x7 -> x8, Pallas kernels: 10.6 us -> 10.6 us  [call(): pl.pallas_call(kernel, out_shape=outs, in_specs=specs, out_specs=[VMEM] *...]
  transfers between devices with their start and end apart: 4 -> 4, of which waited for: 2 -> 2; matrix products, arithmetic and copies ran while one was open for 0% -> 0% of each run, Pallas kernels for 9% -> 10%
where the time goes in v8:
time: 47.2 us; the launch traced here: 46.9 us
  blocking collectives  19.9 us (42%)
  starting transfers between devices  11.1 us (24%)
  Pallas kernels  10.6 us (22%)
  waiting for transfers between devices  3.97 us (8%)
  between operations  0.7 us (1%)
  local copies, waits for them, and re-layouts  0.65 us (1%)
    all_to_all x2, blocking collectives, shards(): exchange = lambda x, axes: lax.all_to_all(x, axes, 0, 0)  19.9 us
    pallas_call x8, Pallas kernels, call(): pl.pallas_call(kernel, out_shape=outs, in_specs=specs, out_specs=[VMEM] *...  10.6 us
    all_to_all x1, starting transfers between devices, shards(): exchange = lambda x, axes: lax.all_to_all(x, axes, 0, 0)  3.49 us
    ppermute x1, starting transfers between devices, shards(): halos = [lax.ppermute(edges[0], 'gy', [(0, 1), (1, 0)])]  3.06 us
    ppermute x1, starting transfers between devices, shards(): lax.ppermute(packs[-1], ROWS, [((i + 1) % lines, i) for i in range(lines)])  2.37 us
    all_to_all x1, waiting for transfers between devices, shards(): exchange = lambda x, axes: lax.all_to_all(x, axes, 0, 0)  2.33 us
    ppermute x1, starting transfers between devices, shards(): lax.ppermute(packs[0], ROWS, [(i, (i + 1) % lines) for i in range(lines)])  2.14 us
    ppermute x1, waiting for transfers between devices, shards(): halos = [lax.ppermute(edges[0], 'gy', [(0, 1), (1, 0)])]  1.63 us
  transfers between devices with their start and end apart: 4, of which 2 were waited for; matrix products, arithmetic and copies ran while one was open for 0% of the time, Pallas kernels for 10%

profile of v8, /device:TPU:0, one launch (start us, length us, event | category | flops | bytes accessed | tf_op | source)
XLA Modules:
  0.0 46.9 jit_solution(2205071709553998829)
XLA Ops:
  0.6 1.0 %shard_map.50 = (f32[4,16,256]{2,1,0:T(8,128)S(1)}, f32[4,16,256]{2,1,0:T(8,128)S(1)}, f32[16,128]{1,0:T(8,128)S(1)}) custom-call(f32[4,16,256]{2,1,0:T(8,128)} %far_state_ref.1, f32[4,16,256]{2,1,0:T(8,128)} %far_damping_ref.1), custom_call_target="tpu_custom_call" | custom-call | tf_op jit(solution)/shard_map/pallas_call | solution.py:515
  1.7 3.1 %collective-permute-start = (f32[16,128]{1,0:T(8,128)S(1)}, f32[16,128]{1,0:T(8,128)S(1)}, u32[]{:S(2)}, u32[]{:S(2)}) collective-permute-start(f32[16,128]{1,0:T(8,128)S(1)} %get-tuple-element.15), channel_id=1, source_target_pairs={{0,1},{1,0},{2,3},{3,2},{4,5},{5,4},{6,7},{7,6},{8,9},{9,8},{10,11... | collective-permute-start | bytes 24584 | tf_op jit(solution)/shard_map/ppermute | solution.py:545
  4.7 1.6 %collective-permute-done.refs_0_ = f32[16,128]{1,0:T(8,128)S(1)} collective-permute-done((f32[16,128]{1,0:T(8,128)S(1)}, f32[16,128]{1,0:T(8,128)S(1)}, u32[]{:S(2)}, u32[]{:S(2)}) %collective-permute-start) | collective-permute-done | bytes 8224 | tf_op jit(solution)/shard_map/ppermute | solution.py:545
  6.4 2.1 %collective-permute-start.1 = (f32[224,128]{1,0:T(8,128)S(1)}, f32[224,128]{1,0:T(8,128)S(1)}, u32[]{:S(2)}, u32[]{:S(2)}) collective-permute-start(f32[224,128]{1,0:T(8,128)S(1)} %get-tuple-element.16), channel_id=1, source_target_pairs={{0,2},{2,4},{4,6},{6,8},{8,10},{10,12},{12,14},{14,16},{16,18},{18... | collective-permute-start | bytes 344072 | tf_op jit(solution)/shard_map/ppermute | solution.py:560
  8.5 2.4 %collective-permute-start.2 = (f32[224,128]{1,0:T(8,128)S(1)}, f32[224,128]{1,0:T(8,128)S(1)}, u32[]{:S(2)}, u32[]{:S(2)}) collective-permute-start(f32[224,128]{1,0:T(8,128)S(1)} %get-tuple-element.17), channel_id=1, source_target_pairs={{2,0},{4,2},{6,4},{8,6},{10,8},{12,10},{14,12},{16,14},{18,16},{20... | collective-permute-start | bytes 344072 | tf_op jit(solution)/shard_map/ppermute | solution.py:561
  10.9 0.6 %shard_map.52 = f32[32,2,128]{2,1,0:T(2,128)S(1)} custom-call(f32[4,16,256]{2,1,0:T(8,128)S(1)} %get-tuple-element.13.state_ref, f32[4,16,256]{2,1,0:T(8,128)S(1)} %get-tuple-element.14.damping_ref), custom_call_target="tpu_custom_call" | custom-call | tf_op jit(solution)/shard_map/pallas_call | solution.py:515
  11.5 10.9 %all_to_all.15.guess_ref = f32[32,2,128]{2,1,0:T(2,128)S(1)} all-to-all(f32[32,2,128]{2,1,0:T(2,128)S(1)} %shard_map.52), channel_id=1, replica_groups=mesh['sub'=4,'gx'=4,'gy'=2] {'sub','gx','gy'}, dimensions={0} | all-to-all | bytes 65536 | tf_op jit(solution)/shard_map/all_to_all | solution.py:524
  22.4 0.4 shard_map.53.refs_3_.small_ref
  22.9 0.0 collective-permute-done.1.refs_1_
  22.9 0.0 collective-permute-done.2.refs_2_
  22.9 2.1 %shard_map.54 = (f32[13,4,16,256]{3,2,1,0:T(8,128)S(1)}, f32[32,4,128]{2,1,0:T(4,128)S(1)}) custom-call(f32[4,16,256]{2,1,0:T(8,128)S(1)} %get-tuple-element.13.state_ref, f32[4,16,256]{2,1,0:T(8,128)S(1)} %get-tuple-element.14.damping_ref, f32[16,128]{1,0:T(8,128)S(1)} %collective-permute-done.refs_0_, f32[224,128]{1,0:T(8,128)S(1)} %collective-permute-done.1.refs_1_, ...), custom_call_target="tpu_custom_call" | custom-call | tf_op jit(solution)/shard_map/pallas_call | solution.py:515
  25.0 9.0 %all_to_all.16.received_ref = f32[32,4,128]{2,1,0:T(4,128)S(1)} all-to-all(f32[32,4,128]{2,1,0:T(4,128)S(1)} %get-tuple-element.18), channel_id=1, replica_groups=mesh['sub'=4,'gx'=4,'gy'=2] {'sub','gx','gy'}, dimensions={0} | all-to-all | bytes 131072 | tf_op jit(solution)/shard_map/all_to_all | solution.py:524
  34.0 2.2 %shard_map.55 = (f32[3,16,128]{2,1,0:T(8,128)S(1)}, f32[16,4,256]{2,1,0:T(4,128)}) custom-call(f32[32,4,128]{2,1,0:T(4,128)S(1)} %all_to_all.16.received_ref, f32[2,16,128]{2,1,0:T(8,128)S(1)} %shard_map.53.refs_3_.small_ref, f32[13,4,16,256]{3,2,1,0:T(8,128)S(1)} %get-tuple-element.19.basis_ref), custom_call_target="tpu_custom_call" | custom-call | tf_op jit(solution)/shard_map/pallas_call | solution.py:515
  36.2 3.5 %all-to-all-start.2 = ((f32[16,4,256]{2,1,0:T(4,128)}), f32[16,4,256]{2,1,0:T(4,128)S(1)}, u32[]{:S(2)}, u32[]{:S(2)}) async-start(f32[16,4,256]{2,1,0:T(4,128)} %get-tuple-element.23), calls=%async_computation.2 | async-start | bytes 131072 | tf_op jit(solution)/shard_map/all_to_all | solution.py:524
  39.7 0.0 copy-start
  39.7 0.6 %copy-done = f32[4]{0:T(128)S(1)} copy-done((f32[4]{0:T(128)S(1)}, f32[4]{0:T(128)}, u32[]{:S(2)}) %copy-start) | copy-done | bytes 40
  40.4 3.6 %shard_map.56 = (f32[4,16,256]{2,1,0:T(8,128)}, f32[8,128]{1,0:T(8,128)S(1)}) custom-call(f32[4]{0:T(128)S(1)} %copy-done, f32[3,16,128]{2,1,0:T(8,128)S(1)} %get-tuple-element.20.small_ref, f32[4,16,256]{2,1,0:T(8,128)S(1)} %get-tuple-element.13.state_ref, f32[13,4,16,256]{3,2,1,0:T(8,128)S(1)} %get-tuple-element.19.basis_ref), custom_call_target="tpu_custom_call" | custom-call | tf_op jit(solution)/shard_map/pallas_call | solution.py:515
  44.0 2.3 %all-to-all-done.2.peaks_ref = f32[16,4,256]{2,1,0:T(4,128)S(1)} async-done(((f32[16,4,256]{2,1,0:T(4,128)}), f32[16,4,256]{2,1,0:T(4,128)S(1)}, u32[]{:S(2)}, u32[]{:S(2)}) %all-to-all-start.2) | async-done | bytes 65568 | tf_op jit(solution)/shard_map/all_to_all | solution.py:524
  46.3 0.6 %shard_map.57 = f32[4,256]{1,0:T(4,128)} custom-call(f32[8,128]{1,0:T(8,128)S(1)} %get-tuple-element.22.highest_ref, f32[16,4,256]{2,1,0:T(4,128)S(1)} %all-to-all-done.2.peaks_ref), custom_call_target="tpu_custom_call" | custom-call | tf_op jit(solution)/shard_map/pallas_call | solution.py:515
  (1 shorter events, 0.0 us)
Async XLA Ops:
  1.7 4.7 %collective-permute-start = (f32[16,128]{1,0:T(8,128)S(1)}, f32[16,128]{1,0:T(8,128)S(1)}, u32[]{:S(2)}, u32[]{:S(2)}) collective-permute-start(f32[16,128]{1,0:T(8,128)S(1)} %get-tuple-element.15), channel_id=1, source_target_pairs={{0,1},{1,0},{2,3},{3,2},{4,5},{5,4},{6,7},{7,6},{8,9},{9,8},{10,11... | collective-permute-start | bytes 24584 | tf_op jit(solution)/shard_map/ppermute | solution.py:545
  6.4 16.5 %collective-permute-start.1 = (f32[224,128]{1,0:T(8,128)S(1)}, f32[224,128]{1,0:T(8,128)S(1)}, u32[]{:S(2)}, u32[]{:S(2)}) collective-permute-start(f32[224,128]{1,0:T(8,128)S(1)} %get-tuple-element.16), channel_id=1, source_target_pairs={{0,2},{2,4},{4,6},{6,8},{8,10},{10,12},{12,14},{14,16},{16,18},{18... | collective-permute-start | bytes 344072 | tf_op jit(solution)/shard_map/ppermute | solution.py:560
  8.5 14.3 %collective-permute-start.2 = (f32[224,128]{1,0:T(8,128)S(1)}, f32[224,128]{1,0:T(8,128)S(1)}, u32[]{:S(2)}, u32[]{:S(2)}) collective-permute-start(f32[224,128]{1,0:T(8,128)S(1)} %get-tuple-element.17), channel_id=1, source_target_pairs={{2,0},{4,2},{6,4},{8,6},{10,8},{12,10},{14,12},{16,14},{18,16},{20... | collective-permute-start | bytes 344072 | tf_op jit(solution)/shard_map/ppermute | solution.py:561
  36.2 10.1 %all-to-all-start.2 = ((f32[16,4,256]{2,1,0:T(4,128)}), f32[16,4,256]{2,1,0:T(4,128)S(1)}, u32[]{:S(2)}, u32[]{:S(2)}) async-start(f32[16,4,256]{2,1,0:T(4,128)} %get-tuple-element.23), calls=%async_computation.2 | async-start | bytes 131072 | tf_op jit(solution)/shard_map/all_to_all | solution.py:524
  39.7 0.7 %copy-start = (f32[4]{0:T(128)S(1)}, f32[4]{0:T(128)}, u32[]{:S(2)}) copy-start(f32[4]{0:T(128)} %weights_ref.1) | copy-start | bytes 52
